TPU v7x, 128 devices: a whole 4x4x4 slice. The times are simulated.
128 devices in a mesh: sample: 2 (over core), slab: 64 (over z, y, x).
Axes of the slice: x: 4, y: 4, z: 4, core: 2. Of those that a mesh axis runs over, the one named last changes fastest.
Arguments:
- force: float32 [3, 256, 32, 256], P(None, 'slab', None, 'sample'), parts along dimension 3, may hold values from -8 to 8, as said below
- modulus: float32 [256, 32, 256], P('slab', None, 'sample'), parts along dimension 2, may hold values from 0.2 to 1
Outputs:
- fine_field: float32 [3, 256, 32, 256], P(None, 'slab', None, 'sample'), parts along dimension 3
- coarse_field: float32 [3, 128, 16, 128], P(None, 'slab', None, 'sample'), parts along dimension 3
- compliance: float32 [4], P('sample'), parts along dimension 0
There are 2 independent parts, one for each index of `sample`. A program takes and returns all parts, laid end to end along the dimension named above; each array names one. Nothing has to cross between parts.
Inputs may be any that keep to these rules, and one draw needn't show every extreme that they name: Body force on each cell and component.
All inputs are finite; a program needn't handle non-finite values.
Results may differ from a plain program's by a relative error of at most 0.0001.
Values sent between devices are 32-bit elements; how exact they have to be, the bound alone decides.
No kernel may reach another device: no remote copies, remote signals or barrier semaphores. Data moves between devices by JAX's collectives and lax.ppermute only.
A program may use at most 128 MiB of HBM per device.

v0:
```python
import jax
import jax.numpy as jnp
from jax import lax
from jax.sharding import PartitionSpec as P

ITERS = 2
SMOOTH = 2
CDEG = 4


def extended(block, sides, width):
    for axis, dim in sides:
        count = lax.axis_size(axis)
        forward = [(i, i + 1) for i in range(count - 1)]
        backward = [(target, source) for source, target in forward]
        low = lax.ppermute(
            lax.slice_in_dim(block, block.shape[dim] - width, None, axis=dim), axis, forward
        )
        high = lax.ppermute(lax.slice_in_dim(block, 0, width, axis=dim), axis, backward)
        block = jnp.concatenate([low, block, high], axis=dim)
    return block


def from_behind(x, axis, by):
    peers = lax.axis_size(axis)
    pairs = [(i, i + by) for i in range(peers) if 0 <= i + by < peers]
    return lax.ppermute(x, axis, pairs)


def from_everyone(x, axis):
    peers = lax.axis_size(axis)
    return lax.all_to_all(jnp.broadcast_to(x[None], (peers, *x.shape)), axis, 0, 0, tiled=True)


def of_everyone(x, axis):
    return from_everyone(x, axis).sum(axis=0)


def in_one(arrays, axis):
    ends = [0]
    for a in arrays:
        ends.append(ends[-1] + a.size)
    so_far = of_everyone(jnp.concatenate([a.ravel() for a in arrays]), axis)
    return tuple((so_far[b:e].reshape(a.shape) for a, b, e in zip(arrays, ends, ends[1:])))


def shift_back(values, dimension):
    length = values.shape[dimension]
    zeroes = jnp.zeros_like(lax.slice_in_dim(values, 0, 1, axis=dimension))
    return jnp.concatenate(
        [zeroes, lax.slice_in_dim(values, 0, length - 1, axis=dimension)], axis=dimension
    )


def shift_ahead(values, dimension):
    length = values.shape[dimension]
    zeroes = jnp.zeros_like(lax.slice_in_dim(values, 0, 1, axis=dimension))
    return jnp.concatenate(
        [lax.slice_in_dim(values, 1, length, axis=dimension), zeroes], axis=dimension
    )


def operate_extended(padded, lame_ext):
    lower = padded[:, :-1]
    grad_z = padded[:, 1:] - lower
    grad_y = shift_ahead(lower, 2) - lower
    grad_x = shift_ahead(lower, 3) - lower
    spread = lame_ext * (grad_x[0] + grad_y[1] + grad_z[2])
    flux_z = lame_ext * grad_z
    inner_y = lame_ext[1:] * grad_y[:, 1:]
    inner_x = lame_ext[1:] * grad_x[:, 1:]
    inner_s = spread[1:]
    result = (
        flux_z[:, :-1]
        - flux_z[:, 1:]
        + (shift_back(inner_y, 2) - inner_y)
        + (shift_back(inner_x, 3) - inner_x)
    )
    pressure = jnp.stack(
        [shift_back(inner_s, 2) - inner_s, shift_back(inner_s, 1) - inner_s, spread[:-1] - inner_s]
    )
    return result + pressure


def operate_split(displace, lame_ext):
    padded = extended(displace, (("slab", 1),), 1)
    return operate_extended(padded, lame_ext)


def extend(lame):
    below = from_behind(lame[-1:], "slab", 1)
    return jnp.concatenate([below, lame], 0)


def diag_inverse(lame_ext):
    lame = lame_ext[1:]
    laplace = lame + lame_ext[:-1] + (lame + shift_back(lame, 1)) + (lame + shift_back(lame, 2))
    diagonal = jnp.stack(
        [
            laplace + lame + shift_back(lame, 2),
            laplace + lame + shift_back(lame, 1),
            laplace + lame + lame_ext[:-1],
        ]
    )
    return 1.0 / diagonal


def restrict_scalar(values):
    shape = values.shape
    return values.reshape(shape[0] // 2, 2, shape[1] // 2, 2, shape[2] // 2, 2).mean(axis=(1, 3, 5))


def restrict_vector(values):
    shape = values.shape
    return values.reshape(shape[0], shape[1] // 2, 2, shape[2] // 2, 2, shape[3] // 2, 2).mean(
        axis=(2, 4, 6)
    )


def prolong(values):
    return jnp.repeat(jnp.repeat(jnp.repeat(values, 2, 1), 2, 2), 2, 3)


def chebyshev(iterate, residue, operator, inverse, degree, low_end, high_end):
    centre = (high_end + low_end) / 2.0
    half_width = (high_end - low_end) / 2.0
    spread_ratio = centre / half_width
    rho_now = 1.0 / spread_ratio
    update = inverse * residue / centre
    for section in range(degree):
        iterate = iterate + update
        residue = residue - operator(update)
        if section + 1 < degree:
            rho_next = 1.0 / (2.0 * spread_ratio - rho_now)
            update = rho_next * rho_now * update + 2.0 * rho_next / half_width * (inverse * residue)
            rho_now = rho_next
    return (iterate, residue)


def body(force, modulus):
    lame = 0.4 * modulus
    lame_ext = extend(lame)
    fine_inverse = diag_inverse(lame_ext)

    def fine_operator(vector):
        return operate_split(vector, lame_ext)

    coarse_lame = restrict_scalar(lame)
    coarse_ext = extend(coarse_lame)
    coarse_inverse = diag_inverse(coarse_ext)

    def coarse_solve(rhs_local, degree):
        solved, unused = chebyshev(
            jnp.zeros_like(rhs_local),
            rhs_local,
            lambda vector: operate_split(vector, coarse_ext),
            coarse_inverse,
            degree,
            0.02,
            2.0,
        )
        return solved

    iterate = jnp.zeros_like(force)
    residue = force
    for cycle in range(ITERS):
        iterate, residue = chebyshev(
            iterate, residue, fine_operator, fine_inverse, SMOOTH, 0.25, 2.0
        )
        correction = coarse_solve(4.0 * restrict_vector(residue), CDEG)
        expanded = prolong(correction)
        iterate = iterate + expanded
        residue = residue - fine_operator(expanded)
        iterate, residue = chebyshev(
            iterate, residue, fine_operator, fine_inverse, SMOOTH, 0.25, 2.0
        )
    coarse_force = restrict_vector(force)
    coarse_field = coarse_solve(4.0 * coarse_force, 2 * CDEG)
    totals = in_one((jnp.sum(force * iterate), jnp.sum(coarse_force * coarse_field)), "slab")
    cells = float(lame.size * lax.axis_size("slab"))
    compliance = jnp.stack([totals[0] / cells, totals[1] / (cells / 8.0)])
    return (iterate, coarse_field, compliance)


def solution(mesh):
    return jax.shard_map(
        body,
        mesh=mesh,
        in_specs=(P(None, "slab", None, "sample"), P("slab", None, "sample")),
        out_specs=(P(None, "slab", None, "sample"), P(None, "slab", None, "sample"), P("sample")),
        check_vma=False,
    )
```

profile of v0, /device:TPU:32, one launch (start us, length us, event | category | flops | bytes accessed | tf_op | source)
XLA Modules:
  0.0 428.4 jit_solution(3396315356986258996)
XLA Ops:
  1.5 5.6 %reshape.106 = f32[2,2,16,2,64,2]{5,4,3,2,1,0:T(8,128)} reshape(f32[4,32,128]{2,1,0:T(8,128)S(1)} %broadcast_multiply_fusion.26) | data formatting | bytes 131072 | tf_op jit(solution)/shard_map/reshape | solution.py:110
  7.1 2.5 reduce_sum.63
  9.6 3.4 collective-permute-start.3
  13.0 3.4 collective-permute-start
  17.8 14.6 %reshape.115 = f32[3,2,2,16,2,64,2]{6,5,4,3,2,1,0:T(8,128)} reshape(f32[3,4,32,128]{3,2,1,0:T(8,128)} %param.2) | data formatting | bytes 393216 | tf_op jit(solution)/shard_map/reshape | solution.py:115
  32.4 5.5 %reduce_sum.66 = f32[3,2,16,64]{3,2,1,0:T(8,128)S(1)} reduce(f32[3,2,2,16,2,64,2]{6,5,4,3,2,1,0:T(8,128)} %reshape.115, f32[]{:T(128)} %constant.27.clone.1), dimensions={2,4,6}, to_apply=%region_3.0 | reduce | flops 43008 | bytes 221188 | tf_op jit(solution)/shard_map/reduce_sum | solution.py:115
  38.1 6.7 %collective-permute-start.32 = (f32[3,1,16,64]{3,2,1,0:T(8,128)S(1)}, f32[3,1,16,64]{3,2,1,0:T(8,128)S(1)}, u32[]{:S(2)}, u32[]{:S(2)}) collective-permute-start(f32[3,1,16,64]{3,2,1,0:T(8,128)S(1)} %get-tuple-element.247), channel_id=1, source_target_pairs={{1,0},{2,1},{3,2},{4,3},{5,4},{6,5},{7,6},{8,7},{9,8},{10,9},{11,1... | collective-permute-start | bytes 36872 | tf_op jit(solution)/shard_map/ppermute | solution.py:19
  46.7 8.0 %collective-permute-done.33 = f32[3,1,16,64]{3,2,1,0:T(8,128)S(1)} collective-permute-done((f32[3,1,16,64]{3,2,1,0:T(8,128)S(1)}, f32[3,1,16,64]{3,2,1,0:T(8,128)S(1)}, u32[]{:S(2)}, u32[]{:S(2)}) %collective-permute-start.33) | collective-permute-done | bytes 12320 | tf_op jit(solution)/shard_map/ppermute | solution.py:16
  57.4 3.9 collective-permute-start.35
  61.5 5.9 %collective-permute-done.35 = f32[3,1,16,64]{3,2,1,0:T(8,128)S(1)} collective-permute-done((f32[3,1,16,64]{3,2,1,0:T(8,128)S(1)}, f32[3,1,16,64]{3,2,1,0:T(8,128)S(1)}, u32[]{:S(2)}, u32[]{:S(2)}) %collective-permute-start.35) | collective-permute-done | bytes 12320 | tf_op jit(solution)/shard_map/ppermute | solution.py:16
  70.5 8.1 %collective-permute-start.36 = (f32[3,1,16,64]{3,2,1,0:T(8,128)S(1)}, f32[3,1,16,64]{3,2,1,0:T(8,128)S(1)}, u32[]{:S(2)}, u32[]{:S(2)}) collective-permute-start(f32[3,1,16,64]{3,2,1,0:T(8,128)S(1)} %get-tuple-element.243), channel_id=1, source_target_pairs={{1,0},{2,1},{3,2},{4,3},{5,4},{6,5},{7,6},{8,7},{9,8},{10,9},{11,1... | collective-permute-start | bytes 36872 | tf_op jit(solution)/shard_map/ppermute | solution.py:19
  80.4 1.9 collective-permute-start.39
  82.5 8.4 %collective-permute-start.1 = (f32[3,1,32,128]{2,3,1,0:T(8,128)}, f32[3,1,32,128]{2,3,1,0:T(8,128)S(1)}, u32[]{:S(2)}, u32[]{:S(2)}) collective-permute-start(f32[3,1,32,128]{2,3,1,0:T(8,128)} %get-tuple-element.142), channel_id=1, source_target_pairs={{1,0},{2,1},{3,2},{4,3},{5,4},{6,5},{7,6},{8,7},{9,8},{10,9},{11,1... | collective-permute-start | bytes 147464 | tf_op jit(solution)/shard_map/ppermute | solution.py:19
  92.9 8.1 %collective-permute-start.38 = (f32[3,1,16,64]{3,2,1,0:T(8,128)S(1)}, f32[3,1,16,64]{3,2,1,0:T(8,128)S(1)}, u32[]{:S(2)}, u32[]{:S(2)}) collective-permute-start(f32[3,1,16,64]{3,2,1,0:T(8,128)S(1)} %get-tuple-element.241), channel_id=1, source_target_pairs={{1,0},{2,1},{3,2},{4,3},{5,4},{6,5},{7,6},{8,7},{9,8},{10,9},{11,1... | collective-permute-start | bytes 36872 | tf_op jit(solution)/shard_map/ppermute | solution.py:19
  103.4 8.4 %collective-permute-start.40 = (f32[3,1,16,64]{3,2,1,0:T(8,128)S(1)}, f32[3,1,16,64]{3,2,1,0:T(8,128)S(1)}, u32[]{:S(2)}, u32[]{:S(2)}) collective-permute-start(f32[3,1,16,64]{3,2,1,0:T(8,128)S(1)} %get-tuple-element.239), channel_id=1, source_target_pairs={{1,0},{2,1},{3,2},{4,3},{5,4},{6,5},{7,6},{8,7},{9,8},{10,9},{11,1... | collective-permute-start | bytes 36872 | tf_op jit(solution)/shard_map/ppermute | solution.py:19
  114.9 6.8 %collective-permute-done.41 = f32[3,1,16,64]{3,2,1,0:T(8,128)S(1)} collective-permute-done((f32[3,1,16,64]{3,2,1,0:T(8,128)S(1)}, f32[3,1,16,64]{3,2,1,0:T(8,128)S(1)}, u32[]{:S(2)}, u32[]{:S(2)}) %collective-permute-start.41) | collective-permute-done | bytes 12320 | tf_op jit(solution)/shard_map/ppermute | solution.py:16
  126.3 4.1 collective-permute-start.5
  131.1 7.0 %collective-permute-done.5 = f32[3,1,32,128]{2,3,1,0:T(8,128)S(1)} collective-permute-done((f32[3,1,32,128]{2,3,1,0:T(8,128)S(1)}, f32[3,1,32,128]{2,3,1,0:T(8,128)S(1)}, u32[]{:S(2)}, u32[]{:S(2)}) %collective-permute-start.5) | collective-permute-done | bytes 49184 | tf_op jit(solution)/shard_map/ppermute | solution.py:16
  140.5 13.9 %reshape.107 = f32[3,2,2,16,2,64,2]{6,5,4,3,2,1,0:T(8,128)} reshape(f32[3,4,32,128]{3,2,1,0:T(8,128)S(1)} %copy.198) | data formatting | bytes 393216 | tf_op jit(solution)/shard_map/reshape | solution.py:115
  154.4 5.5 %reduce_sum.64 = f32[3,2,16,64]{3,2,1,0:T(8,128)S(1)} reduce(f32[3,2,2,16,2,64,2]{6,5,4,3,2,1,0:T(8,128)} %reshape.107, f32[]{:T(128)} %constant.27.clone.1), dimensions={2,4,6}, to_apply=%region_1.0 | reduce | flops 43008 | bytes 221188 | tf_op jit(solution)/shard_map/reduce_sum | solution.py:115
  163.5 8.1 %collective-permute-start.42 = (f32[3,1,16,64]{3,2,1,0:T(8,128)S(1)}, f32[3,1,16,64]{3,2,1,0:T(8,128)S(1)}, u32[]{:S(2)}, u32[]{:S(2)}) collective-permute-start(f32[3,1,16,64]{3,2,1,0:T(8,128)S(1)} %get-tuple-element.236), channel_id=1, source_target_pairs={{1,0},{2,1},{3,2},{4,3},{5,4},{6,5},{7,6},{8,7},{9,8},{10,9},{11,1... | collective-permute-start | bytes 36872 | tf_op jit(solution)/shard_map/ppermute | solution.py:19
  173.5 8.1 %collective-permute-start.6 = (f32[3,1,16,64]{3,2,1,0:T(8,128)S(1)}, f32[3,1,16,64]{3,2,1,0:T(8,128)S(1)}, u32[]{:S(2)}, u32[]{:S(2)}) collective-permute-start(f32[3,1,16,64]{3,2,1,0:T(8,128)S(1)} %get-tuple-element.259), channel_id=1, source_target_pairs={{1,0},{2,1},{3,2},{4,3},{5,4},{6,5},{7,6},{8,7},{9,8},{10,9},{11,1... | collective-permute-start | bytes 36872 | tf_op jit(solution)/shard_map/ppermute | solution.py:19
  186.8 8.4 %collective-permute-start.8 = (f32[3,1,16,64]{3,2,1,0:T(8,128)S(1)}, f32[3,1,16,64]{3,2,1,0:T(8,128)S(1)}, u32[]{:S(2)}, u32[]{:S(2)}) collective-permute-start(f32[3,1,16,64]{3,2,1,0:T(8,128)S(1)} %get-tuple-element.257), channel_id=1, source_target_pairs={{1,0},{2,1},{3,2},{4,3},{5,4},{6,5},{7,6},{8,7},{9,8},{10,9},{11,1... | collective-permute-start | bytes 36872 | tf_op jit(solution)/shard_map/ppermute | solution.py:19
  198.9 8.4 %collective-permute-start.10 = (f32[3,1,16,64]{3,2,1,0:T(8,128)S(1)}, f32[3,1,16,64]{3,2,1,0:T(8,128)S(1)}, u32[]{:S(2)}, u32[]{:S(2)}) collective-permute-start(f32[3,1,16,64]{3,2,1,0:T(8,128)S(1)} %get-tuple-element.255), channel_id=1, source_target_pairs={{1,0},{2,1},{3,2},{4,3},{5,4},{6,5},{7,6},{8,7},{9,8},{10,9},{11,1... | collective-permute-start | bytes 36872 | tf_op jit(solution)/shard_map/ppermute | solution.py:19
  212.1 1.9 collective-permute-start.13
  214.0 8.4 %collective-permute-start.12 = (f32[3,1,32,128]{2,3,1,0:T(8,128)S(1)}, f32[3,1,32,128]{2,3,1,0:T(8,128)S(1)}, u32[]{:S(2)}, u32[]{:S(2)}) collective-permute-start(f32[3,1,32,128]{2,3,1,0:T(8,128)S(1)} %get-tuple-element.138), channel_id=1, source_target_pairs={{1,0},{2,1},{3,2},{4,3},{5,4},{6,5},{7,6},{8,7},{9,8},{10,9},{11,1... | collective-permute-start | bytes 147464 | tf_op jit(solution)/shard_map/ppermute | solution.py:19
  222.5 2.3 collective-permute-done.13
  231.4 8.6 %collective-permute-start.14 = (f32[3,1,32,128]{2,3,1,0:T(8,128)S(1)}, f32[3,1,32,128]{2,3,1,0:T(8,128)S(1)}, u32[]{:S(2)}, u32[]{:S(2)}) collective-permute-start(f32[3,1,32,128]{2,3,1,0:T(8,128)S(1)} %get-tuple-element.136), channel_id=1, source_target_pairs={{1,0},{2,1},{3,2},{4,3},{5,4},{6,5},{7,6},{8,7},{9,8},{10,9},{11,1... | collective-permute-start | bytes 147464 | tf_op jit(solution)/shard_map/ppermute | solution.py:19
  240.0 3.1 collective-permute-done.15
  246.2 1.9 collective-permute-start.17
  248.1 8.8 %collective-permute-start.16 = (f32[3,1,32,128]{2,3,1,0:T(8,128)S(1)}, f32[3,1,32,128]{2,3,1,0:T(8,128)S(1)}, u32[]{:S(2)}, u32[]{:S(2)}) collective-permute-start(f32[3,1,32,128]{2,3,1,0:T(8,128)S(1)} %get-tuple-element.134), channel_id=1, source_target_pairs={{1,0},{2,1},{3,2},{4,3},{5,4},{6,5},{7,6},{8,7},{9,8},{10,9},{11,1... | collective-permute-start | bytes 147464 | tf_op jit(solution)/shard_map/ppermute | solution.py:19
  257.0 2.0 collective-permute-done.17
  263.9 8.6 %collective-permute-start.18 = (f32[3,1,32,128]{2,3,1,0:T(8,128)S(1)}, f32[3,1,32,128]{2,3,1,0:T(8,128)S(1)}, u32[]{:S(2)}, u32[]{:S(2)}) collective-permute-start(f32[3,1,32,128]{2,3,1,0:T(8,128)S(1)} %get-tuple-element.132), channel_id=1, source_target_pairs={{1,0},{2,1},{3,2},{4,3},{5,4},{6,5},{7,6},{8,7},{9,8},{10,9},{11,1... | collective-permute-start | bytes 147464 | tf_op jit(solution)/shard_map/ppermute | solution.py:19
  279.5 8.6 %collective-permute-start.20 = (f32[3,1,32,128]{2,3,1,0:T(8,128)S(1)}, f32[3,1,32,128]{2,3,1,0:T(8,128)S(1)}, u32[]{:S(2)}, u32[]{:S(2)}) collective-permute-start(f32[3,1,32,128]{2,3,1,0:T(8,128)S(1)} %get-tuple-element.130), channel_id=1, source_target_pairs={{1,0},{2,1},{3,2},{4,3},{5,4},{6,5},{7,6},{8,7},{9,8},{10,9},{11,1... | collective-permute-start | bytes 147464 | tf_op jit(solution)/shard_map/ppermute | solution.py:19
  295.2 13.9 %reshape.111 = f32[3,2,2,16,2,64,2]{6,5,4,3,2,1,0:T(8,128)} reshape(f32[3,4,32,128]{3,2,1,0:T(8,128)S(1)} %copy.205) | data formatting | bytes 393216 | tf_op jit(solution)/shard_map/reshape | solution.py:115
  309.2 5.5 %reduce_sum.65 = f32[3,2,16,64]{3,2,1,0:T(8,128)S(1)} reduce(f32[3,2,2,16,2,64,2]{6,5,4,3,2,1,0:T(8,128)} %reshape.111, f32[]{:T(128)} %constant.27.clone.1), dimensions={2,4,6}, to_apply=%region_2.0 | reduce | flops 43008 | bytes 221188 | tf_op jit(solution)/shard_map/reduce_sum | solution.py:115
  318.3 8.6 %collective-permute-start.44 = (f32[3,1,16,64]{3,2,1,0:T(8,128)S(1)}, f32[3,1,16,64]{3,2,1,0:T(8,128)S(1)}, u32[]{:S(2)}, u32[]{:S(2)}) collective-permute-start(f32[3,1,16,64]{3,2,1,0:T(8,128)S(1)} %get-tuple-element.233), channel_id=1, source_target_pairs={{1,0},{2,1},{3,2},{4,3},{5,4},{6,5},{7,6},{8,7},{9,8},{10,9},{11,1... | collective-permute-start | bytes 36872 | tf_op jit(solution)/shard_map/ppermute | solution.py:19
  328.8 8.1 %collective-permute-start.22 = (f32[3,1,16,64]{3,2,1,0:T(8,128)S(1)}, f32[3,1,16,64]{3,2,1,0:T(8,128)S(1)}, u32[]{:S(2)}, u32[]{:S(2)}) collective-permute-start(f32[3,1,16,64]{3,2,1,0:T(8,128)S(1)} %get-tuple-element.253), channel_id=1, source_target_pairs={{1,0},{2,1},{3,2},{4,3},{5,4},{6,5},{7,6},{8,7},{9,8},{10,9},{11,1... | collective-permute-start | bytes 36872 | tf_op jit(solution)/shard_map/ppermute | solution.py:19
  342.1 8.4 %collective-permute-start.24 = (f32[3,1,16,64]{3,2,1,0:T(8,128)S(1)}, f32[3,1,16,64]{3,2,1,0:T(8,128)S(1)}, u32[]{:S(2)}, u32[]{:S(2)}) collective-permute-start(f32[3,1,16,64]{3,2,1,0:T(8,128)S(1)} %get-tuple-element.251), channel_id=1, source_target_pairs={{1,0},{2,1},{3,2},{4,3},{5,4},{6,5},{7,6},{8,7},{9,8},{10,9},{11,1... | collective-permute-start | bytes 36872 | tf_op jit(solution)/shard_map/ppermute | solution.py:19
  354.8 8.4 %collective-permute-start.26 = (f32[3,1,16,64]{3,2,1,0:T(8,128)S(1)}, f32[3,1,16,64]{3,2,1,0:T(8,128)S(1)}, u32[]{:S(2)}, u32[]{:S(2)}) collective-permute-start(f32[3,1,16,64]{3,2,1,0:T(8,128)S(1)} %get-tuple-element.249), channel_id=1, source_target_pairs={{1,0},{2,1},{3,2},{4,3},{5,4},{6,5},{7,6},{8,7},{9,8},{10,9},{11,1... | collective-permute-start | bytes 36872 | tf_op jit(solution)/shard_map/ppermute | solution.py:19
  370.3 8.7 %collective-permute-start.28 = (f32[3,1,32,128]{2,3,1,0:T(8,128)S(1)}, f32[3,1,32,128]{2,3,1,0:T(8,128)S(1)}, u32[]{:S(2)}, u32[]{:S(2)}) collective-permute-start(f32[3,1,32,128]{2,3,1,0:T(8,128)S(1)} %get-tuple-element.128), channel_id=1, source_target_pairs={{1,0},{2,1},{3,2},{4,3},{5,4},{6,5},{7,6},{8,7},{9,8},{10,9},{11,1... | collective-permute-start | bytes 147464 | tf_op jit(solution)/shard_map/ppermute | solution.py:19
  383.7 2.2 collective-permute-start.31
  387.2 8.6 %collective-permute-start.30 = (f32[3,1,32,128]{2,3,1,0:T(8,128)S(1)}, f32[3,1,32,128]{2,3,1,0:T(8,128)S(1)}, u32[]{:S(2)}, u32[]{:S(2)}) collective-permute-start(f32[3,1,32,128]{2,3,1,0:T(8,128)S(1)} %get-tuple-element.126), channel_id=1, source_target_pairs={{1,0},{2,1},{3,2},{4,3},{5,4},{6,5},{7,6},{8,7},{9,8},{10,9},{11,1... | collective-permute-start | bytes 147464 | tf_op jit(solution)/shard_map/ppermute | solution.py:19
  396.7 2.3 collective-permute-done.30
  400.0 3.0 multiply_reduce_fusion
  405.0 12.1 %all-to-all-start = ((f32[64,1,2]{2,1,0:T(1,128)}), f32[64,1,2]{2,1,0:T(1,128)S(1)}, u32[]{:S(2)}, u32[]{:S(2)}) async-start(f32[64,1,2]{2,1,0:T(1,128)} %broadcast_in_dim.20), calls=%async_computation | async-start | bytes 65536 | tf_op jit(solution)/shard_map/all_to_all | solution.py:32
  417.1 2.1 copy.211
  419.2 6.5 %all-to-all-done = f32[64,1,2]{2,1,0:T(1,128)S(1)} async-done(((f32[64,1,2]{2,1,0:T(1,128)}), f32[64,1,2]{2,1,0:T(1,128)S(1)}, u32[]{:S(2)}, u32[]{:S(2)}) %all-to-all-start) | async-done | bytes 544 | tf_op jit(solution)/shard_map/all_to_all | solution.py:32
  (356 shorter events, 106.2 us)
Async XLA Ops:
  9.6 28.3 %collective-permute-start.3 = (f32[1,16,64]{2,1,0:T(8,128)S(1)}, f32[1,16,64]{2,1,0:T(8,128)S(1)}, u32[]{:S(2)}, u32[]{:S(2)}) collective-permute-start(f32[1,16,64]{2,1,0:T(8,128)S(1)} %slice.1698), channel_id=1, source_target_pairs={{0,1},{1,2},{2,3},{3,4},{4,5},{5,6},{6,7},{7,8},{8,9},{9,10},{10,1... | collective-permute-start | bytes 12296 | tf_op jit(solution)/shard_map/ppermute | solution.py:27
  13.0 41.9 %collective-permute-start = (f32[1,32,128]{2,1,0:T(8,128)S(1)}, f32[1,32,128]{2,1,0:T(8,128)S(1)}, u32[]{:S(2)}, u32[]{:S(2)}) collective-permute-start(f32[1,32,128]{2,1,0:T(8,128)S(1)} %slice.1674), channel_id=1, source_target_pairs={{0,1},{1,2},{2,3},{3,4},{4,5},{5,6},{6,7},{7,8},{8,9},{9,10},{10,1... | collective-permute-start | bytes 49160 | tf_op jit(solution)/shard_map/ppermute | solution.py:27
  38.1 16.7 %collective-permute-start.32 = (f32[3,1,16,64]{3,2,1,0:T(8,128)S(1)}, f32[3,1,16,64]{3,2,1,0:T(8,128)S(1)}, u32[]{:S(2)}, u32[]{:S(2)}) collective-permute-start(f32[3,1,16,64]{3,2,1,0:T(8,128)S(1)} %get-tuple-element.247), channel_id=1, source_target_pairs={{1,0},{2,1},{3,2},{4,3},{5,4},{6,5},{7,6},{8,7},{9,8},{10,9},{11,1... | collective-permute-start | bytes 36872 | tf_op jit(solution)/shard_map/ppermute | solution.py:19
  44.7 9.9 %collective-permute-start.33 = (f32[3,1,16,64]{3,2,1,0:T(8,128)S(1)}, f32[3,1,16,64]{3,2,1,0:T(8,128)S(1)}, u32[]{:S(2)}, u32[]{:S(2)}) collective-permute-start(f32[3,1,16,64]{3,2,1,0:T(8,128)S(1)} %get-tuple-element.248), channel_id=1, source_target_pairs={{0,1},{1,2},{2,3},{3,4},{4,5},{5,6},{6,7},{7,8},{8,9},{9,10},{10,1... | collective-permute-start | bytes 36872 | tf_op jit(solution)/shard_map/ppermute | solution.py:16
  55.5 12.0 %collective-permute-start.34 = (f32[3,1,16,64]{3,2,1,0:T(8,128)S(1)}, f32[3,1,16,64]{3,2,1,0:T(8,128)S(1)}, u32[]{:S(2)}, u32[]{:S(2)}) collective-permute-start(f32[3,1,16,64]{3,2,1,0:T(8,128)S(1)} %get-tuple-element.245), channel_id=1, source_target_pairs={{1,0},{2,1},{3,2},{4,3},{5,4},{6,5},{7,6},{8,7},{9,8},{10,9},{11,1... | collective-permute-start | bytes 36872 | tf_op jit(solution)/shard_map/ppermute | solution.py:19
  57.4 9.9 %collective-permute-start.35 = (f32[3,1,16,64]{3,2,1,0:T(8,128)S(1)}, f32[3,1,16,64]{3,2,1,0:T(8,128)S(1)}, u32[]{:S(2)}, u32[]{:S(2)}) collective-permute-start(f32[3,1,16,64]{3,2,1,0:T(8,128)S(1)} %get-tuple-element.246), channel_id=1, source_target_pairs={{0,1},{1,2},{2,3},{3,4},{4,5},{5,6},{6,7},{7,8},{8,9},{9,10},{10,1... | collective-permute-start | bytes 36872 | tf_op jit(solution)/shard_map/ppermute | solution.py:16
  67.8 10.8 %collective-permute-start.37 = (f32[3,1,16,64]{3,2,1,0:T(8,128)S(1)}, f32[3,1,16,64]{3,2,1,0:T(8,128)S(1)}, u32[]{:S(2)}, u32[]{:S(2)}) collective-permute-start(f32[3,1,16,64]{3,2,1,0:T(8,128)S(1)} %get-tuple-element.244), channel_id=1, source_target_pairs={{0,1},{1,2},{2,3},{3,4},{4,5},{5,6},{6,7},{7,8},{8,9},{9,10},{10,1... | collective-permute-start | bytes 36872 | tf_op jit(solution)/shard_map/ppermute | solution.py:16
  70.5 9.6 %collective-permute-start.36 = (f32[3,1,16,64]{3,2,1,0:T(8,128)S(1)}, f32[3,1,16,64]{3,2,1,0:T(8,128)S(1)}, u32[]{:S(2)}, u32[]{:S(2)}) collective-permute-start(f32[3,1,16,64]{3,2,1,0:T(8,128)S(1)} %get-tuple-element.243), channel_id=1, source_target_pairs={{1,0},{2,1},{3,2},{4,3},{5,4},{6,5},{7,6},{8,7},{9,8},{10,9},{11,1... | collective-permute-start | bytes 36872 | tf_op jit(solution)/shard_map/ppermute | solution.py:19
  80.4 20.6 %collective-permute-start.39 = (f32[3,1,16,64]{3,2,1,0:T(8,128)S(1)}, f32[3,1,16,64]{3,2,1,0:T(8,128)S(1)}, u32[]{:S(2)}, u32[]{:S(2)}) collective-permute-start(f32[3,1,16,64]{3,2,1,0:T(8,128)S(1)} %get-tuple-element.242), channel_id=1, source_target_pairs={{0,1},{1,2},{2,3},{3,4},{4,5},{5,6},{6,7},{7,8},{8,9},{9,10},{10,1... | collective-permute-start | bytes 36872 | tf_op jit(solution)/shard_map/ppermute | solution.py:16
  82.5 31.7 %collective-permute-start.1 = (f32[3,1,32,128]{2,3,1,0:T(8,128)}, f32[3,1,32,128]{2,3,1,0:T(8,128)S(1)}, u32[]{:S(2)}, u32[]{:S(2)}) collective-permute-start(f32[3,1,32,128]{2,3,1,0:T(8,128)} %get-tuple-element.142), channel_id=1, source_target_pairs={{1,0},{2,1},{3,2},{4,3},{5,4},{6,5},{7,6},{8,7},{9,8},{10,9},{11,1... | collective-permute-start | bytes 147464 | tf_op jit(solution)/shard_map/ppermute | solution.py:19
  91.0 22.8 %collective-permute-start.2 = (f32[3,1,32,128]{2,3,1,0:T(8,128)}, f32[3,1,32,128]{2,3,1,0:T(8,128)S(1)}, u32[]{:S(2)}, u32[]{:S(2)}) collective-permute-start(f32[3,1,32,128]{2,3,1,0:T(8,128)} %get-tuple-element.143), channel_id=1, source_target_pairs={{0,1},{1,2},{2,3},{3,4},{4,5},{5,6},{6,7},{7,8},{8,9},{9,10},{10,1... | collective-permute-start | bytes 147464 | tf_op jit(solution)/shard_map/ppermute | solution.py:16
  92.9 9.6 %collective-permute-start.38 = (f32[3,1,16,64]{3,2,1,0:T(8,128)S(1)}, f32[3,1,16,64]{3,2,1,0:T(8,128)S(1)}, u32[]{:S(2)}, u32[]{:S(2)}) collective-permute-start(f32[3,1,16,64]{3,2,1,0:T(8,128)S(1)} %get-tuple-element.241), channel_id=1, source_target_pairs={{1,0},{2,1},{3,2},{4,3},{5,4},{6,5},{7,6},{8,7},{9,8},{10,9},{11,1... | collective-permute-start | bytes 36872 | tf_op jit(solution)/shard_map/ppermute | solution.py:19
  103.4 18.5 %collective-permute-start.40 = (f32[3,1,16,64]{3,2,1,0:T(8,128)S(1)}, f32[3,1,16,64]{3,2,1,0:T(8,128)S(1)}, u32[]{:S(2)}, u32[]{:S(2)}) collective-permute-start(f32[3,1,16,64]{3,2,1,0:T(8,128)S(1)} %get-tuple-element.239), channel_id=1, source_target_pairs={{1,0},{2,1},{3,2},{4,3},{5,4},{6,5},{7,6},{8,7},{9,8},{10,9},{11,1... | collective-permute-start | bytes 36872 | tf_op jit(solution)/shard_map/ppermute | solution.py:19
  111.8 9.9 %collective-permute-start.41 = (f32[3,1,16,64]{3,2,1,0:T(8,128)S(1)}, f32[3,1,16,64]{3,2,1,0:T(8,128)S(1)}, u32[]{:S(2)}, u32[]{:S(2)}) collective-permute-start(f32[3,1,16,64]{3,2,1,0:T(8,128)S(1)} %get-tuple-element.240), channel_id=1, source_target_pairs={{0,1},{1,2},{2,3},{3,4},{4,5},{5,6},{6,7},{7,8},{8,9},{9,10},{10,1... | collective-permute-start | bytes 36872 | tf_op jit(solution)/shard_map/ppermute | solution.py:16
  124.4 14.2 %collective-permute-start.4 = (f32[3,1,32,128]{2,3,1,0:T(8,128)S(1)}, f32[3,1,32,128]{2,3,1,0:T(8,128)S(1)}, u32[]{:S(2)}, u32[]{:S(2)}) collective-permute-start(f32[3,1,32,128]{2,3,1,0:T(8,128)S(1)} %get-tuple-element.140), channel_id=1, source_target_pairs={{1,0},{2,1},{3,2},{4,3},{5,4},{6,5},{7,6},{8,7},{9,8},{10,9},{11,1... | collective-permute-start | bytes 147464 | tf_op jit(solution)/shard_map/ppermute | solution.py:19
  126.3 11.8 %collective-permute-start.5 = (f32[3,1,32,128]{2,3,1,0:T(8,128)S(1)}, f32[3,1,32,128]{2,3,1,0:T(8,128)S(1)}, u32[]{:S(2)}, u32[]{:S(2)}) collective-permute-start(f32[3,1,32,128]{2,3,1,0:T(8,128)S(1)} %get-tuple-element.141), channel_id=1, source_target_pairs={{0,1},{1,2},{2,3},{3,4},{4,5},{5,6},{6,7},{7,8},{8,9},{9,10},{10,1... | collective-permute-start | bytes 147464 | tf_op jit(solution)/shard_map/ppermute | solution.py:16
  161.5 20.2 %collective-permute-start.7 = (f32[3,1,16,64]{3,2,1,0:T(8,128)S(1)}, f32[3,1,16,64]{3,2,1,0:T(8,128)S(1)}, u32[]{:S(2)}, u32[]{:S(2)}) collective-permute-start(f32[3,1,16,64]{3,2,1,0:T(8,128)S(1)} %get-tuple-element.260), channel_id=1, source_target_pairs={{0,1},{1,2},{2,3},{3,4},{4,5},{5,6},{6,7},{7,8},{8,9},{9,10},{10,1... | collective-permute-start | bytes 36872 | tf_op jit(solution)/shard_map/ppermute | solution.py:16
  163.5 19.9 %collective-permute-start.42 = (f32[3,1,16,64]{3,2,1,0:T(8,128)S(1)}, f32[3,1,16,64]{3,2,1,0:T(8,128)S(1)}, u32[]{:S(2)}, u32[]{:S(2)}) collective-permute-start(f32[3,1,16,64]{3,2,1,0:T(8,128)S(1)} %get-tuple-element.236), channel_id=1, source_target_pairs={{1,0},{2,1},{3,2},{4,3},{5,4},{6,5},{7,6},{8,7},{9,8},{10,9},{11,1... | collective-permute-start | bytes 36872 | tf_op jit(solution)/shard_map/ppermute | solution.py:19
  171.6 11.6 %collective-permute-start.43 = (f32[3,1,16,64]{3,2,1,0:T(8,128)S(1)}, f32[3,1,16,64]{3,2,1,0:T(8,128)S(1)}, u32[]{:S(2)}, u32[]{:S(2)}) collective-permute-start(f32[3,1,16,64]{3,2,1,0:T(8,128)S(1)} %get-tuple-element.237), channel_id=1, source_target_pairs={{0,1},{1,2},{2,3},{3,4},{4,5},{5,6},{6,7},{7,8},{8,9},{9,10},{10,1... | collective-permute-start | bytes 36872 | tf_op jit(solution)/shard_map/ppermute | solution.py:16
  173.5 9.6 %collective-permute-start.6 = (f32[3,1,16,64]{3,2,1,0:T(8,128)S(1)}, f32[3,1,16,64]{3,2,1,0:T(8,128)S(1)}, u32[]{:S(2)}, u32[]{:S(2)}) collective-permute-start(f32[3,1,16,64]{3,2,1,0:T(8,128)S(1)} %get-tuple-element.259), channel_id=1, source_target_pairs={{1,0},{2,1},{3,2},{4,3},{5,4},{6,5},{7,6},{8,7},{9,8},{10,9},{11,1... | collective-permute-start | bytes 36872 | tf_op jit(solution)/shard_map/ppermute | solution.py:19
  184.8 10.4 %collective-permute-start.9 = (f32[3,1,16,64]{3,2,1,0:T(8,128)S(1)}, f32[3,1,16,64]{3,2,1,0:T(8,128)S(1)}, u32[]{:S(2)}, u32[]{:S(2)}) collective-permute-start(f32[3,1,16,64]{3,2,1,0:T(8,128)S(1)} %get-tuple-element.258), channel_id=1, source_target_pairs={{0,1},{1,2},{2,3},{3,4},{4,5},{5,6},{6,7},{7,8},{8,9},{9,10},{10,1... | collective-permute-start | bytes 36872 | tf_op jit(solution)/shard_map/ppermute | solution.py:16
  186.8 9.9 %collective-permute-start.8 = (f32[3,1,16,64]{3,2,1,0:T(8,128)S(1)}, f32[3,1,16,64]{3,2,1,0:T(8,128)S(1)}, u32[]{:S(2)}, u32[]{:S(2)}) collective-permute-start(f32[3,1,16,64]{3,2,1,0:T(8,128)S(1)} %get-tuple-element.257), channel_id=1, source_target_pairs={{1,0},{2,1},{3,2},{4,3},{5,4},{6,5},{7,6},{8,7},{9,8},{10,9},{11,1... | collective-permute-start | bytes 36872 | tf_op jit(solution)/shard_map/ppermute | solution.py:19
  197.0 10.4 %collective-permute-start.11 = (f32[3,1,16,64]{3,2,1,0:T(8,128)S(1)}, f32[3,1,16,64]{3,2,1,0:T(8,128)S(1)}, u32[]{:S(2)}, u32[]{:S(2)}) collective-permute-start(f32[3,1,16,64]{3,2,1,0:T(8,128)S(1)} %get-tuple-element.256), channel_id=1, source_target_pairs={{0,1},{1,2},{2,3},{3,4},{4,5},{5,6},{6,7},{7,8},{8,9},{9,10},{10,1... | collective-permute-start | bytes 36872 | tf_op jit(solution)/shard_map/ppermute | solution.py:16
  198.9 9.9 %collective-permute-start.10 = (f32[3,1,16,64]{3,2,1,0:T(8,128)S(1)}, f32[3,1,16,64]{3,2,1,0:T(8,128)S(1)}, u32[]{:S(2)}, u32[]{:S(2)}) collective-permute-start(f32[3,1,16,64]{3,2,1,0:T(8,128)S(1)} %get-tuple-element.255), channel_id=1, source_target_pairs={{1,0},{2,1},{3,2},{4,3},{5,4},{6,5},{7,6},{8,7},{9,8},{10,9},{11,1... | collective-permute-start | bytes 36872 | tf_op jit(solution)/shard_map/ppermute | solution.py:19
  212.1 12.7 %collective-permute-start.13 = (f32[3,1,32,128]{2,3,1,0:T(8,128)S(1)}, f32[3,1,32,128]{2,3,1,0:T(8,128)S(1)}, u32[]{:S(2)}, u32[]{:S(2)}) collective-permute-start(f32[3,1,32,128]{2,3,1,0:T(8,128)S(1)} %get-tuple-element.139), channel_id=1, source_target_pairs={{0,1},{1,2},{2,3},{3,4},{4,5},{5,6},{6,7},{7,8},{8,9},{9,10},{10,1... | collective-permute-start | bytes 147464 | tf_op jit(solution)/shard_map/ppermute | solution.py:16
  214.0 12.5 %collective-permute-start.12 = (f32[3,1,32,128]{2,3,1,0:T(8,128)S(1)}, f32[3,1,32,128]{2,3,1,0:T(8,128)S(1)}, u32[]{:S(2)}, u32[]{:S(2)}) collective-permute-start(f32[3,1,32,128]{2,3,1,0:T(8,128)S(1)} %get-tuple-element.138), channel_id=1, source_target_pairs={{1,0},{2,1},{3,2},{4,3},{5,4},{6,5},{7,6},{8,7},{9,8},{10,9},{11,1... | collective-permute-start | bytes 147464 | tf_op jit(solution)/shard_map/ppermute | solution.py:19
  229.5 13.7 %collective-permute-start.15 = (f32[3,1,32,128]{2,3,1,0:T(8,128)S(1)}, f32[3,1,32,128]{2,3,1,0:T(8,128)S(1)}, u32[]{:S(2)}, u32[]{:S(2)}) collective-permute-start(f32[3,1,32,128]{2,3,1,0:T(8,128)S(1)} %get-tuple-element.137), channel_id=1, source_target_pairs={{0,1},{1,2},{2,3},{3,4},{4,5},{5,6},{6,7},{7,8},{8,9},{9,10},{10,1... | collective-permute-start | bytes 147464 | tf_op jit(solution)/shard_map/ppermute | solution.py:16
  231.4 12.9 %collective-permute-start.14 = (f32[3,1,32,128]{2,3,1,0:T(8,128)S(1)}, f32[3,1,32,128]{2,3,1,0:T(8,128)S(1)}, u32[]{:S(2)}, u32[]{:S(2)}) collective-permute-start(f32[3,1,32,128]{2,3,1,0:T(8,128)S(1)} %get-tuple-element.136), channel_id=1, source_target_pairs={{1,0},{2,1},{3,2},{4,3},{5,4},{6,5},{7,6},{8,7},{9,8},{10,9},{11,1... | collective-permute-start | bytes 147464 | tf_op jit(solution)/shard_map/ppermute | solution.py:19
  246.2 12.8 %collective-permute-start.17 = (f32[3,1,32,128]{2,3,1,0:T(8,128)S(1)}, f32[3,1,32,128]{2,3,1,0:T(8,128)S(1)}, u32[]{:S(2)}, u32[]{:S(2)}) collective-permute-start(f32[3,1,32,128]{2,3,1,0:T(8,128)S(1)} %get-tuple-element.135), channel_id=1, source_target_pairs={{0,1},{1,2},{2,3},{3,4},{4,5},{5,6},{6,7},{7,8},{8,9},{9,10},{10,1... | collective-permute-start | bytes 147464 | tf_op jit(solution)/shard_map/ppermute | solution.py:16
  248.1 12.0 %collective-permute-start.16 = (f32[3,1,32,128]{2,3,1,0:T(8,128)S(1)}, f32[3,1,32,128]{2,3,1,0:T(8,128)S(1)}, u32[]{:S(2)}, u32[]{:S(2)}) collective-permute-start(f32[3,1,32,128]{2,3,1,0:T(8,128)S(1)} %get-tuple-element.134), channel_id=1, source_target_pairs={{1,0},{2,1},{3,2},{4,3},{5,4},{6,5},{7,6},{8,7},{9,8},{10,9},{11,1... | collective-permute-start | bytes 147464 | tf_op jit(solution)/shard_map/ppermute | solution.py:19
  262.0 12.3 %collective-permute-start.19 = (f32[3,1,32,128]{2,3,1,0:T(8,128)S(1)}, f32[3,1,32,128]{2,3,1,0:T(8,128)S(1)}, u32[]{:S(2)}, u32[]{:S(2)}) collective-permute-start(f32[3,1,32,128]{2,3,1,0:T(8,128)S(1)} %get-tuple-element.133), channel_id=1, source_target_pairs={{0,1},{1,2},{2,3},{3,4},{4,5},{5,6},{6,7},{7,8},{8,9},{9,10},{10,1... | collective-permute-start | bytes 147464 | tf_op jit(solution)/shard_map/ppermute | solution.py:16
  263.9 11.8 %collective-permute-start.18 = (f32[3,1,32,128]{2,3,1,0:T(8,128)S(1)}, f32[3,1,32,128]{2,3,1,0:T(8,128)S(1)}, u32[]{:S(2)}, u32[]{:S(2)}) collective-permute-start(f32[3,1,32,128]{2,3,1,0:T(8,128)S(1)} %get-tuple-element.132), channel_id=1, source_target_pairs={{1,0},{2,1},{3,2},{4,3},{5,4},{6,5},{7,6},{8,7},{9,8},{10,9},{11,1... | collective-permute-start | bytes 147464 | tf_op jit(solution)/shard_map/ppermute | solution.py:19
  277.6 12.3 %collective-permute-start.21 = (f32[3,1,32,128]{2,3,1,0:T(8,128)S(1)}, f32[3,1,32,128]{2,3,1,0:T(8,128)S(1)}, u32[]{:S(2)}, u32[]{:S(2)}) collective-permute-start(f32[3,1,32,128]{2,3,1,0:T(8,128)S(1)} %get-tuple-element.131), channel_id=1, source_target_pairs={{0,1},{1,2},{2,3},{3,4},{4,5},{5,6},{6,7},{7,8},{8,9},{9,10},{10,1... | collective-permute-start | bytes 147464 | tf_op jit(solution)/shard_map/ppermute | solution.py:16
  279.5 11.8 %collective-permute-start.20 = (f32[3,1,32,128]{2,3,1,0:T(8,128)S(1)}, f32[3,1,32,128]{2,3,1,0:T(8,128)S(1)}, u32[]{:S(2)}, u32[]{:S(2)}) collective-permute-start(f32[3,1,32,128]{2,3,1,0:T(8,128)S(1)} %get-tuple-element.130), channel_id=1, source_target_pairs={{1,0},{2,1},{3,2},{4,3},{5,4},{6,5},{7,6},{8,7},{9,8},{10,9},{11,1... | collective-permute-start | bytes 147464 | tf_op jit(solution)/shard_map/ppermute | solution.py:19
  316.3 20.6 %collective-permute-start.23 = (f32[3,1,16,64]{3,2,1,0:T(8,128)S(1)}, f32[3,1,16,64]{3,2,1,0:T(8,128)S(1)}, u32[]{:S(2)}, u32[]{:S(2)}) collective-permute-start(f32[3,1,16,64]{3,2,1,0:T(8,128)S(1)} %get-tuple-element.254), channel_id=1, source_target_pairs={{0,1},{1,2},{2,3},{3,4},{4,5},{5,6},{6,7},{7,8},{8,9},{9,10},{10,1... | collective-permute-start | bytes 36872 | tf_op jit(solution)/shard_map/ppermute | solution.py:16
  318.3 20.3 %collective-permute-start.44 = (f32[3,1,16,64]{3,2,1,0:T(8,128)S(1)}, f32[3,1,16,64]{3,2,1,0:T(8,128)S(1)}, u32[]{:S(2)}, u32[]{:S(2)}) collective-permute-start(f32[3,1,16,64]{3,2,1,0:T(8,128)S(1)} %get-tuple-element.233), channel_id=1, source_target_pairs={{1,0},{2,1},{3,2},{4,3},{5,4},{6,5},{7,6},{8,7},{9,8},{10,9},{11,1... | collective-permute-start | bytes 36872 | tf_op jit(solution)/shard_map/ppermute | solution.py:19
  326.9 10.2 %collective-permute-start.45 = (f32[3,1,16,64]{3,2,1,0:T(8,128)S(1)}, f32[3,1,16,64]{3,2,1,0:T(8,128)S(1)}, u32[]{:S(2)}, u32[]{:S(2)}) collective-permute-start(f32[3,1,16,64]{3,2,1,0:T(8,128)S(1)} %get-tuple-element.234), channel_id=1, source_target_pairs={{0,1},{1,2},{2,3},{3,4},{4,5},{5,6},{6,7},{7,8},{8,9},{9,10},{10,1... | collective-permute-start | bytes 36872 | tf_op jit(solution)/shard_map/ppermute | solution.py:16
  328.8 9.6 %collective-permute-start.22 = (f32[3,1,16,64]{3,2,1,0:T(8,128)S(1)}, f32[3,1,16,64]{3,2,1,0:T(8,128)S(1)}, u32[]{:S(2)}, u32[]{:S(2)}) collective-permute-start(f32[3,1,16,64]{3,2,1,0:T(8,128)S(1)} %get-tuple-element.253), channel_id=1, source_target_pairs={{1,0},{2,1},{3,2},{4,3},{5,4},{6,5},{7,6},{8,7},{9,8},{10,9},{11,1... | collective-permute-start | bytes 36872 | tf_op jit(solution)/shard_map/ppermute | solution.py:19
  339.3 25.8 %copy-start.22 = (f32[3,16,64]{2,1,0:T(8,128)}, f32[3,16,64]{2,1,0:T(8,128)S(1)}, u32[]{:S(2)}) copy-start(f32[3,16,64]{2,1,0:T(8,128)S(1)} %get-tuple-element.264) | copy-start | bytes 36868
  340.1 10.4 %collective-permute-start.25 = (f32[3,1,16,64]{3,2,1,0:T(8,128)S(1)}, f32[3,1,16,64]{3,2,1,0:T(8,128)S(1)}, u32[]{:S(2)}, u32[]{:S(2)}) collective-permute-start(f32[3,1,16,64]{3,2,1,0:T(8,128)S(1)} %get-tuple-element.252), channel_id=1, source_target_pairs={{0,1},{1,2},{2,3},{3,4},{4,5},{5,6},{6,7},{7,8},{8,9},{9,10},{10,1... | collective-permute-start | bytes 36872 | tf_op jit(solution)/shard_map/ppermute | solution.py:16
  342.1 9.9 %collective-permute-start.24 = (f32[3,1,16,64]{3,2,1,0:T(8,128)S(1)}, f32[3,1,16,64]{3,2,1,0:T(8,128)S(1)}, u32[]{:S(2)}, u32[]{:S(2)}) collective-permute-start(f32[3,1,16,64]{3,2,1,0:T(8,128)S(1)} %get-tuple-element.251), channel_id=1, source_target_pairs={{1,0},{2,1},{3,2},{4,3},{5,4},{6,5},{7,6},{8,7},{9,8},{10,9},{11,1... | collective-permute-start | bytes 36872 | tf_op jit(solution)/shard_map/ppermute | solution.py:19
  352.3 11.0 %collective-permute-start.27 = (f32[3,1,16,64]{3,2,1,0:T(8,128)S(1)}, f32[3,1,16,64]{3,2,1,0:T(8,128)S(1)}, u32[]{:S(2)}, u32[]{:S(2)}) collective-permute-start(f32[3,1,16,64]{3,2,1,0:T(8,128)S(1)} %get-tuple-element.250), channel_id=1, source_target_pairs={{0,1},{1,2},{2,3},{3,4},{4,5},{5,6},{6,7},{7,8},{8,9},{9,10},{10,1... | collective-permute-start | bytes 36872 | tf_op jit(solution)/shard_map/ppermute | solution.py:16
  354.8 9.9 %collective-permute-start.26 = (f32[3,1,16,64]{3,2,1,0:T(8,128)S(1)}, f32[3,1,16,64]{3,2,1,0:T(8,128)S(1)}, u32[]{:S(2)}, u32[]{:S(2)}) collective-permute-start(f32[3,1,16,64]{3,2,1,0:T(8,128)S(1)} %get-tuple-element.249), channel_id=1, source_target_pairs={{1,0},{2,1},{3,2},{4,3},{5,4},{6,5},{7,6},{8,7},{9,8},{10,9},{11,1... | collective-permute-start | bytes 36872 | tf_op jit(solution)/shard_map/ppermute | solution.py:19
  367.5 12.1 %collective-permute-start.29 = (f32[3,1,32,128]{2,3,1,0:T(8,128)S(1)}, f32[3,1,32,128]{2,3,1,0:T(8,128)S(1)}, u32[]{:S(2)}, u32[]{:S(2)}) collective-permute-start(f32[3,1,32,128]{2,3,1,0:T(8,128)S(1)} %get-tuple-element.129), channel_id=1, source_target_pairs={{0,1},{1,2},{2,3},{3,4},{4,5},{5,6},{6,7},{7,8},{8,9},{9,10},{10,1... | collective-permute-start | bytes 147464 | tf_op jit(solution)/shard_map/ppermute | solution.py:16
  370.3 11.6 %collective-permute-start.28 = (f32[3,1,32,128]{2,3,1,0:T(8,128)S(1)}, f32[3,1,32,128]{2,3,1,0:T(8,128)S(1)}, u32[]{:S(2)}, u32[]{:S(2)}) collective-permute-start(f32[3,1,32,128]{2,3,1,0:T(8,128)S(1)} %get-tuple-element.128), channel_id=1, source_target_pairs={{1,0},{2,1},{3,2},{4,3},{5,4},{6,5},{7,6},{8,7},{9,8},{10,9},{11,1... | collective-permute-start | bytes 147464 | tf_op jit(solution)/shard_map/ppermute | solution.py:19
  383.7 12.6 %collective-permute-start.31 = (f32[3,1,32,128]{2,3,1,0:T(8,128)S(1)}, f32[3,1,32,128]{2,3,1,0:T(8,128)S(1)}, u32[]{:S(2)}, u32[]{:S(2)}) collective-permute-start(f32[3,1,32,128]{2,3,1,0:T(8,128)S(1)} %get-tuple-element.127), channel_id=1, source_target_pairs={{0,1},{1,2},{2,3},{3,4},{4,5},{5,6},{6,7},{7,8},{8,9},{9,10},{10,1... | collective-permute-start | bytes 147464 | tf_op jit(solution)/shard_map/ppermute | solution.py:16
  387.2 11.8 %collective-permute-start.30 = (f32[3,1,32,128]{2,3,1,0:T(8,128)S(1)}, f32[3,1,32,128]{2,3,1,0:T(8,128)S(1)}, u32[]{:S(2)}, u32[]{:S(2)}) collective-permute-start(f32[3,1,32,128]{2,3,1,0:T(8,128)S(1)} %get-tuple-element.126), channel_id=1, source_target_pairs={{1,0},{2,1},{3,2},{4,3},{5,4},{6,5},{7,6},{8,7},{9,8},{10,9},{11,1... | collective-permute-start | bytes 147464 | tf_op jit(solution)/shard_map/ppermute | solution.py:19
  405.0 20.7 %all-to-all-start = ((f32[64,1,2]{2,1,0:T(1,128)}), f32[64,1,2]{2,1,0:T(1,128)S(1)}, u32[]{:S(2)}, u32[]{:S(2)}) async-start(f32[64,1,2]{2,1,0:T(1,128)} %broadcast_in_dim.20), calls=%async_computation | async-start | bytes 65536 | tf_op jit(solution)/shard_map/all_to_all | solution.py:32
  (26 other events, 275.7 us)
where the time goes:
time: 432 us; the launch traced here: 428 us
  starting transfers between devices  236 us (55%)
  waiting for transfers between devices  66.1 us (15%)
  local copies, waits for them, and re-layouts  61.6 us (14%)
  other arithmetic  60.1 us (14%)
    ppermute x22, starting transfers between devices, extended(): lax.ppermute(lax.slice_in_dim(block, 0, width, axis=dim), axis, backward)  171 us
    ppermute x22, starting transfers between devices, extended(): lax.ppermute(lax.slice_in_dim(block, block.shape[dim] - width, None, axis...  46.7 us
    reshape x3, local copies, waits for them, and re-layouts, restrict_vector(): values.reshape(shape[0], shape[1] // 2, 2, shape[2] // 2, 2, shape[3] //...  42.4 us
    ppermute x22, waiting for transfers between devices, extended(): lax.ppermute(lax.slice_in_dim(block, block.shape[dim] - width, None, axis...  39.7 us
    ppermute x22, waiting for transfers between devices, extended(): lax.ppermute(lax.slice_in_dim(block, 0, width, axis=dim), axis, backward)  19.9 us
    reduce_sum x3, other arithmetic, restrict_vector(): values.reshape(shape[0], shape[1] // 2, 2, shape[2] // 2, 2, shape[3] //...  16.6 us
    all_to_all x1, starting transfers between devices, from_everyone(): lax.all_to_all(jnp.broadcast_to(x[None], (peers, *x.shape)), axis, 0, 0,...  12.1 us
  transfers between devices with their start and end apart: 47, of which 27 were waited for; matrix products, arithmetic and copies ran while one was open for 8% of the time, Pallas kernels for 0%

commit v1 on v0

v1 whole, which is shorter than its diff:
```python
import math

import jax
import jax.numpy as jnp
from jax import lax
from jax.experimental import pallas as pl
from jax.experimental.pallas import tpu as pltpu
from jax.sharding import PartitionSpec as P

ITERS = 2
SMOOTH = 2
CDEG = 4
FINE = (0.25, 2.0)
COARSE = (0.02, 2.0)


def coefficients(low_end, high_end, degree):
    centre = (high_end + low_end) / 2.0
    half = (high_end - low_end) / 2.0
    ratio = centre / half
    rho = 1.0 / ratio
    steps = []
    for _ in range(degree - 1):
        after = 1.0 / (2.0 * ratio - rho)
        steps.append((after * rho, 2.0 * after / half))
        rho = after
    return 1.0 / centre, steps, ratio


FIRST_F, STEPS_F, _ = coefficients(*FINE, SMOOTH)
FIRST_C, STEPS_C, RATIO_C = coefficients(*COARSE, 2 * CDEG)


def lanes(shape):
    return lax.broadcasted_iota(jnp.int32, shape, len(shape) - 1)


def ahead(v, axis, by=1):
    n = v.shape[axis]
    at = lax.broadcasted_iota(jnp.int32, v.shape, axis)
    return jnp.where(at < n - by, pltpu.roll(v, n - by, axis), 0.0)


def back(v, axis, by=1):
    at = lax.broadcasted_iota(jnp.int32, v.shape, axis)
    return jnp.where(at >= by, pltpu.roll(v, by, axis), 0.0)


def operate(u, m, step):
    low = [c[:-1] for c in u]
    gz = [c[1:] - l for c, l in zip(u, low)]
    gx0 = ahead(low[0], 2, step) - low[0]
    gy1 = ahead(low[1], 1) - low[1]
    s = m * (gx0 + gy1 + gz[2])
    inner = m[1:]
    si = s[1:]
    out = []
    for c in range(3):
        here = low[c][1:]
        fx = inner * (gx0[1:] if c == 0 else ahead(here, 2, step) - here)
        fy = inner * (gy1[1:] if c == 1 else ahead(here, 1) - here)
        fz = m * gz[c]
        if c == 0:
            fx = fx + si
        elif c == 1:
            fy = fy + si
        else:
            fz = fz + s
        out.append((fz[:-1] - fz[1:]) + (back(fy, 1) - fy) + (back(fx, 2, step) - fx))
    return out


def inverse(m, step):
    here = m[1:]
    below = m[:-1]
    by = back(here, 1)
    bx = back(here, 2, step)
    lap = (here + below) + (here + by) + (here + bx) + here
    inside = here > 0.0
    return [
        jnp.where(inside, 1.0 / jnp.where(inside, lap + d, 1.0), 0.0) for d in (bx, by, below)
    ]


def trim(v, n=1):
    return v[n : v.shape[0] - n]


def halve_rows(tmp, v):
    k, rows, _ = v.shape
    tmp[0:k] = v
    return tmp[0:k, pl.ds(0, rows // 2, stride=2), :] + tmp[0:k, pl.ds(1, rows // 2, stride=2), :]


def pack(even_sum, odd_sum):
    even = lanes(even_sum.shape) % 2 == 0
    ax = even_sum.ndim - 1
    near = jnp.where(even, even_sum, odd_sum)
    far = jnp.where(even, pltpu.roll(even_sum, 127, ax), pltpu.roll(odd_sum, 1, ax))
    return near + far


def pair_layers(v):
    return jnp.concatenate([v[i : i + 1] + v[i + 1 : i + 2] for i in range(0, v.shape[0], 2)], 0)


def spread(tmp, e):
    k, rows, _ = e.shape
    even = lanes(e.shape) % 2 == 0
    both = jnp.where(even, e, pltpu.roll(e, 1, 2))
    tmp[0:k, pl.ds(0, rows, stride=2), :] = both
    tmp[0:k, pl.ds(1, rows, stride=2), :] = both
    return tmp[0:k]


def layers(v, order):
    return jnp.concatenate([v[i : i + 1] for i in order], 0)


def by_side(flag, put, a, b):
    lower = flag == 0

    @pl.when(lower)
    def _():
        put(a, b)

    @pl.when(jnp.logical_not(lower))
    def _():
        put(b, a)


def first_kernel(par, f_ref, e_ref, a_ref, b_ref, x_ref, big_ref, small_ref, fe, me, tmp):
    for c in range(3):
        fe[c, 2:6] = f_ref[c]
    me[3:7] = 0.4 * e_ref[...]

    def take(up, down):
        for c in range(3):
            fe[c, 6:8] = up[2 * c : 2 * c + 2]
            fe[c, 0:2] = down[2 * c : 2 * c + 2]
        me[7:9] = 0.4 * up[6:8]
        me[0:3] = 0.4 * down[6:9]

    by_side(par[0], take, a_ref, b_ref)
    m = me[...]
    p = inverse(m, 1)
    r = [fe[c] for c in range(3)]
    w = [p[c] * r[c] * FIRST_F for c in range(3)]
    aw = operate(w, m[1:8], 1)
    r = [trim(r[c]) - aw[c] for c in range(3)]
    now, gain = STEPS_F[0]
    w2 = [now * trim(w[c]) + gain * (trim(p[c]) * r[c]) for c in range(3)]
    aw = operate(w2, m[2:7], 1)
    for c in range(3):
        x_ref[c] = w[c][2:6] + w2[c][1:5]
        done = trim(r[c]) - aw[c]
        big_ref[4 * c : 4 * c + 4] = done
        rc = halve_rows(tmp, pair_layers(done)) * 0.5
        fc = halve_rows(tmp, pair_layers(fe[c, 2:6])) * 0.5
        both = pack(rc, fc)
        small_ref[2 * c : 2 * c + 2] = both
        big_ref[17 + c, 0:16] = both[0]
        big_ref[17 + c, 16:32] = both[1]
    big_ref[12:17] = m[2:7]
    cm = halve_rows(tmp, pair_layers(m[1:7])) * 0.125
    cm = pack(cm, cm)
    small_ref[6:9] = cm
    big_ref[20, 0:16] = cm[0]
    big_ref[20, 16:32] = cm[1]
    big_ref[21, 0:16] = cm[2]
    big_ref[21, 16:32] = cm[2]


def second_kernel(
    par, f_ref, x_ref, mine, own, a1, b1, a2, b2, a3, b3,
    xo_ref, ro_ref, send_a, send_b, small_ref, mo_ref, cmo_ref, xc_ref, rc_ref, sum_ref,
    re, me, cf, cm, tmp,
):
    for c in range(3):
        re[c, 4:8] = mine[4 * c : 4 * c + 4]
        cf[c, 6:8] = own[2 * c : 2 * c + 2]
    me[5:9] = mine[13:17]
    cm[7:9] = own[7:9]

    def near(up, down):
        for c in range(3):
            re[c, 8:12] = up[4 * c : 4 * c + 4]
            re[c, 0:4] = down[4 * c : 4 * c + 4]
            for j in range(2):
                cf[c, 8 + j] = up[17 + c, 16 * j : 16 * j + 16]
                cf[c, 4 + j] = down[17 + c, 16 * j : 16 * j + 16]
        me[9:13] = up[13:17]
        me[0:5] = down[12:17]
        cm[9] = up[20, 16:32]
        cm[10] = up[21, 0:16]
        cm[5] = down[20, 16:32]
        cm[6] = down[21, 0:16]

    def second(up, down):
        for c in range(3):
            cf[c, 10:12] = up[2 * c : 2 * c + 2]
            cf[c, 2:4] = down[2 * c : 2 * c + 2]
        cm[11:13] = up[7:9]
        cm[3:5] = down[7:9]

    def third(up, down):
        for c in range(3):
            cf[c, 12:14] = up[2 * c : 2 * c + 2]
            cf[c, 0:2] = down[2 * c : 2 * c + 2]
        cm[13:15] = up[7:9]
        cm[0:3] = down[6:9]

    by_side(par[0], near, a1, b1)
    by_side(par[1], second, a2, b2)
    by_side(par[2], third, a3, b3)

    mc = cm[...]
    pc = inverse(mc, 2)
    r = [cf[c] for c in range(3)]
    w = [pc[c] * r[c] * FIRST_C for c in range(3)]
    e = [w[c][3:11] for c in range(3)]
    xc = [w[c][6:8] for c in range(3)]
    part = None
    for k in range(1, 7):
        aw = operate(w, mc[k : 15 - k], 2)
        r = [trim(r[c]) - aw[c] for c in range(3)]
        now, gain = STEPS_C[k - 1]
        if k == 4:
            odd = lanes((2, 16, 128)) % 2 == 1
            part = sum(
                jnp.sum(jnp.where(odd, xc[c] * (cf[c, 6:8] + r[c][2:4]), 0.0)) for c in range(3)
            )
        w = [now * trim(w[c]) + gain * (pc[c][k : 14 - k] * r[c]) for c in range(3)]
        if k <= 3:
            e = [e[c] + w[c][3 - k : 11 - k] for c in range(3)]
        xc = [xc[c] + w[c][6 - k : 8 - k] for c in range(3)]
    for c in range(3):
        xc_ref[c] = xc[c]
        rc_ref[c] = r[c]
    last = w

    m = me[...]
    order = [0] + [i for i in range(1, 7) for _ in range(2)] + [7]
    v = [layers(spread(tmp, e[c]), order) for c in range(3)]
    aw = operate(v, m, 1)
    p = inverse(m, 1)
    r = [re[c] - aw[c] for c in range(3)]
    now, gain = STEPS_F[0]
    w = [p[c] * r[c] * FIRST_F for c in range(3)]
    x = [x_ref[c] + v[c][5:9] + w[c][4:8] for c in range(3)]
    aw = operate(w, m[1:12], 1)
    r = [trim(r[c]) - aw[c] for c in range(3)]
    w = [now * trim(w[c]) + gain * (p[c][1:11] * r[c]) for c in range(3)]
    x = [x[c] + w[c][3:7] for c in range(3)]
    aw = operate(w, m[2:11], 1)
    r = [trim(r[c]) - aw[c] for c in range(3)]
    whole = sum(jnp.sum(x[c] * (f_ref[c] + r[c][2:6])) for c in range(3))
    w = [p[c][2:10] * r[c] * FIRST_F for c in range(3)]
    x = [x[c] + w[c][2:6] for c in range(3)]
    aw = operate(w, m[3:10], 1)
    r = [trim(r[c]) - aw[c] for c in range(3)]
    w = [now * trim(w[c]) + gain * (p[c][3:9] * r[c]) for c in range(3)]
    aw = operate(w, m[4:9], 1)
    for c in range(3):
        xo_ref[c] = x[c] + w[c][1:5]
        done = trim(r[c]) - aw[c]
        ro_ref[c] = done
        rc = halve_rows(tmp, pair_layers(done)) * 0.5
        at = lanes(rc.shape) % 2 == 0
        both = jnp.where(at, rc + pltpu.roll(rc, 127, 2), last[c])
        small_ref[2 * c : 2 * c + 2] = both
        for ref in (send_a, send_b):
            ref[3 + c, 0:16] = both[0]
            ref[3 + c, 16:32] = both[1]
    for c in range(3):
        send_a[c] = ro_ref[c, 3 - 3 * par[0]]
        send_b[c] = ro_ref[c, 3 * par[0]]
    mo_ref[...] = m[3:10]
    cmo_ref[...] = mc[2:13]
    at = lanes((1, 128))
    sum_ref[...] = jnp.where(at == 0, whole, 0.0) + jnp.where(at == 1, part, 0.0)


def third_kernel(
    par, x_ref, r_ref, own, m_ref, cm_ref, xc_ref, rc_ref, a1, b1, a2, b2,
    out_ref, coarse_ref, re, cf, tmp,
):
    for c in range(3):
        re[c, 1:5] = r_ref[c]
        cf[c, 4:6] = own[2 * c : 2 * c + 2]

    def near(up, down):
        for c in range(3):
            re[c, 5] = up[c]
            re[c, 0] = down[c]
            for j in range(2):
                cf[c, 6 + j] = up[3 + c, 16 * j : 16 * j + 16]
                cf[c, 2 + j] = down[3 + c, 16 * j : 16 * j + 16]

    def second(up, down):
        for c in range(3):
            cf[c, 8:10] = up[2 * c : 2 * c + 2]
            cf[c, 0:2] = down[2 * c : 2 * c + 2]

    by_side(par[0], near, a1, b1)
    by_side(par[1], second, a2, b2)

    mc = cm_ref[...]
    pc = inverse(mc, 2)

    def either(shape, a, b):
        return jnp.where(lanes(shape) % 2 == 0, a, b)

    r = [cf[c] for c in range(3)]
    w = [either(r[c].shape, pc[c] * r[c] * FIRST_C, r[c]) for c in range(3)]
    r = [
        jnp.concatenate([r[c][0:4], either((2, 16, 128), r[c][4:6], rc_ref[c]), r[c][6:10]], 0)
        for c in range(3)
    ]
    e = [w[c][3:7] for c in range(3)]
    for k in range(1, 4):
        aw = operate(w, mc[k : 11 - k], 2)
        r = [trim(r[c]) - aw[c] for c in range(3)]
        now, gain = STEPS_C[k - 1]
        if k == 1:
            line = (1, 1, 128)
            now = either(line, now, STEPS_C[6][0])
            gain = either(line, gain, STEPS_C[6][1])
        w = [now * trim(w[c]) + gain * (pc[c][k : 10 - k] * r[c]) for c in range(3)]
        if k == 1:
            col = lax.broadcasted_iota(jnp.int32, (128, 64), 1)
            row = lax.broadcasted_iota(jnp.int32, (128, 64), 0)
            pick = jnp.where(row == 2 * col + 1, 1.0, 0.0).astype(jnp.float32)
            for c in range(3):
                whole = (xc_ref[c] + w[c][3:5]).reshape(32, 128)
                coarse_ref[c] = jnp.dot(
                    whole, pick, precision=lax.Precision.HIGHEST, preferred_element_type=jnp.float32
                ).reshape(2, 16, 64)
        e = [e[c] + w[c][3 - k : 7 - k] for c in range(3)]

    m = m_ref[...]
    order = [0, 0, 1, 1, 2, 2, 3, 3]
    v = [layers(spread(tmp, e[c]), order) for c in range(3)]
    aw = operate(v, m, 1)
    p = inverse(m, 1)
    r = [re[c] - aw[c] for c in range(3)]
    now, gain = STEPS_F[0]
    w = [p[c] * r[c] * FIRST_F for c in range(3)]
    aw = operate(w, m[1:6], 1)
    for c in range(3):
        after = r[c][1:5] - aw[c]
        out_ref[c] = x_ref[c] + v[c][2:6] + (1.0 + now) * w[c][1:5] + gain * (p[c][1:5] * after)


def call(kernel, outs, scratch, par, *args, flops=1 << 22):
    return pl.pallas_call(
        kernel,
        out_shape=[jax.ShapeDtypeStruct(s, jnp.float32) for s in outs],
        in_specs=[pl.BlockSpec(memory_space=pltpu.SMEM)]
        + [pl.BlockSpec(memory_space=pltpu.VMEM)] * len(args),
        out_specs=[pl.BlockSpec(memory_space=pltpu.VMEM)] * len(outs),
        scratch_shapes=[pltpu.VMEM(s, jnp.float32) for s in scratch],
        cost_estimate=pl.CostEstimate(flops=flops, bytes_accessed=1 << 20, transcendentals=0),
    )(par, *args)


def swap(x, axis, distance, second):
    n = lax.axis_size(axis)
    pairs = []
    for i in range(n - distance):
        if (i // distance) % 2 == second:
            pairs += [(i, i + distance), (i + distance, i)]
    return lax.ppermute(x, axis, pairs)


def body(force, modulus):
    me = lax.axis_index("slab")
    par = jnp.stack([me % 2, (me // 2) % 2, (me // 3) % 2]).astype(jnp.int32)
    odd = me % 2

    def edge(side):
        f = lax.dynamic_slice_in_dim(force, 2 - 2 * side, 2, 1).reshape(6, 32, 128)
        return jnp.concatenate([f, lax.dynamic_slice_in_dim(modulus, 1 - side, 3, 0)], 0)

    a = swap(edge(odd), "slab", 1, 0)
    b = swap(edge(1 - odd), "slab", 1, 1)
    x, big, small = call(
        first_kernel,
        [(3, 4, 32, 128), (22, 32, 128), (9, 16, 128)],
        [(3, 8, 32, 128), (9, 32, 128), (4, 32, 128)],
        par, force, modulus, a, b,
    )
    got = [swap(big, "slab", 1, 0), swap(big, "slab", 1, 1)]
    got += [swap(small, "slab", d, h) for d in (2, 3) for h in (0, 1)]
    x, r, send_a, send_b, small, m, cm, xc, rc, part = call(
        second_kernel,
        [
            (3, 4, 32, 128), (3, 4, 32, 128), (6, 32, 128), (6, 32, 128), (6, 16, 128),
            (7, 32, 128), (11, 16, 128), (3, 2, 16, 128), (3, 2, 16, 128), (1, 128),
        ],
        [(3, 12, 32, 128), (13, 32, 128), (3, 14, 16, 128), (15, 16, 128), (8, 32, 128)],
        par, force, x, big, small, *got,
    )
    n = lax.axis_size("slab")
    got = [swap(send_a, "slab", 1, 0), swap(send_b, "slab", 1, 1)]
    got += [swap(small, "slab", 2, h) for h in (0, 1)]
    sums = lax.all_to_all(jnp.broadcast_to(part[None], (n, 1, 128)), "slab", 0, 0, tiled=True)
    fine, coarse = call(
        third_kernel,
        [(3, 4, 32, 128), (3, 2, 16, 64)],
        [(3, 6, 32, 128), (3, 10, 16, 128), (4, 32, 128)],
        par, x, r, small, m, cm, xc, rc, *got,
    )
    cells = float(modulus.size * n)
    angle = math.acosh(RATIO_C)
    half = math.cosh(CDEG * angle)
    full = math.cosh(2 * CDEG * angle)
    scale = jnp.array([1.0 / cells, 2.0 * half * half / full / 4.0 / (cells / 8.0)], jnp.float32)
    return fine, coarse, sums.sum(axis=(0, 1))[:2] * scale


def solution(mesh):
    return jax.shard_map(
        body,
        mesh=mesh,
        in_specs=(P(None, "slab", None, "sample"), P("slab", None, "sample")),
        out_specs=(P(None, "slab", None, "sample"), P(None, "slab", None, "sample"), P("sample")),
        check_vma=False,
    )
```

time: 432 us -> 83 us (0.19)
  starting transfers between devices: 236 us -> 48.5 us
  other arithmetic: 60.1 us -> 1.12 us
  local copies, waits for them, and re-layouts: 61.6 us -> 4.99 us
  waiting for transfers between devices: 66.1 us -> 15.1 us
  Pallas kernels: 0 us -> 11.9 us
    ppermute x46 -> x12, starting transfers between devices: 224 us -> 39.9 us  [swap(): return lax.ppermute(x, axis, pairs)]
    reshape x6 -> x0, local copies, waits for them, and re-layouts: 49.9 us -> none  [the longest x3 42.4 us: restrict_vector(): values.reshape(shape[0], shape[1] // 2, 2, shape[2] // 2, 2, shape[3] //...]
    ppermute x46 -> x12, waiting for transfers between devices: 59.6 us -> 15.1 us  [swap(): return lax.ppermute(x, axis, pairs)]
    reduce_sum x7 -> x1, other arithmetic: 23.5 us -> 0.03 us  [body(): return (fine, coarse, sums.sum(axis=(0, 1))[:2] * scale)]
    pallas_call x0 -> x3, Pallas kernels: none -> 11.9 us  [call(): pl.pallas_call(kernel, out_shape=[jax.ShapeDtypeStruct(s, jnp.float32) fo...]
    mul x52 -> x1, other arithmetic: 10.2 us -> 0.51 us  [body(): return (fine, coarse, sums.sum(axis=(0, 1))[:2] * scale)]
    add x15 -> x0, other arithmetic: 6.87 us -> none  [the longest x13 6.68 us: chebyshev(): rho_next * rho_now * update]
    concatenate x47 -> x2, other arithmetic: 6.59 us -> 0.02 us  [edge(): jnp.concatenate([f, lax.dynamic_slice_in_dim(modulus, 1 - side, 3, 0)], 0)]
  transfers between devices with their start and end apart: 47 -> 13, of which waited for: 27 -> 4; matrix products, arithmetic and copies ran while one was open for 8% -> 1% of each run, Pallas kernels for 0% -> 0%
where the time goes in v1:
time: 83 us; the launch traced here: 82.6 us
  starting transfers between devices  48.5 us (58%)
  waiting for transfers between devices  15.1 us (18%)
  Pallas kernels  11.9 us (14%)
  local copies, waits for them, and re-layouts  4.99 us (6%)
  other arithmetic  1.12 us (1%)
  between operations  0.99 us (1%)
    ppermute x12, starting transfers between devices, swap(): return lax.ppermute(x, axis, pairs)  39.9 us
    ppermute x12, waiting for transfers between devices, swap(): return lax.ppermute(x, axis, pairs)  15.1 us
    pallas_call x3, Pallas kernels, call(): pl.pallas_call(kernel, out_shape=[jax.ShapeDtypeStruct(s, jnp.float32) fo...  11.9 us
    all_to_all x1, starting transfers between devices, body(): lax.all_to_all(jnp.broadcast_to(part[None], (n, 1, 128)), 'slab', 0, 0, t...  8.63 us
    unnamed x32, local copies, waits for them, and re-layouts  3.45 us
  transfers between devices with their start and end apart: 13, of which 4 were waited for; matrix products, arithmetic and copies ran while one was open for 1% of the time, Pallas kernels for 0%

profile of v1, /device:TPU:32, one launch (start us, length us, event | category | flops | bytes accessed | tf_op | source)
XLA Modules:
  0.0 82.6 jit_solution(8617548091970728102)
XLA Ops:
  0.6 0.0 copy-start
  0.7 0.9 %constant_dynamic-slice_fusion = (f32[3,32,128]{2,1,0:T(8,128)S(1)}, f32[3,32,128]{2,1,0:T(8,128)S(1)}) fusion(f32[4,32,128]{2,1,0:T(8,128)} %e_ref.1, s32[]{:T(128)S(6)} %select_n.44, s32[]{:T(128)S(6)} %select_n.42), kind=kLoop, calls=%fused_computation.2 | loop fusion | bytes 196616 | tf_op jit(solution)/shard_map/dynamic_slice | solution.py:383
  1.6 0.0 copy-done
  1.6 1.6 %collective-permute-start = (f32[9,32,128]{2,1,0:T(8,128)S(1)}, f32[9,32,128]{2,1,0:T(8,128)S(1)}, u32[]{:S(2)}, u32[]{:S(2)}) collective-permute-start(f32[9,32,128]{2,1,0:T(8,128)S(1)} %pad_maximum_fusion), channel_id=1, source_target_pairs={{0,1},{1,0},{2,3},{3,2},{4,5},{5,4},{6,7},{7,6},{8,9},{9,8},{10,11... | collective-permute-start | bytes 442376 | tf_op jit(solution)/shard_map/ppermute | solution.py:373
  3.2 6.0 %collective-permute-start.1 = (f32[9,32,128]{2,1,0:T(8,128)S(1)}, f32[9,32,128]{2,1,0:T(8,128)S(1)}, u32[]{:S(2)}, u32[]{:S(2)}) collective-permute-start(f32[9,32,128]{2,1,0:T(8,128)S(1)} %pad_maximum_fusion.1), channel_id=1, source_target_pairs={{1,2},{2,1},{3,4},{4,3},{5,6},{6,5},{7,8},{8,7},{9,10},{10,9},{11,... | collective-permute-start | bytes 442376 | tf_op jit(solution)/shard_map/ppermute | solution.py:373
  9.3 0.6 pad_add_fusion.par
  9.8 0.0 collective-permute-done.a_ref
  9.8 4.8 %collective-permute-done.1.b_ref = f32[9,32,128]{2,1,0:T(8,128)S(1)} collective-permute-done((f32[9,32,128]{2,1,0:T(8,128)S(1)}, f32[9,32,128]{2,1,0:T(8,128)S(1)}, u32[]{:S(2)}, u32[]{:S(2)}) %collective-permute-start.1) | collective-permute-done | bytes 147488 | tf_op jit(solution)/shard_map/ppermute | solution.py:373
  14.6 0.0 copy-done.3
  14.6 0.7 copy-done.4
  15.3 2.7 %shard_map.58 = (f32[3,4,32,128]{3,2,1,0:T(8,128)}, f32[22,32,128]{2,1,0:T(8,128)}, f32[9,16,128]{2,1,0:T(8,128)}) custom-call(s32[3]{0:T(128)} %pad_add_fusion.par, f32[3,4,32,128]{3,2,1,0:T(8,128)} %f_ref.3, f32[4,32,128]{2,1,0:T(8,128)} %e_ref.1, f32[9,32,128]{2,1,0:T(8,128)} %copy-done.3, f32[9,32,128]{2,1,0:T(8,128)} %copy-done.4), custom_call_target="tpu_custom_call" | custom-call | flops 4194304 | bytes 1048576 | tf_op jit(solution)/shard_map/pallas_call | solution.py:356
  18.0 6.0 %collective-permute-start.3 = (f32[22,32,128]{2,1,0:T(8,128)}, f32[22,32,128]{2,1,0:T(8,128)S(1)}, u32[]{:S(2)}, u32[]{:S(2)}) collective-permute-start(f32[22,32,128]{2,1,0:T(8,128)} %get-tuple-element.19.mine), channel_id=1, source_target_pairs={{1,2},{2,1},{3,4},{4,3},{5,6},{6,5},{7,8},{8,7},{9,10},{10,9},{11,... | collective-permute-start | bytes 1081352 | tf_op jit(solution)/shard_map/ppermute | solution.py:373
  24.0 0.1 collective-permute-start.2
  24.1 1.9 %collective-permute-start.7 = (f32[9,16,128]{2,1,0:T(8,128)}, f32[9,16,128]{2,1,0:T(8,128)S(1)}, u32[]{:S(2)}, u32[]{:S(2)}) collective-permute-start(f32[9,16,128]{2,1,0:T(8,128)} %get-tuple-element.20.own), channel_id=1, source_target_pairs={{3,6},{6,3},{4,7},{7,4},{5,8},{8,5},{9,12},{12,9},{10,13},{13,10},... | collective-permute-start | bytes 221192 | tf_op jit(solution)/shard_map/ppermute | solution.py:373
  26.0 3.2 %collective-permute-start.6 = (f32[9,16,128]{2,1,0:T(8,128)}, f32[9,16,128]{2,1,0:T(8,128)S(1)}, u32[]{:S(2)}, u32[]{:S(2)}) collective-permute-start(f32[9,16,128]{2,1,0:T(8,128)} %get-tuple-element.20.own), channel_id=1, source_target_pairs={{0,3},{3,0},{1,4},{4,1},{2,5},{5,2},{6,9},{9,6},{7,10},{10,7},{8,1... | collective-permute-start | bytes 221192 | tf_op jit(solution)/shard_map/ppermute | solution.py:373
  29.2 7.7 %collective-permute-start.5 = (f32[9,16,128]{2,1,0:T(8,128)}, f32[9,16,128]{2,1,0:T(8,128)S(1)}, u32[]{:S(2)}, u32[]{:S(2)}) collective-permute-start(f32[9,16,128]{2,1,0:T(8,128)} %get-tuple-element.20.own), channel_id=1, source_target_pairs={{2,4},{4,2},{3,5},{5,3},{6,8},{8,6},{7,9},{9,7},{10,12},{12,10},{1... | collective-permute-start | bytes 221192 | tf_op jit(solution)/shard_map/ppermute | solution.py:373
  36.9 0.0 collective-permute-done.7.b3
  36.9 0.0 copy-start.7
  36.9 0.1 collective-permute-start.4
  37.0 0.0 collective-permute-done.6.a3
  37.1 3.2 %collective-permute-done.5.b2 = f32[9,16,128]{2,1,0:T(8,128)S(1)} collective-permute-done((f32[9,16,128]{2,1,0:T(8,128)}, f32[9,16,128]{2,1,0:T(8,128)S(1)}, u32[]{:S(2)}, u32[]{:S(2)}) %collective-permute-start.5) | collective-permute-done | bytes 73760 | tf_op jit(solution)/shard_map/ppermute | solution.py:373
  40.2 2.9 %collective-permute-done.4.a2 = f32[9,16,128]{2,1,0:T(8,128)S(1)} collective-permute-done((f32[9,16,128]{2,1,0:T(8,128)}, f32[9,16,128]{2,1,0:T(8,128)S(1)}, u32[]{:S(2)}, u32[]{:S(2)}) %collective-permute-start.4) | collective-permute-done | bytes 73760 | tf_op jit(solution)/shard_map/ppermute | solution.py:373
  43.1 0.0 collective-permute-done.3.b1
  43.1 0.0 collective-permute-done.2.a1
  43.1 0.6 copy-done.10
  43.7 0.1 copy-done.1
  43.9 0.1 copy-done.2
  44.0 5.9 %shard_map.59 = (f32[3,4,32,128]{3,2,1,0:T(8,128)}, f32[3,4,32,128]{3,2,1,0:T(8,128)}, f32[6,32,128]{2,1,0:T(8,128)}, f32[6,32,128]{2,1,0:T(8,128)}, f32[6,16,12...) custom-call(s32[3]{0:T(128)} %pad_add_fusion.par, ...), custom_call_target="tpu_custom_call" | custom-call | flops 4194304 | bytes 1048576 | tf_op jit(solution)/shard_map/pallas_call | solution.py:356
  49.9 0.0 copy-start.14
  49.9 0.6 copy-done.14
  50.5 0.6 broadcast_in_dim.9
  51.2 8.6 %all-to-all-start = ((f32[64,1,128]{2,1,0:T(1,128)}), f32[64,1,128]{2,1,0:T(1,128)S(1)}, u32[]{:S(2)}, u32[]{:S(2)}) async-start(f32[64,1,128]{2,1,0:T(1,128)} %broadcast_in_dim.9), calls=%async_computation | async-start | bytes 65536 | tf_op jit(solution)/shard_map/all_to_all | solution.py:407
  59.8 0.0 copy-done.11
  59.8 7.0 %collective-permute-start.11 = (f32[6,16,128]{2,1,0:T(8,128)S(1)}, f32[6,16,128]{2,1,0:T(8,128)S(1)}, u32[]{:S(2)}, u32[]{:S(2)}) collective-permute-start(f32[6,16,128]{2,1,0:T(8,128)S(1)} %copy-done.11), channel_id=1, source_target_pairs={{2,4},{4,2},{3,5},{5,3},{6,8},{8,6},{7,9},{9,7},{10,12},{12,10},{1... | collective-permute-start | bytes 147464 | tf_op jit(solution)/shard_map/ppermute | solution.py:373
  66.8 0.1 collective-permute-start.10
  66.9 0.8 collective-permute-start.8
  67.7 5.4 %collective-permute-start.9 = (f32[6,32,128]{2,1,0:T(8,128)}, f32[6,32,128]{2,1,0:T(8,128)S(1)}, u32[]{:S(2)}, u32[]{:S(2)}) collective-permute-start(f32[6,32,128]{2,1,0:T(8,128)} %get-tuple-element.29), channel_id=1, source_target_pairs={{1,2},{2,1},{3,4},{4,3},{5,6},{6,5},{7,8},{8,7},{9,10},{10,9},{11,... | collective-permute-start | bytes 294920 | tf_op jit(solution)/shard_map/ppermute | solution.py:373
  73.2 0.0 all-to-all-done
  73.2 0.0 copy-start.15
  73.2 0.6 copy-done.15
  73.8 0.5 slice_multiply_fusion
  74.3 0.0 collective-permute-done.11.b2
  74.3 0.0 collective-permute-done.10.a2
  74.4 0.0 collective-permute-done.8.a1
  74.4 4.2 %collective-permute-done.9.b1 = f32[6,32,128]{2,1,0:T(8,128)S(1)} collective-permute-done((f32[6,32,128]{2,1,0:T(8,128)}, f32[6,32,128]{2,1,0:T(8,128)S(1)}, u32[]{:S(2)}, u32[]{:S(2)}) %collective-permute-start.9) | collective-permute-done | bytes 98336 | tf_op jit(solution)/shard_map/ppermute | solution.py:373
  78.6 0.0 copy-done.13
  78.6 0.6 copy-done.6
  79.3 3.3 %shard_map.60 = (f32[3,4,32,128]{3,2,1,0:T(8,128)}, f32[3,2,16,64]{3,2,1,0:T(8,128)}) custom-call(s32[3]{0:T(128)} %pad_add_fusion.par, f32[3,4,32,128]{3,2,1,0:T(8,128)} %get-tuple-element.21.x_ref, f32[3,4,32,128]{3,2,1,0:T(8,128)} %get-tuple-element.22.r_ref, f32[6,16,128]{2,1,0:T(8,128)} %get-tuple-element.23.own, ...), custom_call_target="tpu_custom_call" | custom-call | flops 4194304 | bytes 1048576 | tf_op jit(solution)/shard_map/pallas_call | solution.py:356
  (21 shorter events, 0.1 us)
Async XLA Ops:
  0.6 0.9 %copy-start = (f32[3,4,32,128]{3,2,1,0:T(8,128)S(1)}, f32[3,4,32,128]{3,2,1,0:T(8,128)}, u32[]{:S(2)}) copy-start(f32[3,4,32,128]{3,2,1,0:T(8,128)} %f_ref.3) | copy-start | bytes 589828
  1.6 8.2 %collective-permute-start = (f32[9,32,128]{2,1,0:T(8,128)S(1)}, f32[9,32,128]{2,1,0:T(8,128)S(1)}, u32[]{:S(2)}, u32[]{:S(2)}) collective-permute-start(f32[9,32,128]{2,1,0:T(8,128)S(1)} %pad_maximum_fusion), channel_id=1, source_target_pairs={{0,1},{1,0},{2,3},{3,2},{4,5},{5,4},{6,7},{7,6},{8,9},{9,8},{10,11... | collective-permute-start | bytes 442376 | tf_op jit(solution)/shard_map/ppermute | solution.py:373
  3.2 11.4 %collective-permute-start.1 = (f32[9,32,128]{2,1,0:T(8,128)S(1)}, f32[9,32,128]{2,1,0:T(8,128)S(1)}, u32[]{:S(2)}, u32[]{:S(2)}) collective-permute-start(f32[9,32,128]{2,1,0:T(8,128)S(1)} %pad_maximum_fusion.1), channel_id=1, source_target_pairs={{1,2},{2,1},{3,4},{4,3},{5,6},{6,5},{7,8},{8,7},{9,10},{10,9},{11,... | collective-permute-start | bytes 442376 | tf_op jit(solution)/shard_map/ppermute | solution.py:373
  9.8 4.8 %copy-start.3 = (f32[9,32,128]{2,1,0:T(8,128)}, f32[9,32,128]{2,1,0:T(8,128)S(1)}, u32[]{:S(2)}) copy-start(f32[9,32,128]{2,1,0:T(8,128)S(1)} %collective-permute-done.a_ref) | copy-start | bytes 442372
  14.6 0.7 copy-start.4
  18.0 25.1 %collective-permute-start.3 = (f32[22,32,128]{2,1,0:T(8,128)}, f32[22,32,128]{2,1,0:T(8,128)S(1)}, u32[]{:S(2)}, u32[]{:S(2)}) collective-permute-start(f32[22,32,128]{2,1,0:T(8,128)} %get-tuple-element.19.mine), channel_id=1, source_target_pairs={{1,2},{2,1},{3,4},{4,3},{5,6},{6,5},{7,8},{8,7},{9,10},{10,9},{11,... | collective-permute-start | bytes 1081352 | tf_op jit(solution)/shard_map/ppermute | solution.py:373
  24.0 19.1 %collective-permute-start.2 = (f32[22,32,128]{2,1,0:T(8,128)}, f32[22,32,128]{2,1,0:T(8,128)S(1)}, u32[]{:S(2)}, u32[]{:S(2)}) collective-permute-start(f32[22,32,128]{2,1,0:T(8,128)} %get-tuple-element.19.mine), channel_id=1, source_target_pairs={{0,1},{1,0},{2,3},{3,2},{4,5},{5,4},{6,7},{7,6},{8,9},{9,8},{10,11... | collective-permute-start | bytes 1081352 | tf_op jit(solution)/shard_map/ppermute | solution.py:373
  24.1 12.8 %collective-permute-start.7 = (f32[9,16,128]{2,1,0:T(8,128)}, f32[9,16,128]{2,1,0:T(8,128)S(1)}, u32[]{:S(2)}, u32[]{:S(2)}) collective-permute-start(f32[9,16,128]{2,1,0:T(8,128)} %get-tuple-element.20.own), channel_id=1, source_target_pairs={{3,6},{6,3},{4,7},{7,4},{5,8},{8,5},{9,12},{12,9},{10,13},{13,10},... | collective-permute-start | bytes 221192 | tf_op jit(solution)/shard_map/ppermute | solution.py:373
  26.0 11.0 %collective-permute-start.6 = (f32[9,16,128]{2,1,0:T(8,128)}, f32[9,16,128]{2,1,0:T(8,128)S(1)}, u32[]{:S(2)}, u32[]{:S(2)}) collective-permute-start(f32[9,16,128]{2,1,0:T(8,128)} %get-tuple-element.20.own), channel_id=1, source_target_pairs={{0,3},{3,0},{1,4},{4,1},{2,5},{5,2},{6,9},{9,6},{7,10},{10,7},{8,1... | collective-permute-start | bytes 221192 | tf_op jit(solution)/shard_map/ppermute | solution.py:373
  29.2 11.0 %collective-permute-start.5 = (f32[9,16,128]{2,1,0:T(8,128)}, f32[9,16,128]{2,1,0:T(8,128)S(1)}, u32[]{:S(2)}, u32[]{:S(2)}) collective-permute-start(f32[9,16,128]{2,1,0:T(8,128)} %get-tuple-element.20.own), channel_id=1, source_target_pairs={{2,4},{4,2},{3,5},{5,3},{6,8},{8,6},{7,9},{9,7},{10,12},{12,10},{1... | collective-permute-start | bytes 221192 | tf_op jit(solution)/shard_map/ppermute | solution.py:373
  36.9 6.2 %copy-start.7 = (f32[9,16,128]{2,1,0:T(8,128)}, f32[9,16,128]{2,1,0:T(8,128)S(1)}, u32[]{:S(2)}) copy-start(f32[9,16,128]{2,1,0:T(8,128)S(1)} %collective-permute-done.7.b3) | copy-start | bytes 221188
  36.9 6.1 %collective-permute-start.4 = (f32[9,16,128]{2,1,0:T(8,128)}, f32[9,16,128]{2,1,0:T(8,128)S(1)}, u32[]{:S(2)}, u32[]{:S(2)}) collective-permute-start(f32[9,16,128]{2,1,0:T(8,128)} %get-tuple-element.20.own), channel_id=1, source_target_pairs={{0,2},{2,0},{1,3},{3,1},{4,6},{6,4},{5,7},{7,5},{8,10},{10,8},{9,1... | collective-permute-start | bytes 221192 | tf_op jit(solution)/shard_map/ppermute | solution.py:373
  37.0 6.1 %copy-start.8 = (f32[9,16,128]{2,1,0:T(8,128)}, f32[9,16,128]{2,1,0:T(8,128)S(1)}, u32[]{:S(2)}) copy-start(f32[9,16,128]{2,1,0:T(8,128)S(1)} %collective-permute-done.6.a3) | copy-start | bytes 221188
  40.2 2.9 %copy-start.9 = (f32[9,16,128]{2,1,0:T(8,128)}, f32[9,16,128]{2,1,0:T(8,128)S(1)}, u32[]{:S(2)}) copy-start(f32[9,16,128]{2,1,0:T(8,128)S(1)} %collective-permute-done.5.b2) | copy-start | bytes 221188
  43.1 0.6 copy-start.10
  43.1 0.8 copy-start.1
  43.1 0.9 %copy-start.2 = (f32[22,32,128]{2,1,0:T(8,128)}, f32[22,32,128]{2,1,0:T(8,128)S(1)}, u32[]{:S(2)}) copy-start(f32[22,32,128]{2,1,0:T(8,128)S(1)} %collective-permute-done.2.a1) | copy-start | bytes 1081348
  49.9 0.7 copy-start.14
  50.5 9.3 %copy-start.11 = (f32[6,16,128]{2,1,0:T(8,128)S(1)}, f32[6,16,128]{2,1,0:T(8,128)}, u32[]{:S(2)}) copy-start(f32[6,16,128]{2,1,0:T(8,128)} %get-tuple-element.23.own) | copy-start | bytes 147460
  51.2 22.0 %all-to-all-start = ((f32[64,1,128]{2,1,0:T(1,128)}), f32[64,1,128]{2,1,0:T(1,128)S(1)}, u32[]{:S(2)}, u32[]{:S(2)}) async-start(f32[64,1,128]{2,1,0:T(1,128)} %broadcast_in_dim.9), calls=%async_computation | async-start | bytes 65536 | tf_op jit(solution)/shard_map/all_to_all | solution.py:407
  59.8 14.5 %collective-permute-start.11 = (f32[6,16,128]{2,1,0:T(8,128)S(1)}, f32[6,16,128]{2,1,0:T(8,128)S(1)}, u32[]{:S(2)}, u32[]{:S(2)}) collective-permute-start(f32[6,16,128]{2,1,0:T(8,128)S(1)} %copy-done.11), channel_id=1, source_target_pairs={{2,4},{4,2},{3,5},{5,3},{6,8},{8,6},{7,9},{9,7},{10,12},{12,10},{1... | collective-permute-start | bytes 147464 | tf_op jit(solution)/shard_map/ppermute | solution.py:373
  66.8 7.6 %collective-permute-start.10 = (f32[6,16,128]{2,1,0:T(8,128)S(1)}, f32[6,16,128]{2,1,0:T(8,128)S(1)}, u32[]{:S(2)}, u32[]{:S(2)}) collective-permute-start(f32[6,16,128]{2,1,0:T(8,128)S(1)} %copy-done.11), channel_id=1, source_target_pairs={{0,2},{2,0},{1,3},{3,1},{4,6},{6,4},{5,7},{7,5},{8,10},{10,8},{9,1... | collective-permute-start | bytes 147464 | tf_op jit(solution)/shard_map/ppermute | solution.py:373
  66.9 7.5 %collective-permute-start.8 = (f32[6,32,128]{2,1,0:T(8,128)}, f32[6,32,128]{2,1,0:T(8,128)S(1)}, u32[]{:S(2)}, u32[]{:S(2)}) collective-permute-start(f32[6,32,128]{2,1,0:T(8,128)} %get-tuple-element.28), channel_id=1, source_target_pairs={{0,1},{1,0},{2,3},{3,2},{4,5},{5,4},{6,7},{7,6},{8,9},{9,8},{10,11... | collective-permute-start | bytes 294920 | tf_op jit(solution)/shard_map/ppermute | solution.py:373
  67.7 10.9 %collective-permute-start.9 = (f32[6,32,128]{2,1,0:T(8,128)}, f32[6,32,128]{2,1,0:T(8,128)S(1)}, u32[]{:S(2)}, u32[]{:S(2)}) collective-permute-start(f32[6,32,128]{2,1,0:T(8,128)} %get-tuple-element.29), channel_id=1, source_target_pairs={{1,2},{2,1},{3,4},{4,3},{5,6},{6,5},{7,8},{8,7},{9,10},{10,9},{11,... | collective-permute-start | bytes 294920 | tf_op jit(solution)/shard_map/ppermute | solution.py:373
  73.2 0.7 copy-start.15
  74.3 4.3 %copy-start.12 = (f32[6,16,128]{2,1,0:T(8,128)}, f32[6,16,128]{2,1,0:T(8,128)S(1)}, u32[]{:S(2)}) copy-start(f32[6,16,128]{2,1,0:T(8,128)S(1)} %collective-permute-done.11.b2) | copy-start | bytes 147460
  74.4 4.3 %copy-start.13 = (f32[6,16,128]{2,1,0:T(8,128)}, f32[6,16,128]{2,1,0:T(8,128)S(1)}, u32[]{:S(2)}) copy-start(f32[6,16,128]{2,1,0:T(8,128)S(1)} %collective-permute-done.10.a2) | copy-start | bytes 147460
  74.4 4.3 %copy-start.5 = (f32[6,32,128]{2,1,0:T(8,128)}, f32[6,32,128]{2,1,0:T(8,128)S(1)}, u32[]{:S(2)}) copy-start(f32[6,32,128]{2,1,0:T(8,128)S(1)} %collective-permute-done.8.a1) | copy-start | bytes 294916
  78.6 0.6 copy-start.6

commit v2 on v1

--- a/solution.py
+++ b/solution.py
@@ -360,6 +360,7 @@
         + [pl.BlockSpec(memory_space=pltpu.VMEM)] * len(args),
         out_specs=[pl.BlockSpec(memory_space=pltpu.VMEM)] * len(outs),
         scratch_shapes=[pltpu.VMEM(s, jnp.float32) for s in scratch],
+        compiler_params=pltpu.CompilerParams(vmem_limit_bytes=16 << 20),
         cost_estimate=pl.CostEstimate(flops=flops, bytes_accessed=1 << 20, transcendentals=0),
     )(par, *args)
 

time: 83 us -> 76 us (0.916)
  Pallas kernels: 11.9 us -> 8.1 us
  local copies, waits for them, and re-layouts: 4.99 us -> 2.18 us
    pallas_call x3, Pallas kernels: 11.9 us -> 8.1 us  [call(): pl.pallas_call(kernel, out_shape=[jax.ShapeDtypeStruct(s, jnp.float32) fo...]
    unnamed x32 -> x6, local copies, waits for them, and re-layouts: 3.45 us -> 0.64 us
where the time goes in v2:
time: 76 us; the launch traced here: 75.7 us
  starting transfers between devices  48.6 us (64%)
  waiting for transfers between devices  15.2 us (20%)
  Pallas kernels  8.1 us (11%)
  local copies, waits for them, and re-layouts  2.18 us (3%)
  between operations  0.91 us (1%)
    ppermute x12, starting transfers between devices, swap(): return lax.ppermute(x, axis, pairs)  40 us
    ppermute x12, waiting for transfers between devices, swap(): return lax.ppermute(x, axis, pairs)  15.2 us
    all_to_all x1, starting transfers between devices, body(): lax.all_to_all(jnp.broadcast_to(part[None], (n, 1, 128)), 'slab', 0, 0, t...  8.63 us
    pallas_call x3, Pallas kernels, call(): pl.pallas_call(kernel, out_shape=[jax.ShapeDtypeStruct(s, jnp.float32) fo...  8.1 us
  transfers between devices with their start and end apart: 13, of which 4 were waited for; matrix products, arithmetic and copies ran while one was open for 1% of the time, Pallas kernels for 0%

profile of v2, /device:TPU:32, one launch (start us, length us, event | category | flops | bytes accessed | tf_op | source)
XLA Modules:
  0.0 75.7 jit_solution(10847843618815455356)
XLA Ops:
  0.6 0.0 copy-start
  0.7 0.9 %constant_dynamic-slice_fusion = (f32[3,32,128]{2,1,0:T(8,128)S(1)}, f32[3,32,128]{2,1,0:T(8,128)S(1)}) fusion(f32[4,32,128]{2,1,0:T(8,128)} %e_ref.1, s32[]{:T(128)S(6)} %select_n.44, s32[]{:T(128)S(6)} %select_n.42), kind=kLoop, calls=%fused_computation.2 | loop fusion | bytes 196616 | tf_op jit(solution)/shard_map/dynamic_slice | solution.py:384
  1.6 0.0 copy-done
  1.6 1.6 %collective-permute-start = (f32[9,32,128]{2,1,0:T(8,128)S(1)}, f32[9,32,128]{2,1,0:T(8,128)S(1)}, u32[]{:S(2)}, u32[]{:S(2)}) collective-permute-start(f32[9,32,128]{2,1,0:T(8,128)S(1)} %pad_maximum_fusion), channel_id=1, source_target_pairs={{0,1},{1,0},{2,3},{3,2},{4,5},{5,4},{6,7},{7,6},{8,9},{9,8},{10,11... | collective-permute-start | bytes 442376 | tf_op jit(solution)/shard_map/ppermute | solution.py:374
  3.2 0.0 copy-start.1
  3.2 6.1 %collective-permute-start.1 = (f32[9,32,128]{2,1,0:T(8,128)S(1)}, f32[9,32,128]{2,1,0:T(8,128)S(1)}, u32[]{:S(2)}, u32[]{:S(2)}) collective-permute-start(f32[9,32,128]{2,1,0:T(8,128)S(1)} %pad_maximum_fusion.1), channel_id=1, source_target_pairs={{1,2},{2,1},{3,4},{4,3},{5,6},{6,5},{7,8},{8,7},{9,10},{10,9},{11,... | collective-permute-start | bytes 442376 | tf_op jit(solution)/shard_map/ppermute | solution.py:374
  9.4 0.1 pad_add_fusion.par
  9.5 0.0 collective-permute-done.a_ref
  9.5 5.3 %collective-permute-done.1.b_ref = f32[9,32,128]{2,1,0:T(8,128)S(1)} collective-permute-done((f32[9,32,128]{2,1,0:T(8,128)S(1)}, f32[9,32,128]{2,1,0:T(8,128)S(1)}, u32[]{:S(2)}, u32[]{:S(2)}) %collective-permute-start.1) | collective-permute-done | bytes 147488 | tf_op jit(solution)/shard_map/ppermute | solution.py:374
  14.8 0.0 copy-done.1
  14.8 1.4 %shard_map.58 = (f32[3,4,32,128]{3,2,1,0:T(8,128)S(1)}, f32[22,32,128]{2,1,0:T(8,128)S(1)}, f32[9,16,128]{2,1,0:T(8,128)S(1)}) custom-call(s32[3]{0:T(128)S(1)} %pad_add_fusion.par, f32[3,4,32,128]{3,2,1,0:T(8,128)S(1)} %copy-done, f32[4,32,128]{2,1,0:T(8,128)S(1)} %copy-done.1, f32[9,32,128]{2,1,0:T(8,128)S(1)} %collective-permute-done.a_ref, ...), custom_call_target="tpu_custom_call" | custom-call | flops 4194304 | bytes 1048576 | tf_op jit(solution)/shard_map/pallas_call | solution.py:356
  16.2 6.0 %collective-permute-start.3 = (f32[22,32,128]{2,1,0:T(8,128)S(1)}, f32[22,32,128]{2,1,0:T(8,128)S(1)}, u32[]{:S(2)}, u32[]{:S(2)}) collective-permute-start(f32[22,32,128]{2,1,0:T(8,128)S(1)} %get-tuple-element.19.mine), channel_id=1, source_target_pairs={{1,2},{2,1},{3,4},{4,3},{5,6},{6,5},{7,8},{8,7},{9,10},{10,9},{11,... | collective-permute-start | bytes 1081352 | tf_op jit(solution)/shard_map/ppermute | solution.py:374
  22.2 0.1 collective-permute-start.2
  22.3 1.9 %collective-permute-start.7 = (f32[9,16,128]{2,1,0:T(8,128)S(1)}, f32[9,16,128]{2,1,0:T(8,128)S(1)}, u32[]{:S(2)}, u32[]{:S(2)}) collective-permute-start(f32[9,16,128]{2,1,0:T(8,128)S(1)} %get-tuple-element.20.own), channel_id=1, source_target_pairs={{3,6},{6,3},{4,7},{7,4},{5,8},{8,5},{9,12},{12,9},{10,13},{13,10},... | collective-permute-start | bytes 221192 | tf_op jit(solution)/shard_map/ppermute | solution.py:374
  24.2 3.2 %collective-permute-start.6 = (f32[9,16,128]{2,1,0:T(8,128)S(1)}, f32[9,16,128]{2,1,0:T(8,128)S(1)}, u32[]{:S(2)}, u32[]{:S(2)}) collective-permute-start(f32[9,16,128]{2,1,0:T(8,128)S(1)} %get-tuple-element.20.own), channel_id=1, source_target_pairs={{0,3},{3,0},{1,4},{4,1},{2,5},{5,2},{6,9},{9,6},{7,10},{10,7},{8,1... | collective-permute-start | bytes 221192 | tf_op jit(solution)/shard_map/ppermute | solution.py:374
  27.4 7.7 %collective-permute-start.5 = (f32[9,16,128]{2,1,0:T(8,128)S(1)}, f32[9,16,128]{2,1,0:T(8,128)S(1)}, u32[]{:S(2)}, u32[]{:S(2)}) collective-permute-start(f32[9,16,128]{2,1,0:T(8,128)S(1)} %get-tuple-element.20.own), channel_id=1, source_target_pairs={{2,4},{4,2},{3,5},{5,3},{6,8},{8,6},{7,9},{9,7},{10,12},{12,10},{1... | collective-permute-start | bytes 221192 | tf_op jit(solution)/shard_map/ppermute | solution.py:374
  35.1 0.0 collective-permute-done.7.b3
  35.1 0.1 collective-permute-start.4
  35.2 0.0 collective-permute-done.6.a3
  35.2 3.0 %collective-permute-done.5.b2 = f32[9,16,128]{2,1,0:T(8,128)S(1)} collective-permute-done((f32[9,16,128]{2,1,0:T(8,128)S(1)}, f32[9,16,128]{2,1,0:T(8,128)S(1)}, u32[]{:S(2)}, u32[]{:S(2)}) %collective-permute-start.5) | collective-permute-done | bytes 73760 | tf_op jit(solution)/shard_map/ppermute | solution.py:374
  38.2 2.9 %collective-permute-done.4.a2 = f32[9,16,128]{2,1,0:T(8,128)S(1)} collective-permute-done((f32[9,16,128]{2,1,0:T(8,128)S(1)}, f32[9,16,128]{2,1,0:T(8,128)S(1)}, u32[]{:S(2)}, u32[]{:S(2)}) %collective-permute-start.4) | collective-permute-done | bytes 73760 | tf_op jit(solution)/shard_map/ppermute | solution.py:374
  41.1 0.0 collective-permute-done.3.b1
  41.1 0.0 collective-permute-done.2.a1
  41.1 4.2 %shard_map.59 = (f32[3,4,32,128]{3,2,1,0:T(8,128)S(1)}, f32[3,4,32,128]{3,2,1,0:T(8,128)S(1)}, f32[6,32,128]{2,1,0:T(8,128)S(1)}, f32[6,32,128]{2,1,0:T(8,128)S(...) custom-call(s32[3]{0:T(128)S(1)} %pad_add_fusion.par, ...), custom_call_target="tpu_custom_call" | custom-call | flops 4194304 | bytes 1048576 | tf_op jit(solution)/shard_map/pallas_call | solution.py:356
  45.2 0.6 broadcast_in_dim.9
  45.9 8.6 %all-to-all-start = ((f32[64,1,128]{2,1,0:T(1,128)}), f32[64,1,128]{2,1,0:T(1,128)S(1)}, u32[]{:S(2)}, u32[]{:S(2)}) async-start(f32[64,1,128]{2,1,0:T(1,128)} %broadcast_in_dim.9), calls=%async_computation | async-start | bytes 65536 | tf_op jit(solution)/shard_map/all_to_all | solution.py:408
  54.5 7.0 %collective-permute-start.11 = (f32[6,16,128]{2,1,0:T(8,128)S(1)}, f32[6,16,128]{2,1,0:T(8,128)S(1)}, u32[]{:S(2)}, u32[]{:S(2)}) collective-permute-start(f32[6,16,128]{2,1,0:T(8,128)S(1)} %get-tuple-element.23.own), channel_id=1, source_target_pairs={{2,4},{4,2},{3,5},{5,3},{6,8},{8,6},{7,9},{9,7},{10,12},{12,10},{1... | collective-permute-start | bytes 147464 | tf_op jit(solution)/shard_map/ppermute | solution.py:374
  61.5 0.1 collective-permute-start.10
  61.6 0.8 %collective-permute-start.8 = (f32[6,32,128]{2,1,0:T(8,128)S(1)}, f32[6,32,128]{2,1,0:T(8,128)S(1)}, u32[]{:S(2)}, u32[]{:S(2)}) collective-permute-start(f32[6,32,128]{2,1,0:T(8,128)S(1)} %get-tuple-element.28), channel_id=1, source_target_pairs={{0,1},{1,0},{2,3},{3,2},{4,5},{5,4},{6,7},{7,6},{8,9},{9,8},{10,11... | collective-permute-start | bytes 294920 | tf_op jit(solution)/shard_map/ppermute | solution.py:374
  62.4 5.4 %collective-permute-start.9 = (f32[6,32,128]{2,1,0:T(8,128)S(1)}, f32[6,32,128]{2,1,0:T(8,128)S(1)}, u32[]{:S(2)}, u32[]{:S(2)}) collective-permute-start(f32[6,32,128]{2,1,0:T(8,128)S(1)} %get-tuple-element.29), channel_id=1, source_target_pairs={{1,2},{2,1},{3,4},{4,3},{5,6},{6,5},{7,8},{8,7},{9,10},{10,9},{11,... | collective-permute-start | bytes 294920 | tf_op jit(solution)/shard_map/ppermute | solution.py:374
  67.9 0.0 all-to-all-done
  67.9 0.0 copy-start.2
  67.9 0.6 copy-done.2
  68.5 0.5 slice_multiply_fusion
  69.0 0.0 collective-permute-done.11.b2
  69.0 0.0 collective-permute-done.10.a2
  69.1 0.0 collective-permute-done.8.a1
  69.1 4.1 %collective-permute-done.9.b1 = f32[6,32,128]{2,1,0:T(8,128)S(1)} collective-permute-done((f32[6,32,128]{2,1,0:T(8,128)S(1)}, f32[6,32,128]{2,1,0:T(8,128)S(1)}, u32[]{:S(2)}, u32[]{:S(2)}) %collective-permute-start.9) | collective-permute-done | bytes 98336 | tf_op jit(solution)/shard_map/ppermute | solution.py:374
  73.1 2.5 %shard_map.60 = (f32[3,4,32,128]{3,2,1,0:T(8,128)}, f32[3,2,16,64]{3,2,1,0:T(8,128)}) custom-call(s32[3]{0:T(128)S(1)} %pad_add_fusion.par, f32[3,4,32,128]{3,2,1,0:T(8,128)S(1)} %get-tuple-element.21.x_ref, f32[3,4,32,128]{3,2,1,0:T(8,128)S(1)} %get-tuple-element.22.r_ref, f32[6,16,128]{2,1,0:T(8,128)S(1)} %get-tuple-element.23.own, ...), custom_call_target="tpu_custom_call" | custom-call | flops 4194304 | bytes 1048576 | tf_op jit(solution)/shard_map/pallas_call | solution.py:356
  (4 shorter events, 0.1 us)
Async XLA Ops:
  0.6 0.9 %copy-start = (f32[3,4,32,128]{3,2,1,0:T(8,128)S(1)}, f32[3,4,32,128]{3,2,1,0:T(8,128)}, u32[]{:S(2)}) copy-start(f32[3,4,32,128]{3,2,1,0:T(8,128)} %f_ref.3) | copy-start | bytes 589828
  1.6 7.9 %collective-permute-start = (f32[9,32,128]{2,1,0:T(8,128)S(1)}, f32[9,32,128]{2,1,0:T(8,128)S(1)}, u32[]{:S(2)}, u32[]{:S(2)}) collective-permute-start(f32[9,32,128]{2,1,0:T(8,128)S(1)} %pad_maximum_fusion), channel_id=1, source_target_pairs={{0,1},{1,0},{2,3},{3,2},{4,5},{5,4},{6,7},{7,6},{8,9},{9,8},{10,11... | collective-permute-start | bytes 442376 | tf_op jit(solution)/shard_map/ppermute | solution.py:374
  3.2 11.6 %copy-start.1 = (f32[4,32,128]{2,1,0:T(8,128)S(1)}, f32[4,32,128]{2,1,0:T(8,128)}, u32[]{:S(2)}) copy-start(f32[4,32,128]{2,1,0:T(8,128)} %e_ref.1) | copy-start | bytes 196612
  3.2 11.6 %collective-permute-start.1 = (f32[9,32,128]{2,1,0:T(8,128)S(1)}, f32[9,32,128]{2,1,0:T(8,128)S(1)}, u32[]{:S(2)}, u32[]{:S(2)}) collective-permute-start(f32[9,32,128]{2,1,0:T(8,128)S(1)} %pad_maximum_fusion.1), channel_id=1, source_target_pairs={{1,2},{2,1},{3,4},{4,3},{5,6},{6,5},{7,8},{8,7},{9,10},{10,9},{11,... | collective-permute-start | bytes 442376 | tf_op jit(solution)/shard_map/ppermute | solution.py:374
  16.2 24.9 %collective-permute-start.3 = (f32[22,32,128]{2,1,0:T(8,128)S(1)}, f32[22,32,128]{2,1,0:T(8,128)S(1)}, u32[]{:S(2)}, u32[]{:S(2)}) collective-permute-start(f32[22,32,128]{2,1,0:T(8,128)S(1)} %get-tuple-element.19.mine), channel_id=1, source_target_pairs={{1,2},{2,1},{3,4},{4,3},{5,6},{6,5},{7,8},{8,7},{9,10},{10,9},{11,... | collective-permute-start | bytes 1081352 | tf_op jit(solution)/shard_map/ppermute | solution.py:374
  22.2 18.9 %collective-permute-start.2 = (f32[22,32,128]{2,1,0:T(8,128)S(1)}, f32[22,32,128]{2,1,0:T(8,128)S(1)}, u32[]{:S(2)}, u32[]{:S(2)}) collective-permute-start(f32[22,32,128]{2,1,0:T(8,128)S(1)} %get-tuple-element.19.mine), channel_id=1, source_target_pairs={{0,1},{1,0},{2,3},{3,2},{4,5},{5,4},{6,7},{7,6},{8,9},{9,8},{10,11... | collective-permute-start | bytes 1081352 | tf_op jit(solution)/shard_map/ppermute | solution.py:374
  22.3 12.8 %collective-permute-start.7 = (f32[9,16,128]{2,1,0:T(8,128)S(1)}, f32[9,16,128]{2,1,0:T(8,128)S(1)}, u32[]{:S(2)}, u32[]{:S(2)}) collective-permute-start(f32[9,16,128]{2,1,0:T(8,128)S(1)} %get-tuple-element.20.own), channel_id=1, source_target_pairs={{3,6},{6,3},{4,7},{7,4},{5,8},{8,5},{9,12},{12,9},{10,13},{13,10},... | collective-permute-start | bytes 221192 | tf_op jit(solution)/shard_map/ppermute | solution.py:374
  24.2 11.0 %collective-permute-start.6 = (f32[9,16,128]{2,1,0:T(8,128)S(1)}, f32[9,16,128]{2,1,0:T(8,128)S(1)}, u32[]{:S(2)}, u32[]{:S(2)}) collective-permute-start(f32[9,16,128]{2,1,0:T(8,128)S(1)} %get-tuple-element.20.own), channel_id=1, source_target_pairs={{0,3},{3,0},{1,4},{4,1},{2,5},{5,2},{6,9},{9,6},{7,10},{10,7},{8,1... | collective-permute-start | bytes 221192 | tf_op jit(solution)/shard_map/ppermute | solution.py:374
  27.4 10.8 %collective-permute-start.5 = (f32[9,16,128]{2,1,0:T(8,128)S(1)}, f32[9,16,128]{2,1,0:T(8,128)S(1)}, u32[]{:S(2)}, u32[]{:S(2)}) collective-permute-start(f32[9,16,128]{2,1,0:T(8,128)S(1)} %get-tuple-element.20.own), channel_id=1, source_target_pairs={{2,4},{4,2},{3,5},{5,3},{6,8},{8,6},{7,9},{9,7},{10,12},{12,10},{1... | collective-permute-start | bytes 221192 | tf_op jit(solution)/shard_map/ppermute | solution.py:374
  35.1 5.9 %collective-permute-start.4 = (f32[9,16,128]{2,1,0:T(8,128)S(1)}, f32[9,16,128]{2,1,0:T(8,128)S(1)}, u32[]{:S(2)}, u32[]{:S(2)}) collective-permute-start(f32[9,16,128]{2,1,0:T(8,128)S(1)} %get-tuple-element.20.own), channel_id=1, source_target_pairs={{0,2},{2,0},{1,3},{3,1},{4,6},{6,4},{5,7},{7,5},{8,10},{10,8},{9,1... | collective-permute-start | bytes 221192 | tf_op jit(solution)/shard_map/ppermute | solution.py:374
  45.9 22.0 %all-to-all-start = ((f32[64,1,128]{2,1,0:T(1,128)}), f32[64,1,128]{2,1,0:T(1,128)S(1)}, u32[]{:S(2)}, u32[]{:S(2)}) async-start(f32[64,1,128]{2,1,0:T(1,128)} %broadcast_in_dim.9), calls=%async_computation | async-start | bytes 65536 | tf_op jit(solution)/shard_map/all_to_all | solution.py:408
  54.5 14.5 %collective-permute-start.11 = (f32[6,16,128]{2,1,0:T(8,128)S(1)}, f32[6,16,128]{2,1,0:T(8,128)S(1)}, u32[]{:S(2)}, u32[]{:S(2)}) collective-permute-start(f32[6,16,128]{2,1,0:T(8,128)S(1)} %get-tuple-element.23.own), channel_id=1, source_target_pairs={{2,4},{4,2},{3,5},{5,3},{6,8},{8,6},{7,9},{9,7},{10,12},{12,10},{1... | collective-permute-start | bytes 147464 | tf_op jit(solution)/shard_map/ppermute | solution.py:374
  61.5 7.6 %collective-permute-start.10 = (f32[6,16,128]{2,1,0:T(8,128)S(1)}, f32[6,16,128]{2,1,0:T(8,128)S(1)}, u32[]{:S(2)}, u32[]{:S(2)}) collective-permute-start(f32[6,16,128]{2,1,0:T(8,128)S(1)} %get-tuple-element.23.own), channel_id=1, source_target_pairs={{0,2},{2,0},{1,3},{3,1},{4,6},{6,4},{5,7},{7,5},{8,10},{10,8},{9,1... | collective-permute-start | bytes 147464 | tf_op jit(solution)/shard_map/ppermute | solution.py:374
  61.6 7.5 %collective-permute-start.8 = (f32[6,32,128]{2,1,0:T(8,128)S(1)}, f32[6,32,128]{2,1,0:T(8,128)S(1)}, u32[]{:S(2)}, u32[]{:S(2)}) collective-permute-start(f32[6,32,128]{2,1,0:T(8,128)S(1)} %get-tuple-element.28), channel_id=1, source_target_pairs={{0,1},{1,0},{2,3},{3,2},{4,5},{5,4},{6,7},{7,6},{8,9},{9,8},{10,11... | collective-permute-start | bytes 294920 | tf_op jit(solution)/shard_map/ppermute | solution.py:374
  62.4 10.7 %collective-permute-start.9 = (f32[6,32,128]{2,1,0:T(8,128)S(1)}, f32[6,32,128]{2,1,0:T(8,128)S(1)}, u32[]{:S(2)}, u32[]{:S(2)}) collective-permute-start(f32[6,32,128]{2,1,0:T(8,128)S(1)} %get-tuple-element.29), channel_id=1, source_target_pairs={{1,2},{2,1},{3,4},{4,3},{5,6},{6,5},{7,8},{8,7},{9,10},{10,9},{11,... | collective-permute-start | bytes 294920 | tf_op jit(solution)/shard_map/ppermute | solution.py:374
  67.9 0.7 copy-start.2

commit v3 on v2

v3 whole, which is shorter than its diff:
```python
import functools
import math

import jax
import jax.numpy as jnp
from jax import lax
from jax.experimental import pallas as pl
from jax.experimental.pallas import tpu as pltpu
from jax.sharding import PartitionSpec as P

SMOOTH = 2
CDEG = 4
FINE = (0.25, 2.0)
COARSE = (0.02, 2.0)


def coefficients(low_end, high_end, degree):
    centre = (high_end + low_end) / 2.0
    half = (high_end - low_end) / 2.0
    ratio = centre / half
    rho = 1.0 / ratio
    steps = []
    for _ in range(degree - 1):
        after = 1.0 / (2.0 * ratio - rho)
        steps.append((after * rho, 2.0 * after / half))
        rho = after
    return 1.0 / centre, steps, ratio


FIRST_F, STEPS_F, _ = coefficients(*FINE, SMOOTH)
FIRST_C, STEPS_C, RATIO_C = coefficients(*COARSE, 2 * CDEG)


def lanes(shape):
    return lax.broadcasted_iota(jnp.int32, shape, len(shape) - 1)


def ahead(v, axis, by=1):
    n = v.shape[axis]
    at = lax.broadcasted_iota(jnp.int32, v.shape, axis)
    return jnp.where(at < n - by, pltpu.roll(v, n - by, axis), 0.0)


def back(v, axis, by=1):
    at = lax.broadcasted_iota(jnp.int32, v.shape, axis)
    return jnp.where(at >= by, pltpu.roll(v, by, axis), 0.0)


def operate(u, m, step):
    low = [c[:-1] for c in u]
    gz = [c[1:] - l for c, l in zip(u, low)]
    gx0 = ahead(low[0], 2, step) - low[0]
    gy1 = ahead(low[1], 1) - low[1]
    s = m * (gx0 + gy1 + gz[2])
    inner = m[1:]
    si = s[1:]
    out = []
    for c in range(3):
        here = low[c][1:]
        fx = inner * (gx0[1:] if c == 0 else ahead(here, 2, step) - here)
        fy = inner * (gy1[1:] if c == 1 else ahead(here, 1) - here)
        fz = m * gz[c]
        if c == 0:
            fx = fx + si
        elif c == 1:
            fy = fy + si
        else:
            fz = fz + s
        out.append((fz[:-1] - fz[1:]) + (back(fy, 1) - fy) + (back(fx, 2, step) - fx))
    return out


def inverse(m, step):
    here = m[1:]
    below = m[:-1]
    by = back(here, 1)
    bx = back(here, 2, step)
    lap = (here + below) + (here + by) + (here + bx) + here
    inside = here > 0.0
    return [
        jnp.where(inside, 1.0 / jnp.where(inside, lap + d, 1.0), 0.0) for d in (bx, by, below)
    ]


def trim(v, n=1):
    return v[n : v.shape[0] - n]


def halve_rows(tmp, v):
    k, rows, _ = v.shape
    tmp[0:k] = v
    return tmp[0:k, pl.ds(0, rows // 2, stride=2), :] + tmp[0:k, pl.ds(1, rows // 2, stride=2), :]


def pack(even_sum, odd_sum):
    even = lanes(even_sum.shape) % 2 == 0
    ax = even_sum.ndim - 1
    near = jnp.where(even, even_sum, odd_sum)
    far = jnp.where(even, pltpu.roll(even_sum, 127, ax), pltpu.roll(odd_sum, 1, ax))
    return near + far


def pair_layers(v):
    return jnp.concatenate([v[i : i + 1] + v[i + 1 : i + 2] for i in range(0, v.shape[0], 2)], 0)


def spread(tmp, e):
    k, rows, _ = e.shape
    even = lanes(e.shape) % 2 == 0
    both = jnp.where(even, e, pltpu.roll(e, 1, 2))
    tmp[0:k, pl.ds(0, rows, stride=2), :] = both
    tmp[0:k, pl.ds(1, rows, stride=2), :] = both
    return tmp[0:k]


def layers(v, order):
    return jnp.concatenate([v[i : i + 1] for i in order], 0)


def by_side(flag, put, a, b):
    lower = flag == 0

    @pl.when(lower)
    def _():
        put(a, b)

    @pl.when(jnp.logical_not(lower))
    def _():
        put(b, a)


def side(ref, c, first, count):
    return ref[c, pl.ds(first, count)]


def first_kernel(
    par, f_ref, e_ref, a_ref, b_ref, s_ref,
    x_ref, r_ref, m_ref, cf_ref, cm_ref, send_a, send_b, far_ref,
    fe, tmp,
):
    for c in range(3):
        fe[c, 4:8] = f_ref[c]
    m_ref[5:9] = 0.4 * e_ref[...]
    m_ref[0:1] = 0.4 * s_ref[...]

    def take(up, down):
        for c in range(3):
            fe[c, 8:12] = up[4 * c : 4 * c + 4]
            fe[c, 0:4] = down[4 * c : 4 * c + 4]
        m_ref[9:13] = 0.4 * up[12:16]
        m_ref[1:5] = 0.4 * down[12:16]

    by_side(par[0], take, a_ref, b_ref)
    m = m_ref[...]
    p = inverse(m, 1)
    r = [fe[c] for c in range(3)]
    w = [p[c] * r[c] * FIRST_F for c in range(3)]
    aw = operate(w, m[1:12], 1)
    r = [trim(r[c]) - aw[c] for c in range(3)]
    now, gain = STEPS_F[0]
    w2 = [now * trim(w[c]) + gain * (trim(p[c]) * r[c]) for c in range(3)]
    aw = operate(w2, m[2:11], 1)
    cm = halve_rows(tmp, pair_layers(m[1:13])) * 0.125
    cm = pack(cm, cm)
    cm_ref[...] = cm
    far_ref[12:18] = cm
    for c in range(3):
        x_ref[c] = w[c][4:8] + w2[c][3:7]
        done = trim(r[c]) - aw[c]
        r_ref[c] = done
        rc = halve_rows(tmp, pair_layers(done)) * 0.5
        fc = halve_rows(tmp, pair_layers(fe[c, 2:10])) * 0.5
        both = pack(rc, fc)
        cf_ref[c] = both
        far_ref[4 * c : 4 * c + 4] = both
    for ref, q in ((send_a, par[0]), (send_b, 1 - par[0])):
        for c in range(3):
            ref[4 * c : 4 * c + 4] = side(r_ref, c, 4 * q, 4)
            for j in range(2):
                ref[14 + c, 16 * j : 16 * j + 16] = cf_ref[c, 2 * q + j]
        ref[12:14] = m_ref[pl.ds(2 + 7 * q, 2)]


def second_kernel(
    top, par, f_ref, x_ref, r_ref, m_ref, own, own_cm, a1, b1, a3, b3,
    xo_ref, ro_ref, far_ref, mo_ref, cmo_ref, coarse_ref, sum_ref,
    re, me, cf, cm, tmp,
):
    for c in range(3):
        re[c, 4:12] = r_ref[c]
        cf[c, 6:10] = own[c]
    me[2:15] = m_ref[...]
    cm[6:12] = own_cm[...]

    def near(up, down):
        for c in range(3):
            re[c, 12:16] = up[4 * c : 4 * c + 4]
            re[c, 0:4] = down[4 * c : 4 * c + 4]
            for j in range(2):
                cf[c, 10 + j] = up[14 + c, 16 * j : 16 * j + 16]
                cf[c, 4 + j] = down[14 + c, 16 * j : 16 * j + 16]
        me[15:17] = up[12:14]
        me[0:2] = down[12:14]

    def third(up, down):
        for c in range(3):
            cf[c, 12:16] = up[4 * c : 4 * c + 4]
            cf[c, 0:4] = down[4 * c : 4 * c + 4]
        cm[12:17] = up[12:17]
        cm[0:6] = down[12:18]

    by_side(par[0], near, a1, b1)
    by_side(par[2], third, a3, b3)

    @pl.when(par[3] == 2)
    def _():
        for c in range(3):
            cf[c, 0:3] = jnp.zeros((3, 16, 128), jnp.float32)
            cf[c, 3] = b3[4 * c + 1]
        cm[0:4] = jnp.zeros((4, 16, 128), jnp.float32)
        cm[4:6] = b3[14:16]

    @pl.when(par[3] == top - 2)
    def _():
        for c in range(3):
            cf[c, 12] = b3[4 * c + 2]
            cf[c, 13:16] = jnp.zeros((3, 16, 128), jnp.float32)
        cm[12:14] = b3[14:16]
        cm[14:17] = jnp.zeros((3, 16, 128), jnp.float32)

    mc = cm[...]
    pc = inverse(mc, 2)
    r = [cf[c] for c in range(3)]
    w = [pc[c] * r[c] * FIRST_C for c in range(3)]
    e = [w[c][3:13] for c in range(3)]
    xc = [w[c][7:9] for c in range(3)]
    part = None
    for k in range(1, 8):
        aw = operate(w, mc[k : 17 - k], 2)
        r = [trim(r[c]) - aw[c] for c in range(3)]
        now, gain = STEPS_C[k - 1]
        if k == 4:
            odd = lanes((2, 16, 128)) % 2 == 1
            part = sum(
                jnp.sum(jnp.where(odd, xc[c] * (cf[c, 7:9] + r[c][3:5]), 0.0)) for c in range(3)
            )
        w = [now * trim(w[c]) + gain * (pc[c][k : 16 - k] * r[c]) for c in range(3)]
        if k <= 3:
            e = [e[c] + w[c][3 - k : 13 - k] for c in range(3)]
        xc = [xc[c] + w[c][7 - k : 9 - k] for c in range(3)]
    col = lax.broadcasted_iota(jnp.int32, (128, 64), 1)
    row = lax.broadcasted_iota(jnp.int32, (128, 64), 0)
    pick = jnp.where(row == 2 * col + 1, 1.0, 0.0).astype(jnp.float32)
    for c in range(3):
        coarse_ref[c] = jnp.dot(
            xc[c].reshape(32, 128), pick,
            precision=lax.Precision.HIGHEST, preferred_element_type=jnp.float32,
        ).reshape(2, 16, 64)

    m = me[...]
    order = [0] + [i for i in range(1, 9) for _ in range(2)] + [9]
    v = [layers(spread(tmp, e[c]), order) for c in range(3)]
    aw = operate(v, m, 1)
    p = inverse(m, 1)
    r = [re[c] - aw[c] for c in range(3)]
    now, gain = STEPS_F[0]
    w = [p[c] * r[c] * FIRST_F for c in range(3)]
    x = [x_ref[c] + v[c][7:11] + w[c][6:10] for c in range(3)]
    aw = operate(w, m[1:16], 1)
    r = [trim(r[c]) - aw[c] for c in range(3)]
    w = [now * trim(w[c]) + gain * (p[c][1:15] * r[c]) for c in range(3)]
    x = [x[c] + w[c][5:9] for c in range(3)]
    aw = operate(w, m[2:15], 1)
    r = [trim(r[c]) - aw[c] for c in range(3)]
    whole = sum(jnp.sum(x[c] * (f_ref[c] + r[c][4:8])) for c in range(3))
    w = [p[c][2:14] * r[c] * FIRST_F for c in range(3)]
    x = [x[c] + w[c][4:8] for c in range(3)]
    aw = operate(w, m[3:14], 1)
    r = [trim(r[c]) - aw[c] for c in range(3)]
    w = [now * trim(w[c]) + gain * (p[c][3:13] * r[c]) for c in range(3)]
    aw = operate(w, m[4:13], 1)
    for c in range(3):
        xo_ref[c] = x[c] + w[c][3:7]
        done = trim(r[c]) - aw[c]
        ro_ref[c] = done[1:7]
        rc = halve_rows(tmp, pair_layers(done)) * 0.5
        far_ref[2 * c : 2 * c + 1] = pack(rc[0:1], rc[1:2])
        far_ref[2 * c + 1 : 2 * c + 2] = pack(rc[2:3], rc[3:4])
    mo_ref[...] = m[5:12]
    cmo_ref[...] = mc[3:14]
    at = lanes((1, 128))
    sum_ref[...] = jnp.where(at == 0, whole, 0.0) + jnp.where(at == 1, part, 0.0)


def third_kernel(top, par, x_ref, r_ref, own, m_ref, cm_ref, a2, b2, out_ref, cf, tmp):
    for c in range(3):
        cf[c, 2:4] = own[2 * c : 2 * c + 2]

    def second(up, down):
        for c in range(3):
            cf[c, 4:6] = up[2 * c : 2 * c + 2]
            cf[c, 0:2] = down[2 * c : 2 * c + 2]

    by_side(par[1], second, a2, b2)
    even = lanes((16, 128)) % 2 == 0

    @pl.when(par[3] == 1)
    def _():
        for c in range(3):
            cf[c, 0] = jnp.zeros((16, 128), jnp.float32)
            cf[c, 1] = jnp.where(even, 0.0, b2[2 * c])

    @pl.when(par[3] == top - 1)
    def _():
        for c in range(3):
            cf[c, 4] = jnp.where(even, b2[2 * c + 1], 0.0)
            cf[c, 5] = jnp.zeros((16, 128), jnp.float32)

    mc = cm_ref[...]
    pc = inverse(mc, 2)
    r = []
    for c in range(3):
        near = cf[c]
        far = pltpu.roll(near, 127, 2)
        parts = [t[i : i + 1] for i in range(6) for t in (near, far)]
        r.append(jnp.concatenate(parts[1:11], 0))
    w = [pc[c] * r[c] * FIRST_C for c in range(3)]
    e = [w[c][3:7] for c in range(3)]
    for k in range(1, 4):
        aw = operate(w, mc[k : 11 - k], 2)
        r = [trim(r[c]) - aw[c] for c in range(3)]
        now, gain = STEPS_C[k - 1]
        w = [now * trim(w[c]) + gain * (pc[c][k : 10 - k] * r[c]) for c in range(3)]
        e = [e[c] + w[c][3 - k : 7 - k] for c in range(3)]

    m = m_ref[...]
    order = [0, 0, 1, 1, 2, 2, 3, 3]
    v = [layers(spread(tmp, e[c]), order) for c in range(3)]
    aw = operate(v, m, 1)
    p = inverse(m, 1)
    r = [r_ref[c] - aw[c] for c in range(3)]
    now, gain = STEPS_F[0]
    w = [p[c] * r[c] * FIRST_F for c in range(3)]
    aw = operate(w, m[1:6], 1)
    for c in range(3):
        after = r[c][1:5] - aw[c]
        out_ref[c] = x_ref[c] + v[c][2:6] + (1.0 + now) * w[c][1:5] + gain * (p[c][1:5] * after)


def call(kernel, outs, scratch, par, *args, flops=1 << 22):
    return pl.pallas_call(
        kernel,
        out_shape=[jax.ShapeDtypeStruct(s, jnp.float32) for s in outs],
        in_specs=[pl.BlockSpec(memory_space=pltpu.SMEM)]
        + [pl.BlockSpec(memory_space=pltpu.VMEM)] * len(args),
        out_specs=[pl.BlockSpec(memory_space=pltpu.VMEM)] * len(outs),
        scratch_shapes=[pltpu.VMEM(s, jnp.float32) for s in scratch],
        compiler_params=pltpu.CompilerParams(vmem_limit_bytes=16 << 20),
        cost_estimate=pl.CostEstimate(flops=flops, bytes_accessed=1 << 20, transcendentals=0),
    )(par, *args)


def half(i, distance):
    return (i // distance + (distance == 3 and i % 3 == 1)) % 2


def swap(x, distance, second, extra=(), axis="slab"):
    n = lax.axis_size(axis)
    pairs = list(extra)
    for i in range(n - distance):
        if half(i, distance) == second:
            pairs += [(i, i + distance), (i + distance, i)]
    return lax.ppermute(x, axis, pairs)


def cycles(force, modulus):
    me = lax.axis_index("slab")
    n = lax.axis_size("slab")
    par = jnp.stack([me % 2, (me // 2) % 2, (me // 3 + (me % 3 == 1)) % 2, me]).astype(jnp.int32)
    top = n - 1
    if half(top, 3) != 1 or half(top - 2, 3) != 1 or half(top, 2) != 1:
        raise ValueError("slab count")
    block = jnp.concatenate([force.reshape(12, 32, 128), modulus], 0)
    a = swap(block, 1, 0)
    b = swap(block, 1, 1)
    s = lax.ppermute(modulus[3:4], "slab", [(i, i + 2) for i in range(n - 2)])
    x, r, m, cf, cm, send_a, send_b, far = call(
        first_kernel,
        [
            (3, 4, 32, 128), (3, 8, 32, 128), (13, 32, 128), (3, 4, 16, 128), (6, 16, 128),
            (17, 32, 128), (17, 32, 128), (18, 16, 128),
        ],
        [(3, 12, 32, 128), (6, 32, 128)],
        par, force, modulus, a, b, s,
    )
    got = [swap(send_a, 1, 0), swap(send_b, 1, 1)]
    got += [swap(far, 3, 0), swap(far, 3, 1, ((0, 2), (top, top - 2)))]
    x, r, far, m, cm, coarse, part = call(
        functools.partial(second_kernel, top),
        [
            (3, 4, 32, 128), (3, 6, 32, 128), (6, 16, 128), (7, 32, 128), (11, 16, 128),
            (3, 2, 16, 64), (1, 128),
        ],
        [(3, 16, 32, 128), (17, 32, 128), (3, 16, 16, 128), (17, 16, 128), (10, 32, 128)],
        par, force, x, r, m, cf, cm, *got,
    )
    got = [swap(far, 2, 0), swap(far, 2, 1, ((0, 1), (top, top - 1)))]
    sums = lax.all_to_all(jnp.broadcast_to(part[None], (n, 1, 128)), "slab", 0, 0, tiled=True)
    (fine,) = call(
        functools.partial(third_kernel, top),
        [(3, 4, 32, 128)],
        [(3, 6, 16, 128), (4, 32, 128)],
        par, x, r, far, m, cm, *got,
    )
    cells = float(modulus.size * n)
    angle = math.acosh(RATIO_C)
    part_way = math.cosh(CDEG * angle)
    full = math.cosh(2 * CDEG * angle)
    scale = jnp.array([1.0 / cells, 2.0 * part_way * part_way / full / 4.0 / (cells / 8.0)], jnp.float32)
    return fine, coarse, sums.sum(axis=(0, 1))[:2] * scale


def solution(mesh):
    return jax.shard_map(
        cycles,
        mesh=mesh,
        in_specs=(P(None, "slab", None, "sample"), P("slab", None, "sample")),
        out_specs=(P(None, "slab", None, "sample"), P(None, "slab", None, "sample"), P("sample")),
        check_vma=False,
    )
```

time: 76 us -> 69.5 us (0.914)
  starting transfers between devices: 48.6 us -> 35.5 us
  waiting for transfers between devices: 15.2 us -> 20 us
  Pallas kernels: 8.1 us -> 10 us
  other arithmetic: 0.64 us -> 1.63 us
  local copies, waits for them, and re-layouts: 2.18 us -> 1.29 us
    ppermute x12 -> x8, starting transfers between devices: 40 us -> 23.1 us  [swap(): return lax.ppermute(x, axis, pairs)]
    ppermute x0 -> x1, waiting for transfers between devices: none -> 7.16 us  [cycles(): s = lax.ppermute(modulus[3:4], 'slab', [(i, i + 2) for i in range(n - 2)])]
    ppermute x12 -> x8, waiting for transfers between devices: 15.2 us -> 11.4 us  [swap(): return lax.ppermute(x, axis, pairs)]
    ppermute x0 -> x1, starting transfers between devices: none -> 2.83 us  [cycles(): s = lax.ppermute(modulus[3:4], 'slab', [(i, i + 2) for i in range(n - 2)])]
    pallas_call x3, Pallas kernels: 8.1 us -> 10 us  [call(): pl.pallas_call(kernel, out_shape=[jax.ShapeDtypeStruct(s, jnp.float32) fo...]
    all_to_all x1, waiting for transfers between devices: 0.01 us -> 1.41 us  [cycles(): lax.all_to_all(jnp.broadcast_to(part[None], (n, 1, 128)), 'slab', 0, 0, t...]
    concatenate x2 -> x1, other arithmetic: 0.02 us -> 1.02 us  [cycles(): block = jnp.concatenate([force.reshape(12, 32, 128), modulus], 0)]
    dynamic_slice x2 -> x0, local copies, waits for them, and re-layouts: 0.91 us -> none  [the longest x1 0.89 us: edge(): lax.dynamic_slice_in_dim(modulus, 1 - side, 3, 0)]
  transfers between devices with their start and end apart: 13 -> 10, of which waited for: 4 -> 6; matrix products, arithmetic and copies ran while one was open for 1% -> 1% of each run, Pallas kernels for 0% -> 0%
where the time goes in v3:
time: 69.5 us; the launch traced here: 69.2 us
  starting transfers between devices  35.5 us (51%)
  waiting for transfers between devices  20 us (29%)
  Pallas kernels  10 us (14%)
  other arithmetic  1.63 us (2%)
  local copies, waits for them, and re-layouts  1.29 us (2%)
  between operations  0.84 us (1%)
    ppermute x8, starting transfers between devices, swap(): return lax.ppermute(x, axis, pairs)  23.1 us
    ppermute x8, waiting for transfers between devices, swap(): return lax.ppermute(x, axis, pairs)  11.4 us
    pallas_call x3, Pallas kernels, call(): pl.pallas_call(kernel, out_shape=[jax.ShapeDtypeStruct(s, jnp.float32) fo...  10 us
    all_to_all x1, starting transfers between devices, cycles(): lax.all_to_all(jnp.broadcast_to(part[None], (n, 1, 128)), 'slab', 0, 0, t...  9.52 us
    ppermute x1, waiting for transfers between devices, cycles(): s = lax.ppermute(modulus[3:4], 'slab', [(i, i + 2) for i in range(n - 2)])  7.16 us
    ppermute x1, starting transfers between devices, cycles(): s = lax.ppermute(modulus[3:4], 'slab', [(i, i + 2) for i in range(n - 2)])  2.83 us
    all_to_all x1, waiting for transfers between devices, cycles(): lax.all_to_all(jnp.broadcast_to(part[None], (n, 1, 128)), 'slab', 0, 0, t...  1.41 us
  transfers between devices with their start and end apart: 10, of which 6 were waited for; matrix products, arithmetic and copies ran while one was open for 1% of the time, Pallas kernels for 0%

profile of v3, /device:TPU:32, one launch (start us, length us, event | category | flops | bytes accessed | tf_op | source)
XLA Modules:
  0.0 69.2 jit_solution(7589277072964063675)
XLA Ops:
  0.6 0.0 copy-start.1
  0.6 0.0 copy-start
  0.7 1.0 %pad_maximum_fusion = f32[16,32,128]{2,1,0:T(8,128)S(1)} fusion(f32[4,32,128]{2,1,0:T(8,128)} %e_ref.1, f32[12,32,128]{2,1,0:T(8,128)} %bitcast.7), kind=kLoop, calls=%fused_computation | loop fusion | flops 65536 | bytes 524288 | tf_op jit(solution)/shard_map/concatenate | solution.py:383
  1.7 6.7 %collective-permute-start.1 = (f32[16,32,128]{2,1,0:T(8,128)S(1)}, f32[16,32,128]{2,1,0:T(8,128)S(1)}, u32[]{:S(2)}, u32[]{:S(2)}) collective-permute-start(f32[16,32,128]{2,1,0:T(8,128)S(1)} %pad_maximum_fusion), channel_id=1, source_target_pairs={{1,2},{2,1},{3,4},{4,3},{5,6},{6,5},{7,8},{8,7},{9,10},{10,9},{11,... | collective-permute-start | bytes 786440 | tf_op jit(solution)/shard_map/ppermute | solution.py:373
  8.3 0.1 collective-permute-start
  8.4 0.0 copy-done.1
  8.5 2.8 %collective-permute-start.2 = (f32[1,32,128]{2,1,0:T(8,128)S(1)}, f32[1,32,128]{2,1,0:T(8,128)S(1)}, u32[]{:S(2)}, u32[]{:S(2)}) collective-permute-start(f32[1,32,128]{2,1,0:T(8,128)S(1)} %slice.6), channel_id=1, source_target_pairs={{0,2},{1,3},{2,4},{3,5},{4,6},{5,7},{6,8},{7,9},{8,10},{9,11},{10,... | collective-permute-start | bytes 49160 | tf_op jit(solution)/shard_map/ppermute | solution.py:386
  11.4 0.1 pad_add_fusion.par
  11.4 7.2 %collective-permute-done.2.s_ref = f32[1,32,128]{2,1,0:T(8,128)S(1)} collective-permute-done((f32[1,32,128]{2,1,0:T(8,128)S(1)}, f32[1,32,128]{2,1,0:T(8,128)S(1)}, u32[]{:S(2)}, u32[]{:S(2)}) %collective-permute-start.2) | collective-permute-done | bytes 16416 | tf_op jit(solution)/shard_map/ppermute | solution.py:386
  18.6 0.0 collective-permute-done.1.b_ref
  18.6 0.0 collective-permute-done.a_ref
  18.6 0.0 copy-done
  18.6 1.9 %shard_map.58 = (f32[3,4,32,128]{3,2,1,0:T(8,128)S(1)}, f32[3,8,32,128]{3,2,1,0:T(8,128)S(1)}, f32[13,32,128]{2,1,0:T(8,128)S(1)}, f32[3,4,16,128]{3,2,1,0:T(8,1...) custom-call(s32[4]{0:T(128)S(1)} %pad_add_fusion.par, ...), custom_call_target="tpu_custom_call" | custom-call | flops 4194304 | bytes 1048576 | tf_op jit(solution)/shard_map/pallas_call | solution.py:351
  20.6 2.1 %collective-permute-start.3 = (f32[17,32,128]{2,1,0:T(8,128)S(1)}, f32[17,32,128]{2,1,0:T(8,128)S(1)}, u32[]{:S(2)}, u32[]{:S(2)}) collective-permute-start(f32[17,32,128]{2,1,0:T(8,128)S(1)} %get-tuple-element.23), channel_id=1, source_target_pairs={{0,1},{1,0},{2,3},{3,2},{4,5},{5,4},{6,7},{7,6},{8,9},{9,8},{10,11... | collective-permute-start | bytes 835592 | tf_op jit(solution)/shard_map/ppermute | solution.py:373
  22.6 2.0 %collective-permute-start.4 = (f32[17,32,128]{2,1,0:T(8,128)S(1)}, f32[17,32,128]{2,1,0:T(8,128)S(1)}, u32[]{:S(2)}, u32[]{:S(2)}) collective-permute-start(f32[17,32,128]{2,1,0:T(8,128)S(1)} %get-tuple-element.24), channel_id=1, source_target_pairs={{1,2},{2,1},{3,4},{4,3},{5,6},{6,5},{7,8},{8,7},{9,10},{10,9},{11,... | collective-permute-start | bytes 835592 | tf_op jit(solution)/shard_map/ppermute | solution.py:373
  24.7 3.3 %collective-permute-start.6 = (f32[18,16,128]{2,1,0:T(8,128)S(1)}, f32[18,16,128]{2,1,0:T(8,128)S(1)}, u32[]{:S(2)}, u32[]{:S(2)}) collective-permute-start(f32[18,16,128]{2,1,0:T(8,128)S(1)} %get-tuple-element.25), channel_id=1, source_target_pairs={{0,2},{63,61},{1,4},{4,1},{3,6},{6,3},{5,8},{8,5},{7,10},{10,7},{9... | collective-permute-start | bytes 442376 | tf_op jit(solution)/shard_map/ppermute | solution.py:373
  28.0 1.9 %collective-permute-start.5 = (f32[18,16,128]{2,1,0:T(8,128)S(1)}, f32[18,16,128]{2,1,0:T(8,128)S(1)}, u32[]{:S(2)}, u32[]{:S(2)}) collective-permute-start(f32[18,16,128]{2,1,0:T(8,128)S(1)} %get-tuple-element.25), channel_id=1, source_target_pairs={{0,3},{3,0},{2,5},{5,2},{4,7},{7,4},{6,9},{9,6},{8,11},{11,8},{10,... | collective-permute-start | bytes 442376 | tf_op jit(solution)/shard_map/ppermute | solution.py:373
  29.9 8.2 %collective-permute-done.6.b3 = f32[18,16,128]{2,1,0:T(8,128)S(1)} collective-permute-done((f32[18,16,128]{2,1,0:T(8,128)S(1)}, f32[18,16,128]{2,1,0:T(8,128)S(1)}, u32[]{:S(2)}, u32[]{:S(2)}) %collective-permute-start.6) | collective-permute-done | bytes 147488 | tf_op jit(solution)/shard_map/ppermute | solution.py:373
  38.1 0.0 collective-permute-done.5.a3
  38.1 0.0 collective-permute-done.3.a1
  38.1 0.2 collective-permute-done.4.b1
  38.3 5.6 %shard_map.59 = (f32[3,4,32,128]{3,2,1,0:T(8,128)S(1)}, f32[3,6,32,128]{3,2,1,0:T(8,128)S(1)}, f32[6,16,128]{2,1,0:T(8,128)S(1)}, f32[7,32,128]{2,1,0:T(8,128)S(...) custom-call(s32[4]{0:T(128)S(1)} %pad_add_fusion.par, ...), custom_call_target="tpu_custom_call" | custom-call | flops 4194304 | bytes 1048576 | tf_op jit(solution)/shard_map/pallas_call | solution.py:351
  43.9 0.6 broadcast_in_dim.9
  44.5 9.5 %all-to-all-start = ((f32[64,1,128]{2,1,0:T(1,128)}), f32[64,1,128]{2,1,0:T(1,128)S(1)}, u32[]{:S(2)}, u32[]{:S(2)}) async-start(f32[64,1,128]{2,1,0:T(1,128)} %broadcast_in_dim.9), calls=%async_computation | async-start | bytes 65536 | tf_op jit(solution)/shard_map/all_to_all | solution.py:408
  54.0 7.0 %collective-permute-start.8 = (f32[6,16,128]{2,1,0:T(8,128)S(1)}, f32[6,16,128]{2,1,0:T(8,128)S(1)}, u32[]{:S(2)}, u32[]{:S(2)}) collective-permute-start(f32[6,16,128]{2,1,0:T(8,128)S(1)} %get-tuple-element.28.own), channel_id=1, source_target_pairs={{0,1},{63,62},{2,4},{4,2},{3,5},{5,3},{6,8},{8,6},{7,9},{9,7},{10,... | collective-permute-start | bytes 147464 | tf_op jit(solution)/shard_map/ppermute | solution.py:373
  61.0 0.1 collective-permute-start.7
  61.1 1.4 %all-to-all-done = f32[64,1,128]{2,1,0:T(1,128)S(1)} async-done(((f32[64,1,128]{2,1,0:T(1,128)}), f32[64,1,128]{2,1,0:T(1,128)S(1)}, u32[]{:S(2)}, u32[]{:S(2)}) %all-to-all-start) | async-done | bytes 32800 | tf_op jit(solution)/shard_map/all_to_all | solution.py:408
  62.5 0.0 copy-start.2
  62.6 0.6 copy-done.2
  63.2 0.5 slice_multiply_fusion
  63.7 0.8 %collective-permute-done.8.b2 = f32[6,16,128]{2,1,0:T(8,128)S(1)} collective-permute-done((f32[6,16,128]{2,1,0:T(8,128)S(1)}, f32[6,16,128]{2,1,0:T(8,128)S(1)}, u32[]{:S(2)}, u32[]{:S(2)}) %collective-permute-start.8) | collective-permute-done | bytes 49184 | tf_op jit(solution)/shard_map/ppermute | solution.py:373
  64.5 2.2 %collective-permute-done.7.a2 = f32[6,16,128]{2,1,0:T(8,128)S(1)} collective-permute-done((f32[6,16,128]{2,1,0:T(8,128)S(1)}, f32[6,16,128]{2,1,0:T(8,128)S(1)}, u32[]{:S(2)}, u32[]{:S(2)}) %collective-permute-start.7) | collective-permute-done | bytes 49184 | tf_op jit(solution)/shard_map/ppermute | solution.py:373
  66.7 2.5 %shard_map.60 = f32[3,4,32,128]{3,2,1,0:T(8,128)} custom-call(s32[4]{0:T(128)S(1)} %pad_add_fusion.par, f32[3,4,32,128]{3,2,1,0:T(8,128)S(1)} %get-tuple-element.26.x_ref, f32[3,6,32,128]{3,2,1,0:T(8,128)S(1)} %get-tuple-element.27.r_ref, f32[6,16,128]{2,1,0:T(8,128)S(1)} %get-tuple-element.28.own, f32[7,32,128]{2,1,0:T(8,128)S(1)} %get-tuple-element.29.m_ref, ...), custom_call_target="tpu_custom_call" | custom-call | flops 4194304 | bytes 1048576 | tf_op jit(solution)/shard_map/pallas_call | solution.py:351
  (2 shorter events, 0.0 us)
Async XLA Ops:
  0.6 7.8 %copy-start.1 = (f32[4,32,128]{2,1,0:T(8,128)S(1)}, f32[4,32,128]{2,1,0:T(8,128)}, u32[]{:S(2)}) copy-start(f32[4,32,128]{2,1,0:T(8,128)} %e_ref.1) | copy-start | bytes 196612
  0.6 18.0 %copy-start = (f32[3,4,32,128]{3,2,1,0:T(8,128)S(1)}, f32[3,4,32,128]{3,2,1,0:T(8,128)}, u32[]{:S(2)}) copy-start(f32[3,4,32,128]{3,2,1,0:T(8,128)} %f_ref.3) | copy-start | bytes 589828
  1.7 16.9 %collective-permute-start.1 = (f32[16,32,128]{2,1,0:T(8,128)S(1)}, f32[16,32,128]{2,1,0:T(8,128)S(1)}, u32[]{:S(2)}, u32[]{:S(2)}) collective-permute-start(f32[16,32,128]{2,1,0:T(8,128)S(1)} %pad_maximum_fusion), channel_id=1, source_target_pairs={{1,2},{2,1},{3,4},{4,3},{5,6},{6,5},{7,8},{8,7},{9,10},{10,9},{11,... | collective-permute-start | bytes 786440 | tf_op jit(solution)/shard_map/ppermute | solution.py:373
  8.3 10.3 %collective-permute-start = (f32[16,32,128]{2,1,0:T(8,128)S(1)}, f32[16,32,128]{2,1,0:T(8,128)S(1)}, u32[]{:S(2)}, u32[]{:S(2)}) collective-permute-start(f32[16,32,128]{2,1,0:T(8,128)S(1)} %pad_maximum_fusion), channel_id=1, source_target_pairs={{0,1},{1,0},{2,3},{3,2},{4,5},{5,4},{6,7},{7,6},{8,9},{9,8},{10,11... | collective-permute-start | bytes 786440 | tf_op jit(solution)/shard_map/ppermute | solution.py:373
  8.5 10.1 %collective-permute-start.2 = (f32[1,32,128]{2,1,0:T(8,128)S(1)}, f32[1,32,128]{2,1,0:T(8,128)S(1)}, u32[]{:S(2)}, u32[]{:S(2)}) collective-permute-start(f32[1,32,128]{2,1,0:T(8,128)S(1)} %slice.6), channel_id=1, source_target_pairs={{0,2},{1,3},{2,4},{3,5},{4,6},{5,7},{6,8},{7,9},{8,10},{9,11},{10,... | collective-permute-start | bytes 49160 | tf_op jit(solution)/shard_map/ppermute | solution.py:386
  20.6 17.5 %collective-permute-start.3 = (f32[17,32,128]{2,1,0:T(8,128)S(1)}, f32[17,32,128]{2,1,0:T(8,128)S(1)}, u32[]{:S(2)}, u32[]{:S(2)}) collective-permute-start(f32[17,32,128]{2,1,0:T(8,128)S(1)} %get-tuple-element.23), channel_id=1, source_target_pairs={{0,1},{1,0},{2,3},{3,2},{4,5},{5,4},{6,7},{7,6},{8,9},{9,8},{10,11... | collective-permute-start | bytes 835592 | tf_op jit(solution)/shard_map/ppermute | solution.py:373
  22.6 15.7 %collective-permute-start.4 = (f32[17,32,128]{2,1,0:T(8,128)S(1)}, f32[17,32,128]{2,1,0:T(8,128)S(1)}, u32[]{:S(2)}, u32[]{:S(2)}) collective-permute-start(f32[17,32,128]{2,1,0:T(8,128)S(1)} %get-tuple-element.24), channel_id=1, source_target_pairs={{1,2},{2,1},{3,4},{4,3},{5,6},{6,5},{7,8},{8,7},{9,10},{10,9},{11,... | collective-permute-start | bytes 835592 | tf_op jit(solution)/shard_map/ppermute | solution.py:373
  24.7 13.4 %collective-permute-start.6 = (f32[18,16,128]{2,1,0:T(8,128)S(1)}, f32[18,16,128]{2,1,0:T(8,128)S(1)}, u32[]{:S(2)}, u32[]{:S(2)}) collective-permute-start(f32[18,16,128]{2,1,0:T(8,128)S(1)} %get-tuple-element.25), channel_id=1, source_target_pairs={{0,2},{63,61},{1,4},{4,1},{3,6},{6,3},{5,8},{8,5},{7,10},{10,7},{9... | collective-permute-start | bytes 442376 | tf_op jit(solution)/shard_map/ppermute | solution.py:373
  28.0 10.1 %collective-permute-start.5 = (f32[18,16,128]{2,1,0:T(8,128)S(1)}, f32[18,16,128]{2,1,0:T(8,128)S(1)}, u32[]{:S(2)}, u32[]{:S(2)}) collective-permute-start(f32[18,16,128]{2,1,0:T(8,128)S(1)} %get-tuple-element.25), channel_id=1, source_target_pairs={{0,3},{3,0},{2,5},{5,2},{4,7},{7,4},{6,9},{9,6},{8,11},{11,8},{10,... | collective-permute-start | bytes 442376 | tf_op jit(solution)/shard_map/ppermute | solution.py:373
  44.5 18.0 %all-to-all-start = ((f32[64,1,128]{2,1,0:T(1,128)}), f32[64,1,128]{2,1,0:T(1,128)S(1)}, u32[]{:S(2)}, u32[]{:S(2)}) async-start(f32[64,1,128]{2,1,0:T(1,128)} %broadcast_in_dim.9), calls=%async_computation | async-start | bytes 65536 | tf_op jit(solution)/shard_map/all_to_all | solution.py:408
  54.0 10.5 %collective-permute-start.8 = (f32[6,16,128]{2,1,0:T(8,128)S(1)}, f32[6,16,128]{2,1,0:T(8,128)S(1)}, u32[]{:S(2)}, u32[]{:S(2)}) collective-permute-start(f32[6,16,128]{2,1,0:T(8,128)S(1)} %get-tuple-element.28.own), channel_id=1, source_target_pairs={{0,1},{63,62},{2,4},{4,2},{3,5},{5,3},{6,8},{8,6},{7,9},{9,7},{10,... | collective-permute-start | bytes 147464 | tf_op jit(solution)/shard_map/ppermute | solution.py:373
  61.0 5.7 %collective-permute-start.7 = (f32[6,16,128]{2,1,0:T(8,128)S(1)}, f32[6,16,128]{2,1,0:T(8,128)S(1)}, u32[]{:S(2)}, u32[]{:S(2)}) collective-permute-start(f32[6,16,128]{2,1,0:T(8,128)S(1)} %get-tuple-element.28.own), channel_id=1, source_target_pairs={{0,2},{2,0},{1,3},{3,1},{4,6},{6,4},{5,7},{7,5},{8,10},{10,8},{9,1... | collective-permute-start | bytes 147464 | tf_op jit(solution)/shard_map/ppermute | solution.py:373
  62.5 0.7 copy-start.2

commit v4 on v3

v4 whole, which is shorter than its diff:
```python
import functools
import math

import jax
import jax.numpy as jnp
from jax import lax
from jax.experimental import pallas as pl
from jax.experimental.pallas import tpu as pltpu
from jax.sharding import PartitionSpec as P

SMOOTH = 2
CDEG = 4
FINE = (0.25, 2.0)
COARSE = (0.02, 2.0)


def coefficients(low_end, high_end, degree):
    centre = (high_end + low_end) / 2.0
    half = (high_end - low_end) / 2.0
    ratio = centre / half
    rho = 1.0 / ratio
    steps = []
    for _ in range(degree - 1):
        after = 1.0 / (2.0 * ratio - rho)
        steps.append((after * rho, 2.0 * after / half))
        rho = after
    return 1.0 / centre, steps, ratio


FIRST_F, STEPS_F, _ = coefficients(*FINE, SMOOTH)
NOW_F, GAIN_F = STEPS_F[0]
FIRST_C, STEPS_C, RATIO_C = coefficients(*COARSE, 2 * CDEG)


def lanes(shape):
    return lax.broadcasted_iota(jnp.int32, shape, len(shape) - 1)


LINE = (1, 1, 8, 128)


def ahead_x(v, by):
    return jnp.where(lanes(LINE) < 128 - by, pltpu.roll(v, 128 - by, 3), 0.0)


def back_x(v, by):
    return jnp.where(lanes(LINE) >= by, pltpu.roll(v, by, 3), 0.0)


def ahead_y(v):
    at = lax.broadcasted_iota(jnp.int32, LINE, 2)
    moved = jnp.where(at < 7, pltpu.roll(v[:, :1], 7, 2), 0.0)
    return jnp.concatenate([v[:, 1:], moved], 1)


def back_y(v):
    at = lax.broadcasted_iota(jnp.int32, LINE, 2)
    moved = jnp.where(at >= 1, pltpu.roll(v[:, -1:], 1, 2), 0.0)
    return jnp.concatenate([moved, v[:, :-1]], 1)


def operate(u, m, step):
    low = [c[:-1] for c in u]
    gz = [c[1:] - l for c, l in zip(u, low)]
    gx0 = ahead_x(low[0], step) - low[0]
    gy1 = ahead_y(low[1]) - low[1]
    s = m * (gx0 + gy1 + gz[2])
    inner = m[1:]
    si = s[1:]
    out = []
    for c in range(3):
        here = low[c][1:]
        fx = inner * (gx0[1:] if c == 0 else ahead_x(here, step) - here)
        fy = inner * (gy1[1:] if c == 1 else ahead_y(here) - here)
        fz = m * gz[c]
        if c == 0:
            fx = fx + si
        elif c == 1:
            fy = fy + si
        else:
            fz = fz + s
        out.append((fz[:-1] - fz[1:]) + (back_y(fy) - fy) + (back_x(fx, step) - fx))
    return out


def inverse(m, step, scale=1.0):
    here = m[1:]
    below = m[:-1]
    by = back_y(here)
    bx = back_x(here, step)
    lap = (here + below) + (here + by) + (here + bx) + here
    inside = here > 0.0
    return [
        jnp.where(inside, scale / jnp.where(inside, lap + d, 1.0), 0.0) for d in (bx, by, below)
    ]


def trim(v, n=1):
    return v[n : v.shape[0] - n]


def tiles(v):
    return v.reshape(v.shape[0], v.shape[1] // 8, 8, 128)


def rows(v):
    return v.reshape(v.shape[0], v.shape[1] * 8, 128)


def strided(ref, *at):
    return jnp.concatenate([ref[(*at, pl.ds(v, 8, stride=4), slice(None))] for v in range(4)], 0)


def pack(even_sum, odd_sum):
    even = lanes(LINE) % 2 == 0
    near = jnp.where(even, even_sum, odd_sum)
    far = jnp.where(even, pltpu.roll(even_sum, 127, 3), pltpu.roll(odd_sum, 1, 3))
    return near + far


def pair_cells(v):
    out = []
    for i in range(0, v.shape[0], 2):
        t = v[i : i + 1] + v[i + 1 : i + 2]
        out.append(jnp.concatenate([t[:, 0:1] + t[:, 1:2], t[:, 2:3] + t[:, 3:4]], 1))
    return jnp.concatenate(out, 0)


def spread(e, order):
    even = lanes(LINE) % 2 == 0
    both = jnp.where(even, e, pltpu.roll(e, 1, 3))
    wide = jnp.concatenate([both[:, 0:1], both[:, 0:1], both[:, 1:2], both[:, 1:2]], 1)
    return jnp.concatenate([wide[i : i + 1] for i in order], 0)


def by_side(flag, put, a, b):
    lower = flag == 0

    @pl.when(lower)
    def _():
        put(a, b)

    @pl.when(jnp.logical_not(lower))
    def _():
        put(b, a)


def first_kernel(
    par, f_ref, e_ref, a_ref, b_ref, s_ref,
    x_ref, r_ref, m_ref, p_ref, cf_ref, cm_ref, send_a, send_b, far_ref,
    fe,
):
    for z in range(4):
        for c in range(3):
            fe[c, 4 + z] = strided(f_ref, c, z)
        m_ref[5 + z] = 0.4 * strided(e_ref, z)
    m_ref[0] = 0.4 * strided(s_ref, 0)

    def take(up, down):
        for z in range(4):
            for c in range(3):
                fe[c, 8 + z] = strided(up, 4 * c + z)
                fe[c, z] = strided(down, 4 * c + z)
            m_ref[9 + z] = 0.4 * strided(up, 12 + z)
            m_ref[1 + z] = 0.4 * strided(down, 12 + z)

    by_side(par[0], take, a_ref, b_ref)
    m = tiles(m_ref[...])
    p = inverse(m, 1, GAIN_F)
    r = [tiles(fe[c]) for c in range(3)]
    w = [p[c] * r[c] * (FIRST_F / GAIN_F) for c in range(3)]
    aw = operate(w, m[1:12], 1)
    f = r
    r = [trim(r[c]) - aw[c] for c in range(3)]
    w2 = [NOW_F * trim(w[c]) + trim(p[c]) * r[c] for c in range(3)]
    aw = operate(w2, m[2:11], 1)
    cm = pair_cells(m[1:13]) * 0.125
    cm = rows(pack(cm, cm))
    cm_ref[...] = cm
    far_ref[12:18] = cm
    for c in range(3):
        p_ref[c] = rows(p[c])
        x_ref[c] = rows(w[c][4:8] + w2[c][3:7])
        done = trim(r[c]) - aw[c]
        r_ref[c] = rows(done)
        both = rows(pack(pair_cells(done) * 0.5, pair_cells(f[c][2:10]) * 0.5))
        cf_ref[c] = both
        far_ref[4 * c : 4 * c + 4] = both
    for ref, q in ((send_a, par[0]), (send_b, 1 - par[0])):
        for c in range(3):
            ref[4 * c : 4 * c + 4] = r_ref[c, pl.ds(4 * q, 4)]
            for j in range(2):
                ref[14 + c, 16 * j : 16 * j + 16] = cf_ref[c, 2 * q + j]
        ref[12:14] = m_ref[pl.ds(2 + 7 * q, 2)]


def second_kernel(
    top, par, f_ref, x_ref, r_ref, m_ref, p_ref, own, own_cm, a1, b1, a3, b3,
    xo_ref, ro_ref, far_ref, cmo_ref, pco_ref, xc_ref, rc_ref, wc_ref, sum_ref,
    re, me, cf, cm,
):
    for c in range(3):
        re[c, 4:12] = r_ref[c]
        cf[c, 6:10] = own[c]
    me[2:15] = m_ref[...]
    cm[6:12] = own_cm[...]

    def near(up, down):
        for c in range(3):
            re[c, 12:16] = up[4 * c : 4 * c + 4]
            re[c, 0:4] = down[4 * c : 4 * c + 4]
            for j in range(2):
                cf[c, 10 + j] = up[14 + c, 16 * j : 16 * j + 16]
                cf[c, 4 + j] = down[14 + c, 16 * j : 16 * j + 16]
        me[15:17] = up[12:14]
        me[0:2] = down[12:14]

    def third(up, down):
        for c in range(3):
            cf[c, 12:16] = up[4 * c : 4 * c + 4]
            cf[c, 0:4] = down[4 * c : 4 * c + 4]
        cm[12:17] = up[12:17]
        cm[0:6] = down[12:18]

    by_side(par[0], near, a1, b1)
    by_side(par[2], third, a3, b3)

    @pl.when(par[3] == 2)
    def _():
        for c in range(3):
            cf[c, 0:3] = jnp.zeros((3, 16, 128), jnp.float32)
            cf[c, 3] = b3[4 * c + 1]
        cm[0:4] = jnp.zeros((4, 16, 128), jnp.float32)
        cm[4:6] = b3[14:16]

    @pl.when(par[3] == top - 2)
    def _():
        for c in range(3):
            cf[c, 12] = b3[4 * c + 2]
            cf[c, 13:16] = jnp.zeros((3, 16, 128), jnp.float32)
        cm[12:14] = b3[14:16]
        cm[14:17] = jnp.zeros((3, 16, 128), jnp.float32)

    mc = tiles(cm[...])
    pc = inverse(mc, 2)
    r = [tiles(cf[c]) for c in range(3)]
    own_rhs = [t[7:9] for t in r]
    w = [pc[c] * r[c] * FIRST_C for c in range(3)]
    e = [w[c][3:13] for c in range(3)]
    xc = [w[c][7:9] for c in range(3)]
    part = None
    for k in range(1, 5):
        aw = operate(w, mc[k : 17 - k], 2)
        r = [trim(r[c]) - aw[c] for c in range(3)]
        now, gain = STEPS_C[k - 1]
        if k == 4:
            odd = lanes(LINE) % 2 == 1
            part = sum(
                jnp.sum(jnp.where(odd, xc[c] * (own_rhs[c] + r[c][3:5]), 0.0)) for c in range(3)
            )
        w = [now * trim(w[c]) + gain * (pc[c][k : 16 - k] * r[c]) for c in range(3)]
        if k <= 3:
            e = [e[c] + w[c][3 - k : 13 - k] for c in range(3)]
        xc = [xc[c] + w[c][7 - k : 9 - k] for c in range(3)]
    for c in range(3):
        xc_ref[c] = rows(xc[c])
        rc_ref[c] = rows(r[c])
        wc_ref[c] = rows(w[c])
        pco_ref[c] = rows(pc[c][3:13])

    m = tiles(me[...])
    order = [0] + [i for i in range(1, 9) for _ in range(2)] + [9]
    v = [spread(e[c], order) for c in range(3)]
    aw = operate(v, m, 1)
    low = inverse(m[0:3], 1, GAIN_F)
    high = inverse(m[14:17], 1, GAIN_F)
    p = [jnp.concatenate([low[c], tiles(p_ref[c]), high[c]], 0) for c in range(3)]
    r = [tiles(re[c]) - aw[c] for c in range(3)]
    start = FIRST_F / GAIN_F
    w = [p[c] * r[c] * start for c in range(3)]
    x = [tiles(x_ref[c]) + v[c][7:11] + w[c][6:10] for c in range(3)]
    aw = operate(w, m[1:16], 1)
    r = [trim(r[c]) - aw[c] for c in range(3)]
    w = [NOW_F * trim(w[c]) + p[c][1:15] * r[c] for c in range(3)]
    x = [x[c] + w[c][5:9] for c in range(3)]
    aw = operate(w, m[2:15], 1)
    r = [trim(r[c]) - aw[c] for c in range(3)]
    f = [
        jnp.concatenate([strided(f_ref, c, z).reshape(1, 4, 8, 128) for z in range(4)], 0)
        for c in range(3)
    ]
    whole = sum(jnp.sum(x[c] * (f[c] + r[c][4:8])) for c in range(3))
    w = [p[c][2:14] * r[c] * start for c in range(3)]
    x = [x[c] + w[c][4:8] for c in range(3)]
    aw = operate(w, m[3:14], 1)
    r = [trim(r[c]) - aw[c] for c in range(3)]
    w = [NOW_F * trim(w[c]) + p[c][3:13] * r[c] for c in range(3)]
    aw = operate(w, m[4:13], 1)
    for c in range(3):
        xo_ref[c] = rows(x[c] + w[c][3:7])
        done = trim(r[c]) - aw[c]
        ro_ref[c] = rows(done[1:7])
        rc = pair_cells(done) * 0.5
        far_ref[2 * c : 2 * c + 1] = rows(pack(rc[0:1], rc[1:2]))
        far_ref[2 * c + 1 : 2 * c + 2] = rows(pack(rc[2:3], rc[3:4]))
    cmo_ref[...] = cm[3:14]
    at = lanes((1, 128))
    line = jnp.where(at == 0, whole, 0.0) + jnp.where(at == 1, part, 0.0)
    sum_ref[...] = jnp.broadcast_to(line[None], sum_ref.shape)


def late_kernel(cm_ref, pc_ref, xc_ref, rc_ref, wc_ref, coarse_ref):
    mc = tiles(cm_ref[...])
    pc = [tiles(pc_ref[c]) for c in range(3)]
    xc = [tiles(xc_ref[c]) for c in range(3)]
    r = [tiles(rc_ref[c]) for c in range(3)]
    w = [tiles(wc_ref[c]) for c in range(3)]
    for k in range(5, 8):
        aw = operate(w, mc[k - 3 : 14 - k], 2)
        r = [trim(r[c]) - aw[c] for c in range(3)]
        now, gain = STEPS_C[k - 1]
        w = [now * trim(w[c]) + gain * (pc[c][k - 3 : 13 - k] * r[c]) for c in range(3)]
        xc = [xc[c] + w[c][7 - k : 9 - k] for c in range(3)]
    col = lax.broadcasted_iota(jnp.int32, (128, 64), 1)
    row = lax.broadcasted_iota(jnp.int32, (128, 64), 0)
    pick = jnp.where(row == 2 * col + 1, 1.0, 0.0).astype(jnp.float32)
    for c in range(3):
        solved = jnp.dot(
            xc[c].reshape(32, 128), pick,
            precision=lax.Precision.HIGHEST, preferred_element_type=jnp.float32,
        )
        for z in range(2):
            for t in range(2):
                at = 16 * z + 8 * t
                coarse_ref[c, z, pl.ds(t, 8, stride=2), :] = solved[at : at + 8]


def third_kernel(
    top, scale, par, x_ref, r_ref, own, m_ref, p_ref, cm_ref, pc_ref, sums, a2, b2, out_ref, sum_ref, cf
):
    for c in range(3):
        cf[c, 2:4] = own[2 * c : 2 * c + 2]

    def second(up, down):
        for c in range(3):
            cf[c, 4:6] = up[2 * c : 2 * c + 2]
            cf[c, 0:2] = down[2 * c : 2 * c + 2]

    by_side(par[1], second, a2, b2)
    even = lanes((16, 128)) % 2 == 0

    @pl.when(par[3] == 1)
    def _():
        for c in range(3):
            cf[c, 0] = jnp.zeros((16, 128), jnp.float32)
            cf[c, 1] = jnp.where(even, 0.0, b2[2 * c])

    @pl.when(par[3] == top - 1)
    def _():
        for c in range(3):
            cf[c, 4] = jnp.where(even, b2[2 * c + 1], 0.0)
            cf[c, 5] = jnp.zeros((16, 128), jnp.float32)

    for k in range(2):
        sum_ref[k] = jnp.sum(jnp.where(lanes((64, 1, 128)) == k, sums[...], 0.0)) * scale[k]
    mc = tiles(cm_ref[...])
    pc = [tiles(pc_ref[c]) for c in range(3)]
    r = []
    for c in range(3):
        near = tiles(cf[c])
        far = pltpu.roll(near, 127, 3)
        parts = [t[i : i + 1] for i in range(6) for t in (near, far)]
        r.append(jnp.concatenate(parts[1:11], 0))
    w = [pc[c] * r[c] * FIRST_C for c in range(3)]
    e = [w[c][3:7] for c in range(3)]
    for k in range(1, 4):
        aw = operate(w, mc[k : 11 - k], 2)
        r = [trim(r[c]) - aw[c] for c in range(3)]
        now, gain = STEPS_C[k - 1]
        w = [now * trim(w[c]) + gain * (pc[c][k : 10 - k] * r[c]) for c in range(3)]
        e = [e[c] + w[c][3 - k : 7 - k] for c in range(3)]

    m = tiles(m_ref[3:10])
    order = [0, 0, 1, 1, 2, 2, 3, 3]
    v = [spread(e[c], order) for c in range(3)]
    aw = operate(v, m, 1)
    p = [tiles(p_ref[c, 3:9]) for c in range(3)]
    r = [tiles(r_ref[c]) - aw[c] for c in range(3)]
    w = [p[c] * r[c] * (FIRST_F / GAIN_F) for c in range(3)]
    aw = operate(w, m[1:6], 1)
    for c in range(3):
        after = r[c][1:5] - aw[c]
        x = tiles(x_ref[c]) + v[c][2:6] + (1.0 + NOW_F) * w[c][1:5] + p[c][1:5] * after
        for z in range(4):
            for t in range(4):
                out_ref[c, z, pl.ds(t, 8, stride=4), :] = x[z, t]


def call(kernel, outs, scratch, *args, par=None, small=(), flops=1 << 22):
    head = () if par is None else (par,)
    places = [pltpu.SMEM if i in small else pltpu.VMEM for i in range(len(outs))]
    return pl.pallas_call(
        kernel,
        out_shape=[jax.ShapeDtypeStruct(s, jnp.float32) for s in outs],
        in_specs=[pl.BlockSpec(memory_space=pltpu.SMEM)] * len(head)
        + [pl.BlockSpec(memory_space=pltpu.VMEM)] * len(args),
        out_specs=[pl.BlockSpec(memory_space=place) for place in places],
        scratch_shapes=[pltpu.VMEM(s, jnp.float32) for s in scratch],
        compiler_params=pltpu.CompilerParams(vmem_limit_bytes=16 << 20),
        cost_estimate=pl.CostEstimate(flops=flops, bytes_accessed=1 << 20, transcendentals=0),
    )(*head, *args)


def half(i, distance):
    return (i // distance + (distance == 3 and i % 3 == 1)) % 2


def swap(x, distance, second, extra=(), axis="slab"):
    n = lax.axis_size(axis)
    pairs = list(extra)
    for i in range(n - distance):
        if half(i, distance) == second:
            pairs += [(i, i + distance), (i + distance, i)]
    return lax.ppermute(x, axis, pairs)


def cycles(force, modulus):
    me = lax.axis_index("slab")
    n = lax.axis_size("slab")
    par = jnp.stack([me % 2, (me // 2) % 2, (me // 3 + (me % 3 == 1)) % 2, me]).astype(jnp.int32)
    top = n - 1
    if half(top, 3) != 1 or half(top - 2, 3) != 1 or half(top, 2) != 1:
        raise ValueError("slab count")
    block = jnp.concatenate([force.reshape(12, 32, 128), modulus], 0)
    a = swap(block, 1, 0)
    b = swap(block, 1, 1)
    s = lax.ppermute(modulus[3:4], "slab", [(i, i + 2) for i in range(n - 2)])
    x, r, m, p, cf, cm, send_a, send_b, far = call(
        first_kernel,
        [
            (3, 4, 32, 128), (3, 8, 32, 128), (13, 32, 128), (3, 12, 32, 128), (3, 4, 16, 128),
            (6, 16, 128), (17, 32, 128), (17, 32, 128), (18, 16, 128),
        ],
        [(3, 12, 32, 128)],
        force, modulus, a, b, s, par=par,
    )
    got = [swap(send_a, 1, 0), swap(send_b, 1, 1)]
    got += [swap(far, 3, 0), swap(far, 3, 1, ((0, 2), (top, top - 2)))]
    x, r, far, cm, pc, xc, rc, wc, part = call(
        functools.partial(second_kernel, top),
        [
            (3, 4, 32, 128), (3, 6, 32, 128), (6, 16, 128), (11, 16, 128), (3, 10, 16, 128),
            (3, 2, 16, 128), (3, 8, 16, 128), (3, 8, 16, 128), (n, 1, 128),
        ],
        [(3, 16, 32, 128), (17, 32, 128), (3, 16, 16, 128), (17, 16, 128)],
        force, x, r, m, p, cf, cm, *got, par=par,
    )
    got = [swap(far, 2, 0), swap(far, 2, 1, ((0, 1), (top, top - 1)))]
    sums = lax.all_to_all(part, "slab", 0, 0, tiled=True)
    (coarse,) = call(late_kernel, [(3, 2, 16, 64)], [], cm, pc, xc, rc, wc)
    cells = float(modulus.size * n)
    angle = math.acosh(RATIO_C)
    part_way = math.cosh(CDEG * angle)
    full = math.cosh(2 * CDEG * angle)
    scale = (1.0 / cells, 2.0 * part_way * part_way / full / 4.0 / (cells / 8.0))
    fine, total = call(
        functools.partial(third_kernel, top, scale),
        [(3, 4, 32, 128), (2,)],
        [(3, 6, 16, 128)],
        x, r, far, m, p, cm, pc, sums, *got, par=par, small=(1,),
    )
    return fine, coarse, total


def solution(mesh):
    return jax.shard_map(
        cycles,
        mesh=mesh,
        in_specs=(P(None, "slab", None, "sample"), P("slab", None, "sample")),
        out_specs=(P(None, "slab", None, "sample"), P(None, "slab", None, "sample"), P("sample")),
        check_vma=False,
    )
```

time: 69.5 us -> 71.6 us (1.030)
  the two profiles are of different devices: /device:TPU:32 before, /device:TPU:0 now
where the time goes in v4:
time: 71.6 us; the launch traced here: 71.3 us
  starting transfers between devices  45.4 us (63%)
  waiting for transfers between devices  13.6 us (19%)
  Pallas kernels  10.4 us (15%)
  other arithmetic  1.1 us (2%)
  between operations  0.81 us (1%)
    ppermute x8, starting transfers between devices, swap(): return lax.ppermute(x, axis, pairs)  25.2 us
    all_to_all x1, starting transfers between devices, cycles(): sums = lax.all_to_all(part, 'slab', 0, 0, tiled=True)  15.6 us
    pallas_call x4, Pallas kernels, call(): pl.pallas_call(kernel, out_shape=[jax.ShapeDtypeStruct(s, jnp.float32) fo...  10.4 us
    all_to_all x1, waiting for transfers between devices, cycles(): sums = lax.all_to_all(part, 'slab', 0, 0, tiled=True)  8.13 us
    ppermute x1, starting transfers between devices, cycles(): s = lax.ppermute(modulus[3:4], 'slab', [(i, i + 2) for i in range(n - 2)])  4.62 us
    ppermute x8, waiting for transfers between devices, swap(): return lax.ppermute(x, axis, pairs)  4.18 us
  transfers between devices with their start and end apart: 10, of which 4 were waited for; matrix products, arithmetic and copies ran while one was open for 0% of the time, Pallas kernels for 2%

profile of v4, /device:TPU:0, one launch (start us, length us, event | category | flops | bytes accessed | tf_op | source)
XLA Modules:
  0.0 71.3 jit_solution(10505675656185968561)
XLA Ops:
  0.6 0.0 copy-start.1
  0.6 0.0 copy-start
  0.6 1.0 %pad_maximum_fusion = f32[16,32,128]{2,1,0:T(8,128)S(1)} fusion(f32[4,32,128]{2,1,0:T(8,128)} %e_ref.1, f32[12,32,128]{2,1,0:T(8,128)} %bitcast.5), kind=kLoop, calls=%fused_computation | loop fusion | flops 65536 | bytes 524288 | tf_op jit(solution)/shard_map/concatenate | solution.py:434
  1.7 0.7 collective-permute-start.1
  2.4 4.4 %collective-permute-start = (f32[16,32,128]{2,1,0:T(8,128)S(1)}, f32[16,32,128]{2,1,0:T(8,128)S(1)}, u32[]{:S(2)}, u32[]{:S(2)}) collective-permute-start(f32[16,32,128]{2,1,0:T(8,128)S(1)} %pad_maximum_fusion), channel_id=1, source_target_pairs={{0,1},{1,0},{2,3},{3,2},{4,5},{5,4},{6,7},{7,6},{8,9},{9,8},{10,11... | collective-permute-start | bytes 786440 | tf_op jit(solution)/shard_map/ppermute | solution.py:424
  6.8 0.0 copy-done.1
  6.8 4.6 %collective-permute-start.2 = (f32[1,32,128]{2,1,0:T(8,128)S(1)}, f32[1,32,128]{2,1,0:T(8,128)S(1)}, u32[]{:S(2)}, u32[]{:S(2)}) collective-permute-start(f32[1,32,128]{2,1,0:T(8,128)S(1)} %slice.3), channel_id=1, source_target_pairs={{0,2},{1,3},{2,4},{3,5},{4,6},{5,7},{6,8},{7,9},{8,10},{9,11},{10,... | collective-permute-start | bytes 49160 | tf_op jit(solution)/shard_map/ppermute | solution.py:437
  11.5 0.1 pad_add_fusion.par
  11.5 1.3 %collective-permute-done.2.s_ref = f32[1,32,128]{2,1,0:T(8,128)S(1)} collective-permute-done((f32[1,32,128]{2,1,0:T(8,128)S(1)}, f32[1,32,128]{2,1,0:T(8,128)S(1)}, u32[]{:S(2)}, u32[]{:S(2)}) %collective-permute-start.2) | collective-permute-done | bytes 16416 | tf_op jit(solution)/shard_map/ppermute | solution.py:437
  12.8 0.0 collective-permute-done.1.b_ref
  12.8 0.1 collective-permute-done.a_ref
  13.0 0.0 copy-done
  13.0 1.8 %shard_map.49 = (f32[3,4,32,128]{3,2,1,0:T(8,128)S(1)}, f32[3,8,32,128]{3,2,1,0:T(8,128)S(1)}, f32[13,32,128]{2,1,0:T(8,128)S(1)}, f32[3,12,32,128]{3,2,1,0:T(8,...) custom-call(s32[4]{0:T(128)S(1)} %pad_add_fusion.par, ...), custom_call_target="tpu_custom_call" | custom-call | flops 4194304 | bytes 1048576 | tf_op jit(solution)/shard_map/pallas_call | solution.py:402
  14.8 1.8 %collective-permute-start.3 = (f32[17,32,128]{2,1,0:T(8,128)S(1)}, f32[17,32,128]{2,1,0:T(8,128)S(1)}, u32[]{:S(2)}, u32[]{:S(2)}) collective-permute-start(f32[17,32,128]{2,1,0:T(8,128)S(1)} %get-tuple-element.29), channel_id=1, source_target_pairs={{0,1},{1,0},{2,3},{3,2},{4,5},{5,4},{6,7},{7,6},{8,9},{9,8},{10,11... | collective-permute-start | bytes 835592 | tf_op jit(solution)/shard_map/ppermute | solution.py:424
  16.6 0.7 collective-permute-start.4
  17.3 6.6 %collective-permute-start.6 = (f32[18,16,128]{2,1,0:T(8,128)S(1)}, f32[18,16,128]{2,1,0:T(8,128)S(1)}, u32[]{:S(2)}, u32[]{:S(2)}) collective-permute-start(f32[18,16,128]{2,1,0:T(8,128)S(1)} %get-tuple-element.31), channel_id=1, source_target_pairs={{0,2},{63,61},{1,4},{4,1},{3,6},{6,3},{5,8},{8,5},{7,10},{10,7},{9... | collective-permute-start | bytes 442376 | tf_op jit(solution)/shard_map/ppermute | solution.py:424
  23.9 4.9 %collective-permute-start.5 = (f32[18,16,128]{2,1,0:T(8,128)S(1)}, f32[18,16,128]{2,1,0:T(8,128)S(1)}, u32[]{:S(2)}, u32[]{:S(2)}) collective-permute-start(f32[18,16,128]{2,1,0:T(8,128)S(1)} %get-tuple-element.31), channel_id=1, source_target_pairs={{0,3},{3,0},{2,5},{5,2},{4,7},{7,4},{6,9},{9,6},{8,11},{11,8},{10,... | collective-permute-start | bytes 442376 | tf_op jit(solution)/shard_map/ppermute | solution.py:424
  28.8 0.0 collective-permute-done.6.b3
  28.8 4.0 %collective-permute-done.5.a3 = f32[18,16,128]{2,1,0:T(8,128)S(1)} collective-permute-done((f32[18,16,128]{2,1,0:T(8,128)S(1)}, f32[18,16,128]{2,1,0:T(8,128)S(1)}, u32[]{:S(2)}, u32[]{:S(2)}) %collective-permute-start.5) | collective-permute-done | bytes 147488 | tf_op jit(solution)/shard_map/ppermute | solution.py:424
  32.8 0.0 collective-permute-done.3.a1
  32.8 0.0 collective-permute-done.4.b1
  32.8 4.8 %shard_map.50 = (f32[3,4,32,128]{3,2,1,0:T(8,128)S(1)}, f32[3,6,32,128]{3,2,1,0:T(8,128)S(1)}, f32[6,16,128]{2,1,0:T(8,128)S(1)}, f32[11,16,128]{2,1,0:T(8,128)S...) custom-call(s32[4]{0:T(128)S(1)} %pad_add_fusion.par, ...), custom_call_target="tpu_custom_call" | custom-call | flops 4194304 | bytes 1048576 | tf_op jit(solution)/shard_map/pallas_call | solution.py:402
  37.6 1.3 %collective-permute-start.8 = (f32[6,16,128]{2,1,0:T(8,128)S(1)}, f32[6,16,128]{2,1,0:T(8,128)S(1)}, u32[]{:S(2)}, u32[]{:S(2)}) collective-permute-start(f32[6,16,128]{2,1,0:T(8,128)S(1)} %get-tuple-element.34.own), channel_id=1, source_target_pairs={{0,1},{63,62},{2,4},{4,2},{3,5},{5,3},{6,8},{8,6},{7,9},{9,7},{10,... | collective-permute-start | bytes 147464 | tf_op jit(solution)/shard_map/ppermute | solution.py:424
  38.9 4.8 %collective-permute-start.7 = (f32[6,16,128]{2,1,0:T(8,128)S(1)}, f32[6,16,128]{2,1,0:T(8,128)S(1)}, u32[]{:S(2)}, u32[]{:S(2)}) collective-permute-start(f32[6,16,128]{2,1,0:T(8,128)S(1)} %get-tuple-element.34.own), channel_id=1, source_target_pairs={{0,2},{2,0},{1,3},{3,1},{4,6},{6,4},{5,7},{7,5},{8,10},{10,8},{9,1... | collective-permute-start | bytes 147464 | tf_op jit(solution)/shard_map/ppermute | solution.py:424
  43.7 15.6 %all-to-all-start = ((f32[64,1,128]{2,1,0:T(1,128)}), f32[64,1,128]{2,1,0:T(1,128)S(1)}, u32[]{:S(2)}, u32[]{:S(2)}) async-start(f32[64,1,128]{2,1,0:T(1,128)} %get-tuple-element.37), calls=%async_computation | async-start | bytes 65536 | tf_op jit(solution)/shard_map/all_to_all | solution.py:459
  59.3 1.4 %shard_map.52 = f32[3,2,16,64]{3,2,1,0:T(8,128)} custom-call(f32[11,16,128]{2,1,0:T(8,128)S(1)} %get-tuple-element.35.cm_ref, f32[3,10,16,128]{3,2,1,0:T(8,128)S(1)} %get-tuple-element.36.pc_ref, f32[3,2,16,128]{3,2,1,0:T(8,128)S(1)} %get-tuple-element.39.xc_ref, f32[3,8,16,128]{3,2,1,0:T(8,128)S(1)} %get-tuple-element.40.rc_ref, ...), custom_call_target="tpu_custom_call" | custom-call | flops 4194304 | bytes 1048576 | tf_op jit(solution)/shard_map/pallas_call | solution.py:402
  60.7 8.1 %all-to-all-done.sums = f32[64,1,128]{2,1,0:T(1,128)S(1)} async-done(((f32[64,1,128]{2,1,0:T(1,128)}), f32[64,1,128]{2,1,0:T(1,128)S(1)}, u32[]{:S(2)}, u32[]{:S(2)}) %all-to-all-start) | async-done | bytes 32800 | tf_op jit(solution)/shard_map/all_to_all | solution.py:459
  68.8 0.0 collective-permute-done.8.b2
  68.8 0.0 collective-permute-done.7.a2
  68.8 2.5 %shard_map.51 = (f32[3,4,32,128]{3,2,1,0:T(8,128)}, f32[2]{0:T(128)}) custom-call(s32[4]{0:T(128)S(1)} %pad_add_fusion.par, f32[3,4,32,128]{3,2,1,0:T(8,128)S(1)} %get-tuple-element.32.x_ref, f32[3,6,32,128]{3,2,1,0:T(8,128)S(1)} %get-tuple-element.33.r_ref, f32[6,16,128]{2,1,0:T(8,128)S(1)} %get-tuple-element.34.own, ...), custom_call_target="tpu_custom_call" | custom-call | flops 4194304 | bytes 1048576 | tf_op jit(solution)/shard_map/pallas_call | solution.py:402
  (1 shorter events, 0.0 us)
Async XLA Ops:
  0.6 6.1 %copy-start.1 = (f32[4,32,128]{2,1,0:T(8,128)S(1)}, f32[4,32,128]{2,1,0:T(8,128)}, u32[]{:S(2)}) copy-start(f32[4,32,128]{2,1,0:T(8,128)} %e_ref.1) | copy-start | bytes 196612
  0.6 12.3 %copy-start = (f32[3,4,32,128]{3,2,1,0:T(8,128)S(1)}, f32[3,4,32,128]{3,2,1,0:T(8,128)}, u32[]{:S(2)}) copy-start(f32[3,4,32,128]{3,2,1,0:T(8,128)} %f_ref.3) | copy-start | bytes 589828
  1.7 11.2 %collective-permute-start.1 = (f32[16,32,128]{2,1,0:T(8,128)S(1)}, f32[16,32,128]{2,1,0:T(8,128)S(1)}, u32[]{:S(2)}, u32[]{:S(2)}) collective-permute-start(f32[16,32,128]{2,1,0:T(8,128)S(1)} %pad_maximum_fusion), channel_id=1, source_target_pairs={{1,2},{2,1},{3,4},{4,3},{5,6},{6,5},{7,8},{8,7},{9,10},{10,9},{11,... | collective-permute-start | bytes 786440 | tf_op jit(solution)/shard_map/ppermute | solution.py:424
  2.4 10.6 %collective-permute-start = (f32[16,32,128]{2,1,0:T(8,128)S(1)}, f32[16,32,128]{2,1,0:T(8,128)S(1)}, u32[]{:S(2)}, u32[]{:S(2)}) collective-permute-start(f32[16,32,128]{2,1,0:T(8,128)S(1)} %pad_maximum_fusion), channel_id=1, source_target_pairs={{0,1},{1,0},{2,3},{3,2},{4,5},{5,4},{6,7},{7,6},{8,9},{9,8},{10,11... | collective-permute-start | bytes 786440 | tf_op jit(solution)/shard_map/ppermute | solution.py:424
  6.8 6.1 %collective-permute-start.2 = (f32[1,32,128]{2,1,0:T(8,128)S(1)}, f32[1,32,128]{2,1,0:T(8,128)S(1)}, u32[]{:S(2)}, u32[]{:S(2)}) collective-permute-start(f32[1,32,128]{2,1,0:T(8,128)S(1)} %slice.3), channel_id=1, source_target_pairs={{0,2},{1,3},{2,4},{3,5},{4,6},{5,7},{6,8},{7,9},{8,10},{9,11},{10,... | collective-permute-start | bytes 49160 | tf_op jit(solution)/shard_map/ppermute | solution.py:437
  14.8 18.0 %collective-permute-start.3 = (f32[17,32,128]{2,1,0:T(8,128)S(1)}, f32[17,32,128]{2,1,0:T(8,128)S(1)}, u32[]{:S(2)}, u32[]{:S(2)}) collective-permute-start(f32[17,32,128]{2,1,0:T(8,128)S(1)} %get-tuple-element.29), channel_id=1, source_target_pairs={{0,1},{1,0},{2,3},{3,2},{4,5},{5,4},{6,7},{7,6},{8,9},{9,8},{10,11... | collective-permute-start | bytes 835592 | tf_op jit(solution)/shard_map/ppermute | solution.py:424
  16.6 16.2 %collective-permute-start.4 = (f32[17,32,128]{2,1,0:T(8,128)S(1)}, f32[17,32,128]{2,1,0:T(8,128)S(1)}, u32[]{:S(2)}, u32[]{:S(2)}) collective-permute-start(f32[17,32,128]{2,1,0:T(8,128)S(1)} %get-tuple-element.30), channel_id=1, source_target_pairs={{1,2},{2,1},{3,4},{4,3},{5,6},{6,5},{7,8},{8,7},{9,10},{10,9},{11,... | collective-permute-start | bytes 835592 | tf_op jit(solution)/shard_map/ppermute | solution.py:424
  17.3 11.5 %collective-permute-start.6 = (f32[18,16,128]{2,1,0:T(8,128)S(1)}, f32[18,16,128]{2,1,0:T(8,128)S(1)}, u32[]{:S(2)}, u32[]{:S(2)}) collective-permute-start(f32[18,16,128]{2,1,0:T(8,128)S(1)} %get-tuple-element.31), channel_id=1, source_target_pairs={{0,2},{63,61},{1,4},{4,1},{3,6},{6,3},{5,8},{8,5},{7,10},{10,7},{9... | collective-permute-start | bytes 442376 | tf_op jit(solution)/shard_map/ppermute | solution.py:424
  23.9 8.9 %collective-permute-start.5 = (f32[18,16,128]{2,1,0:T(8,128)S(1)}, f32[18,16,128]{2,1,0:T(8,128)S(1)}, u32[]{:S(2)}, u32[]{:S(2)}) collective-permute-start(f32[18,16,128]{2,1,0:T(8,128)S(1)} %get-tuple-element.31), channel_id=1, source_target_pairs={{0,3},{3,0},{2,5},{5,2},{4,7},{7,4},{6,9},{9,6},{8,11},{11,8},{10,... | collective-permute-start | bytes 442376 | tf_op jit(solution)/shard_map/ppermute | solution.py:424
  37.6 31.2 %collective-permute-start.8 = (f32[6,16,128]{2,1,0:T(8,128)S(1)}, f32[6,16,128]{2,1,0:T(8,128)S(1)}, u32[]{:S(2)}, u32[]{:S(2)}) collective-permute-start(f32[6,16,128]{2,1,0:T(8,128)S(1)} %get-tuple-element.34.own), channel_id=1, source_target_pairs={{0,1},{63,62},{2,4},{4,2},{3,5},{5,3},{6,8},{8,6},{7,9},{9,7},{10,... | collective-permute-start | bytes 147464 | tf_op jit(solution)/shard_map/ppermute | solution.py:424
  38.9 29.9 %collective-permute-start.7 = (f32[6,16,128]{2,1,0:T(8,128)S(1)}, f32[6,16,128]{2,1,0:T(8,128)S(1)}, u32[]{:S(2)}, u32[]{:S(2)}) collective-permute-start(f32[6,16,128]{2,1,0:T(8,128)S(1)} %get-tuple-element.34.own), channel_id=1, source_target_pairs={{0,2},{2,0},{1,3},{3,1},{4,6},{6,4},{5,7},{7,5},{8,10},{10,8},{9,1... | collective-permute-start | bytes 147464 | tf_op jit(solution)/shard_map/ppermute | solution.py:424
  43.7 25.1 %all-to-all-start = ((f32[64,1,128]{2,1,0:T(1,128)}), f32[64,1,128]{2,1,0:T(1,128)S(1)}, u32[]{:S(2)}, u32[]{:S(2)}) async-start(f32[64,1,128]{2,1,0:T(1,128)} %get-tuple-element.37), calls=%async_computation | async-start | bytes 65536 | tf_op jit(solution)/shard_map/all_to_all | solution.py:459

commit v5 on v4

--- a/solution.py
+++ b/solution.py
@@ -146,7 +146,7 @@
 
 
 def first_kernel(
-    par, f_ref, e_ref, a_ref, b_ref, s_ref,
+    f_ref, e_ref, a_ref, b_ref, s_ref,
     x_ref, r_ref, m_ref, p_ref, cf_ref, cm_ref, send_a, send_b, far_ref,
     fe,
 ):
@@ -164,7 +164,8 @@
             m_ref[9 + z] = 0.4 * strided(up, 12 + z)
             m_ref[1 + z] = 0.4 * strided(down, 12 + z)
 
-    by_side(par[0], take, a_ref, b_ref)
+    me = lax.axis_index("slab")
+    by_side(me % 2, take, a_ref, b_ref)
     m = tiles(m_ref[...])
     p = inverse(m, 1, GAIN_F)
     r = [tiles(fe[c]) for c in range(3)]
@@ -186,7 +187,7 @@
         both = rows(pack(pair_cells(done) * 0.5, pair_cells(f[c][2:10]) * 0.5))
         cf_ref[c] = both
         far_ref[4 * c : 4 * c + 4] = both
-    for ref, q in ((send_a, par[0]), (send_b, 1 - par[0])):
+    for ref, q in ((send_a, me % 2), (send_b, 1 - me % 2)):
         for c in range(3):
             ref[4 * c : 4 * c + 4] = r_ref[c, pl.ds(4 * q, 4)]
             for j in range(2):
@@ -195,7 +196,7 @@
 
 
 def second_kernel(
-    top, par, f_ref, x_ref, r_ref, m_ref, p_ref, own, own_cm, a1, b1, a3, b3,
+    top, f_ref, x_ref, r_ref, m_ref, p_ref, own, own_cm, a1, b1, a3, b3,
     xo_ref, ro_ref, far_ref, cmo_ref, pco_ref, xc_ref, rc_ref, wc_ref, sum_ref,
     re, me, cf, cm,
 ):
@@ -222,10 +223,11 @@
         cm[12:17] = up[12:17]
         cm[0:6] = down[12:18]
 
-    by_side(par[0], near, a1, b1)
-    by_side(par[2], third, a3, b3)
-
-    @pl.when(par[3] == 2)
+    place = lax.axis_index("slab")
+    by_side(half(place, 1), near, a1, b1)
+    by_side(half(place, 3), third, a3, b3)
+
+    @pl.when(place == 2)
     def _():
         for c in range(3):
             cf[c, 0:3] = jnp.zeros((3, 16, 128), jnp.float32)
@@ -233,7 +235,7 @@
         cm[0:4] = jnp.zeros((4, 16, 128), jnp.float32)
         cm[4:6] = b3[14:16]
 
-    @pl.when(par[3] == top - 2)
+    @pl.when(place == top - 2)
     def _():
         for c in range(3):
             cf[c, 12] = b3[4 * c + 2]
@@ -336,7 +338,7 @@
 
 
 def third_kernel(
-    top, scale, par, x_ref, r_ref, own, m_ref, p_ref, cm_ref, pc_ref, sums, a2, b2, out_ref, sum_ref, cf
+    top, scale, x_ref, r_ref, own, m_ref, p_ref, cm_ref, pc_ref, sums, a2, b2, out_ref, sum_ref, cf
 ):
     for c in range(3):
         cf[c, 2:4] = own[2 * c : 2 * c + 2]
@@ -346,16 +348,17 @@
             cf[c, 4:6] = up[2 * c : 2 * c + 2]
             cf[c, 0:2] = down[2 * c : 2 * c + 2]
 
-    by_side(par[1], second, a2, b2)
+    place = lax.axis_index("slab")
+    by_side(half(place, 2), second, a2, b2)
     even = lanes((16, 128)) % 2 == 0
 
-    @pl.when(par[3] == 1)
+    @pl.when(place == 1)
     def _():
         for c in range(3):
             cf[c, 0] = jnp.zeros((16, 128), jnp.float32)
             cf[c, 1] = jnp.where(even, 0.0, b2[2 * c])
 
-    @pl.when(par[3] == top - 1)
+    @pl.when(place == top - 1)
     def _():
         for c in range(3):
             cf[c, 4] = jnp.where(even, b2[2 * c + 1], 0.0)
@@ -396,23 +399,23 @@
                 out_ref[c, z, pl.ds(t, 8, stride=4), :] = x[z, t]
 
 
-def call(kernel, outs, scratch, *args, par=None, small=(), flops=1 << 22):
-    head = () if par is None else (par,)
+def call(kernel, outs, scratch, *args, small=(), flops=1 << 22):
     places = [pltpu.SMEM if i in small else pltpu.VMEM for i in range(len(outs))]
     return pl.pallas_call(
         kernel,
         out_shape=[jax.ShapeDtypeStruct(s, jnp.float32) for s in outs],
-        in_specs=[pl.BlockSpec(memory_space=pltpu.SMEM)] * len(head)
-        + [pl.BlockSpec(memory_space=pltpu.VMEM)] * len(args),
+        in_specs=[pl.BlockSpec(memory_space=pltpu.VMEM)] * len(args),
         out_specs=[pl.BlockSpec(memory_space=place) for place in places],
         scratch_shapes=[pltpu.VMEM(s, jnp.float32) for s in scratch],
         compiler_params=pltpu.CompilerParams(vmem_limit_bytes=16 << 20),
         cost_estimate=pl.CostEstimate(flops=flops, bytes_accessed=1 << 20, transcendentals=0),
-    )(*head, *args)
+    )(*args)
 
 
 def half(i, distance):
-    return (i // distance + (distance == 3 and i % 3 == 1)) % 2
+    if distance == 3:
+        i = i + 3 * (i % 3) * (2 - i % 3)
+    return (i // distance) % 2
 
 
 def swap(x, distance, second, extra=(), axis="slab"):
@@ -425,9 +428,7 @@
 
 
 def cycles(force, modulus):
-    me = lax.axis_index("slab")
     n = lax.axis_size("slab")
-    par = jnp.stack([me % 2, (me // 2) % 2, (me // 3 + (me % 3 == 1)) % 2, me]).astype(jnp.int32)
     top = n - 1
     if half(top, 3) != 1 or half(top - 2, 3) != 1 or half(top, 2) != 1:
         raise ValueError("slab count")
@@ -442,7 +443,7 @@
             (6, 16, 128), (17, 32, 128), (17, 32, 128), (18, 16, 128),
         ],
         [(3, 12, 32, 128)],
-        force, modulus, a, b, s, par=par,
+        force, modulus, a, b, s,
     )
     got = [swap(send_a, 1, 0), swap(send_b, 1, 1)]
     got += [swap(far, 3, 0), swap(far, 3, 1, ((0, 2), (top, top - 2)))]
@@ -453,7 +454,7 @@
             (3, 2, 16, 128), (3, 8, 16, 128), (3, 8, 16, 128), (n, 1, 128),
         ],
         [(3, 16, 32, 128), (17, 32, 128), (3, 16, 16, 128), (17, 16, 128)],
-        force, x, r, m, p, cf, cm, *got, par=par,
+        force, x, r, m, p, cf, cm, *got,
     )
     got = [swap(far, 2, 0), swap(far, 2, 1, ((0, 1), (top, top - 1)))]
     sums = lax.all_to_all(part, "slab", 0, 0, tiled=True)
@@ -467,7 +468,7 @@
         functools.partial(third_kernel, top, scale),
         [(3, 4, 32, 128), (2,)],
         [(3, 6, 16, 128)],
-        x, r, far, m, p, cm, pc, sums, *got, par=par, small=(1,),
+        x, r, far, m, p, cm, pc, sums, *got, small=(1,),
     )
     return fine, coarse, total
 

time: 71.6 us -> 70.1 us (0.979)
  Pallas kernels: 10.4 us -> 8.85 us
    pallas_call x4, Pallas kernels: 10.4 us -> 8.85 us  [call(): pl.pallas_call(kernel, out_shape=[jax.ShapeDtypeStruct(s, jnp.float32) fo...]
where the time goes in v5:
time: 70.1 us; the launch traced here: 69.8 us
  starting transfers between devices  45.4 us (65%)
  waiting for transfers between devices  13.7 us (20%)
  Pallas kernels  8.85 us (13%)
  other arithmetic  1.02 us (1%)
  between operations  0.73 us (1%)
    ppermute x8, starting transfers between devices, swap(): return lax.ppermute(x, axis, pairs)  25.2 us
    all_to_all x1, starting transfers between devices, cycles(): sums = lax.all_to_all(part, 'slab', 0, 0, tiled=True)  15.6 us
    pallas_call x4, Pallas kernels, call(): pl.pallas_call(kernel, out_shape=[jax.ShapeDtypeStruct(s, jnp.float32) fo...  8.85 us
    all_to_all x1, waiting for transfers between devices, cycles(): sums = lax.all_to_all(part, 'slab', 0, 0, tiled=True)  8.13 us
    ppermute x1, starting transfers between devices, cycles(): s = lax.ppermute(modulus[3:4], 'slab', [(i, i + 2) for i in range(n - 2)])  4.62 us
    ppermute x8, waiting for transfers between devices, swap(): return lax.ppermute(x, axis, pairs)  4.18 us
    ppermute x1, waiting for transfers between devices, cycles(): s = lax.ppermute(modulus[3:4], 'slab', [(i, i + 2) for i in range(n - 2)])  1.43 us
  transfers between devices with their start and end apart: 10, of which 4 were waited for; matrix products, arithmetic and copies ran while one was open for 0% of the time, Pallas kernels for 2%

profile of v5, /device:TPU:0, one launch (start us, length us, event | category | flops | bytes accessed | tf_op | source)
XLA Modules:
  0.0 69.8 jit_solution(9458034555126216657)
XLA Ops:
  0.6 0.0 copy-start.1
  0.6 0.0 copy-start
  0.6 1.0 %pad_maximum_fusion = f32[16,32,128]{2,1,0:T(8,128)S(1)} fusion(f32[4,32,128]{2,1,0:T(8,128)} %e_ref.1, f32[12,32,128]{2,1,0:T(8,128)} %bitcast.1), kind=kLoop, calls=%fused_computation | loop fusion | flops 65536 | bytes 524288 | tf_op jit(solution)/shard_map/concatenate | solution.py:435
  1.7 0.7 collective-permute-start.1
  2.4 4.4 %collective-permute-start = (f32[16,32,128]{2,1,0:T(8,128)S(1)}, f32[16,32,128]{2,1,0:T(8,128)S(1)}, u32[]{:S(2)}, u32[]{:S(2)}) collective-permute-start(f32[16,32,128]{2,1,0:T(8,128)S(1)} %pad_maximum_fusion), channel_id=1, source_target_pairs={{0,1},{1,0},{2,3},{3,2},{4,5},{5,4},{6,7},{7,6},{8,9},{9,8},{10,11... | collective-permute-start | bytes 786440 | tf_op jit(solution)/shard_map/ppermute | solution.py:427
  6.8 0.0 copy-done.1
  6.8 4.6 %collective-permute-start.2 = (f32[1,32,128]{2,1,0:T(8,128)S(1)}, f32[1,32,128]{2,1,0:T(8,128)S(1)}, u32[]{:S(2)}, u32[]{:S(2)}) collective-permute-start(f32[1,32,128]{2,1,0:T(8,128)S(1)} %slice.3), channel_id=1, source_target_pairs={{0,2},{1,3},{2,4},{3,5},{4,6},{5,7},{6,8},{7,9},{8,10},{9,11},{10,... | collective-permute-start | bytes 49160 | tf_op jit(solution)/shard_map/ppermute | solution.py:438
  11.4 1.4 %collective-permute-done.2.s_ref = f32[1,32,128]{2,1,0:T(8,128)S(1)} collective-permute-done((f32[1,32,128]{2,1,0:T(8,128)S(1)}, f32[1,32,128]{2,1,0:T(8,128)S(1)}, u32[]{:S(2)}, u32[]{:S(2)}) %collective-permute-start.2) | collective-permute-done | bytes 16416 | tf_op jit(solution)/shard_map/ppermute | solution.py:438
  12.8 0.0 collective-permute-done.1.b_ref
  12.8 0.1 collective-permute-done.a_ref
  13.0 0.0 copy-done
  13.0 1.3 %shard_map.49 = (f32[3,4,32,128]{3,2,1,0:T(8,128)S(1)}, f32[3,8,32,128]{3,2,1,0:T(8,128)S(1)}, f32[13,32,128]{2,1,0:T(8,128)S(1)}, f32[3,12,32,128]{3,2,1,0:T(8,...) custom-call(f32[3,4,32,128]{3,2,1,0:T(8,128)S(1)} %copy-done, ...), custom_call_target="tpu_custom_call" | custom-call | flops 4194304 | bytes 1048576 | tf_op jit(solution)/shard_map/pallas_call | solution.py:404
  14.3 1.8 %collective-permute-start.3 = (f32[17,32,128]{2,1,0:T(8,128)S(1)}, f32[17,32,128]{2,1,0:T(8,128)S(1)}, u32[]{:S(2)}, u32[]{:S(2)}) collective-permute-start(f32[17,32,128]{2,1,0:T(8,128)S(1)} %get-tuple-element.29), channel_id=1, source_target_pairs={{0,1},{1,0},{2,3},{3,2},{4,5},{5,4},{6,7},{7,6},{8,9},{9,8},{10,11... | collective-permute-start | bytes 835592 | tf_op jit(solution)/shard_map/ppermute | solution.py:427
  16.1 0.7 collective-permute-start.4
  16.8 6.6 %collective-permute-start.6 = (f32[18,16,128]{2,1,0:T(8,128)S(1)}, f32[18,16,128]{2,1,0:T(8,128)S(1)}, u32[]{:S(2)}, u32[]{:S(2)}) collective-permute-start(f32[18,16,128]{2,1,0:T(8,128)S(1)} %get-tuple-element.31), channel_id=1, source_target_pairs={{0,2},{63,61},{1,4},{4,1},{3,6},{6,3},{5,8},{8,5},{7,10},{10,7},{9... | collective-permute-start | bytes 442376 | tf_op jit(solution)/shard_map/ppermute | solution.py:427
  23.4 4.9 %collective-permute-start.5 = (f32[18,16,128]{2,1,0:T(8,128)S(1)}, f32[18,16,128]{2,1,0:T(8,128)S(1)}, u32[]{:S(2)}, u32[]{:S(2)}) collective-permute-start(f32[18,16,128]{2,1,0:T(8,128)S(1)} %get-tuple-element.31), channel_id=1, source_target_pairs={{0,3},{3,0},{2,5},{5,2},{4,7},{7,4},{6,9},{9,6},{8,11},{11,8},{10,... | collective-permute-start | bytes 442376 | tf_op jit(solution)/shard_map/ppermute | solution.py:427
  28.3 0.0 collective-permute-done.6.b3
  28.3 4.0 %collective-permute-done.5.a3 = f32[18,16,128]{2,1,0:T(8,128)S(1)} collective-permute-done((f32[18,16,128]{2,1,0:T(8,128)S(1)}, f32[18,16,128]{2,1,0:T(8,128)S(1)}, u32[]{:S(2)}, u32[]{:S(2)}) %collective-permute-start.5) | collective-permute-done | bytes 147488 | tf_op jit(solution)/shard_map/ppermute | solution.py:427
  32.3 0.0 collective-permute-done.3.a1
  32.3 0.0 collective-permute-done.4.b1
  32.3 4.2 %shard_map.50 = (f32[3,4,32,128]{3,2,1,0:T(8,128)S(1)}, f32[3,6,32,128]{3,2,1,0:T(8,128)S(1)}, f32[6,16,128]{2,1,0:T(8,128)S(1)}, f32[11,16,128]{2,1,0:T(8,128)S...) custom-call(f32[3,4,32,128]{3,2,1,0:T(8,128)S(1)} %copy-done, ...), custom_call_target="tpu_custom_call" | custom-call | flops 4194304 | bytes 1048576 | tf_op jit(solution)/shard_map/pallas_call | solution.py:404
  36.6 1.3 %collective-permute-start.8 = (f32[6,16,128]{2,1,0:T(8,128)S(1)}, f32[6,16,128]{2,1,0:T(8,128)S(1)}, u32[]{:S(2)}, u32[]{:S(2)}) collective-permute-start(f32[6,16,128]{2,1,0:T(8,128)S(1)} %get-tuple-element.34.own), channel_id=1, source_target_pairs={{0,1},{63,62},{2,4},{4,2},{3,5},{5,3},{6,8},{8,6},{7,9},{9,7},{10,... | collective-permute-start | bytes 147464 | tf_op jit(solution)/shard_map/ppermute | solution.py:427
  37.9 4.8 %collective-permute-start.7 = (f32[6,16,128]{2,1,0:T(8,128)S(1)}, f32[6,16,128]{2,1,0:T(8,128)S(1)}, u32[]{:S(2)}, u32[]{:S(2)}) collective-permute-start(f32[6,16,128]{2,1,0:T(8,128)S(1)} %get-tuple-element.34.own), channel_id=1, source_target_pairs={{0,2},{2,0},{1,3},{3,1},{4,6},{6,4},{5,7},{7,5},{8,10},{10,8},{9,1... | collective-permute-start | bytes 147464 | tf_op jit(solution)/shard_map/ppermute | solution.py:427
  42.7 15.6 %all-to-all-start = ((f32[64,1,128]{2,1,0:T(1,128)}), f32[64,1,128]{2,1,0:T(1,128)S(1)}, u32[]{:S(2)}, u32[]{:S(2)}) async-start(f32[64,1,128]{2,1,0:T(1,128)} %get-tuple-element.37), calls=%async_computation | async-start | bytes 65536 | tf_op jit(solution)/shard_map/all_to_all | solution.py:460
  58.3 1.4 %shard_map.52 = f32[3,2,16,64]{3,2,1,0:T(8,128)} custom-call(f32[11,16,128]{2,1,0:T(8,128)S(1)} %get-tuple-element.35.cm_ref, f32[3,10,16,128]{3,2,1,0:T(8,128)S(1)} %get-tuple-element.36.pc_ref, f32[3,2,16,128]{3,2,1,0:T(8,128)S(1)} %get-tuple-element.39.xc_ref, f32[3,8,16,128]{3,2,1,0:T(8,128)S(1)} %get-tuple-element.40.rc_ref, ...), custom_call_target="tpu_custom_call" | custom-call | flops 4194304 | bytes 1048576 | tf_op jit(solution)/shard_map/pallas_call | solution.py:404
  59.7 8.1 %all-to-all-done.sums = f32[64,1,128]{2,1,0:T(1,128)S(1)} async-done(((f32[64,1,128]{2,1,0:T(1,128)}), f32[64,1,128]{2,1,0:T(1,128)S(1)}, u32[]{:S(2)}, u32[]{:S(2)}) %all-to-all-start) | async-done | bytes 32800 | tf_op jit(solution)/shard_map/all_to_all | solution.py:460
  67.8 0.0 collective-permute-done.8.b2
  67.8 0.0 collective-permute-done.7.a2
  67.8 2.0 %shard_map.51 = (f32[3,4,32,128]{3,2,1,0:T(8,128)}, f32[2]{0:T(128)}) custom-call(f32[3,4,32,128]{3,2,1,0:T(8,128)S(1)} %get-tuple-element.32.x_ref, f32[3,6,32,128]{3,2,1,0:T(8,128)S(1)} %get-tuple-element.33.r_ref, f32[6,16,128]{2,1,0:T(8,128)S(1)} %get-tuple-element.34.own, f32[13,32,128]{2,1,0:T(8,128)S(1)} %get-tuple-element.25.m_ref, ...), custom_call_target="tpu_custom_call" | custom-call | flops 4194304 | bytes 1048576 | tf_op jit(solution)/shard_map/pallas_call | solution.py:404
  (1 shorter events, 0.0 us)
Async XLA Ops:
  0.6 6.1 %copy-start.1 = (f32[4,32,128]{2,1,0:T(8,128)S(1)}, f32[4,32,128]{2,1,0:T(8,128)}, u32[]{:S(2)}) copy-start(f32[4,32,128]{2,1,0:T(8,128)} %e_ref.1) | copy-start | bytes 196612
  0.6 12.3 %copy-start = (f32[3,4,32,128]{3,2,1,0:T(8,128)S(1)}, f32[3,4,32,128]{3,2,1,0:T(8,128)}, u32[]{:S(2)}) copy-start(f32[3,4,32,128]{3,2,1,0:T(8,128)} %f_ref.3) | copy-start | bytes 589828
  1.7 11.2 %collective-permute-start.1 = (f32[16,32,128]{2,1,0:T(8,128)S(1)}, f32[16,32,128]{2,1,0:T(8,128)S(1)}, u32[]{:S(2)}, u32[]{:S(2)}) collective-permute-start(f32[16,32,128]{2,1,0:T(8,128)S(1)} %pad_maximum_fusion), channel_id=1, source_target_pairs={{1,2},{2,1},{3,4},{4,3},{5,6},{6,5},{7,8},{8,7},{9,10},{10,9},{11,... | collective-permute-start | bytes 786440 | tf_op jit(solution)/shard_map/ppermute | solution.py:427
  2.4 10.6 %collective-permute-start = (f32[16,32,128]{2,1,0:T(8,128)S(1)}, f32[16,32,128]{2,1,0:T(8,128)S(1)}, u32[]{:S(2)}, u32[]{:S(2)}) collective-permute-start(f32[16,32,128]{2,1,0:T(8,128)S(1)} %pad_maximum_fusion), channel_id=1, source_target_pairs={{0,1},{1,0},{2,3},{3,2},{4,5},{5,4},{6,7},{7,6},{8,9},{9,8},{10,11... | collective-permute-start | bytes 786440 | tf_op jit(solution)/shard_map/ppermute | solution.py:427
  6.8 6.1 %collective-permute-start.2 = (f32[1,32,128]{2,1,0:T(8,128)S(1)}, f32[1,32,128]{2,1,0:T(8,128)S(1)}, u32[]{:S(2)}, u32[]{:S(2)}) collective-permute-start(f32[1,32,128]{2,1,0:T(8,128)S(1)} %slice.3), channel_id=1, source_target_pairs={{0,2},{1,3},{2,4},{3,5},{4,6},{5,7},{6,8},{7,9},{8,10},{9,11},{10,... | collective-permute-start | bytes 49160 | tf_op jit(solution)/shard_map/ppermute | solution.py:438
  14.3 18.1 %collective-permute-start.3 = (f32[17,32,128]{2,1,0:T(8,128)S(1)}, f32[17,32,128]{2,1,0:T(8,128)S(1)}, u32[]{:S(2)}, u32[]{:S(2)}) collective-permute-start(f32[17,32,128]{2,1,0:T(8,128)S(1)} %get-tuple-element.29), channel_id=1, source_target_pairs={{0,1},{1,0},{2,3},{3,2},{4,5},{5,4},{6,7},{7,6},{8,9},{9,8},{10,11... | collective-permute-start | bytes 835592 | tf_op jit(solution)/shard_map/ppermute | solution.py:427
  16.1 16.2 %collective-permute-start.4 = (f32[17,32,128]{2,1,0:T(8,128)S(1)}, f32[17,32,128]{2,1,0:T(8,128)S(1)}, u32[]{:S(2)}, u32[]{:S(2)}) collective-permute-start(f32[17,32,128]{2,1,0:T(8,128)S(1)} %get-tuple-element.30), channel_id=1, source_target_pairs={{1,2},{2,1},{3,4},{4,3},{5,6},{6,5},{7,8},{8,7},{9,10},{10,9},{11,... | collective-permute-start | bytes 835592 | tf_op jit(solution)/shard_map/ppermute | solution.py:427
  16.8 11.5 %collective-permute-start.6 = (f32[18,16,128]{2,1,0:T(8,128)S(1)}, f32[18,16,128]{2,1,0:T(8,128)S(1)}, u32[]{:S(2)}, u32[]{:S(2)}) collective-permute-start(f32[18,16,128]{2,1,0:T(8,128)S(1)} %get-tuple-element.31), channel_id=1, source_target_pairs={{0,2},{63,61},{1,4},{4,1},{3,6},{6,3},{5,8},{8,5},{7,10},{10,7},{9... | collective-permute-start | bytes 442376 | tf_op jit(solution)/shard_map/ppermute | solution.py:427
  23.4 8.9 %collective-permute-start.5 = (f32[18,16,128]{2,1,0:T(8,128)S(1)}, f32[18,16,128]{2,1,0:T(8,128)S(1)}, u32[]{:S(2)}, u32[]{:S(2)}) collective-permute-start(f32[18,16,128]{2,1,0:T(8,128)S(1)} %get-tuple-element.31), channel_id=1, source_target_pairs={{0,3},{3,0},{2,5},{5,2},{4,7},{7,4},{6,9},{9,6},{8,11},{11,8},{10,... | collective-permute-start | bytes 442376 | tf_op jit(solution)/shard_map/ppermute | solution.py:427
  36.6 31.2 %collective-permute-start.8 = (f32[6,16,128]{2,1,0:T(8,128)S(1)}, f32[6,16,128]{2,1,0:T(8,128)S(1)}, u32[]{:S(2)}, u32[]{:S(2)}) collective-permute-start(f32[6,16,128]{2,1,0:T(8,128)S(1)} %get-tuple-element.34.own), channel_id=1, source_target_pairs={{0,1},{63,62},{2,4},{4,2},{3,5},{5,3},{6,8},{8,6},{7,9},{9,7},{10,... | collective-permute-start | bytes 147464 | tf_op jit(solution)/shard_map/ppermute | solution.py:427
  37.9 29.9 %collective-permute-start.7 = (f32[6,16,128]{2,1,0:T(8,128)S(1)}, f32[6,16,128]{2,1,0:T(8,128)S(1)}, u32[]{:S(2)}, u32[]{:S(2)}) collective-permute-start(f32[6,16,128]{2,1,0:T(8,128)S(1)} %get-tuple-element.34.own), channel_id=1, source_target_pairs={{0,2},{2,0},{1,3},{3,1},{4,6},{6,4},{5,7},{7,5},{8,10},{10,8},{9,1... | collective-permute-start | bytes 147464 | tf_op jit(solution)/shard_map/ppermute | solution.py:427
  42.7 25.1 %all-to-all-start = ((f32[64,1,128]{2,1,0:T(1,128)}), f32[64,1,128]{2,1,0:T(1,128)S(1)}, u32[]{:S(2)}, u32[]{:S(2)}) async-start(f32[64,1,128]{2,1,0:T(1,128)} %get-tuple-element.37), calls=%async_computation | async-start | bytes 65536 | tf_op jit(solution)/shard_map/all_to_all | solution.py:460

commit v6 on v5

--- a/solution.py
+++ b/solution.py
@@ -187,7 +187,7 @@
         both = rows(pack(pair_cells(done) * 0.5, pair_cells(f[c][2:10]) * 0.5))
         cf_ref[c] = both
         far_ref[4 * c : 4 * c + 4] = both
-    for ref, q in ((send_a, me % 2), (send_b, 1 - me % 2)):
+    for ref, q in ((send_a, 0), (send_b, 1)):
         for c in range(3):
             ref[4 * c : 4 * c + 4] = r_ref[c, pl.ds(4 * q, 4)]
             for j in range(2):
@@ -224,7 +224,16 @@
         cm[0:6] = down[12:18]
 
     place = lax.axis_index("slab")
-    by_side(half(place, 1), near, a1, b1)
+    near(a1, b1)
+
+    @pl.when(place == 0)
+    def _():
+        me[0:2] = jnp.zeros((2, 32, 128), jnp.float32)
+
+    @pl.when(place == top)
+    def _():
+        me[15:17] = jnp.zeros((2, 32, 128), jnp.float32)
+
     by_side(half(place, 3), third, a3, b3)
 
     @pl.when(place == 2)
@@ -427,6 +436,11 @@
     return lax.ppermute(x, axis, pairs)
 
 
+def shift(x, by, axis="slab"):
+    n = lax.axis_size(axis)
+    return lax.ppermute(x, axis, [(i, (i + by) % n) for i in range(n)])
+
+
 def cycles(force, modulus):
     n = lax.axis_size("slab")
     top = n - 1
@@ -445,7 +459,7 @@
         [(3, 12, 32, 128)],
         force, modulus, a, b, s,
     )
-    got = [swap(send_a, 1, 0), swap(send_b, 1, 1)]
+    got = [shift(send_b, -1), shift(send_a, 1)]
     got += [swap(far, 3, 0), swap(far, 3, 1, ((0, 2), (top, top - 2)))]
     x, r, far, cm, pc, xc, rc, wc, part = call(
         functools.partial(second_kernel, top),

time: 70.1 us -> 68.1 us (0.971)
  starting transfers between devices: 45.4 us -> 37.2 us
  waiting for transfers between devices: 13.7 us -> 20.2 us
    ppermute x8 -> x6, starting transfers between devices: 25.2 us -> 9.67 us  [swap(): return lax.ppermute(x, axis, pairs)]
    ppermute x0 -> x2, starting transfers between devices: none -> 10.6 us  [shift(): return lax.ppermute(x, axis, [(i, (i + by) % n) for i in range(n)])]
    ppermute x0 -> x2, waiting for transfers between devices: none -> 4.15 us  [shift(): return lax.ppermute(x, axis, [(i, (i + by) % n) for i in range(n)])]
    all_to_all x1, starting transfers between devices: 15.6 us -> 12.3 us  [cycles(): sums = lax.all_to_all(part, 'slab', 0, 0, tiled=True)]
    ppermute x8 -> x6, waiting for transfers between devices: 4.18 us -> 6.46 us  [swap(): return lax.ppermute(x, axis, pairs)]
  transfers between devices with their start and end apart: 10 -> 10, of which waited for: 4 -> 6; matrix products, arithmetic and copies ran while one was open for 0% -> 0% of each run, Pallas kernels for 2% -> 2%
where the time goes in v6:
time: 68.1 us; the launch traced here: 67.9 us
  starting transfers between devices  37.2 us (55%)
  waiting for transfers between devices  20.2 us (30%)
  Pallas kernels  8.78 us (13%)
  other arithmetic  1.02 us (1%)
  between operations  0.73 us (1%)
    all_to_all x1, starting transfers between devices, cycles(): sums = lax.all_to_all(part, 'slab', 0, 0, tiled=True)  12.3 us
    ppermute x2, starting transfers between devices, shift(): return lax.ppermute(x, axis, [(i, (i + by) % n) for i in range(n)])  10.6 us
    ppermute x6, starting transfers between devices, swap(): return lax.ppermute(x, axis, pairs)  9.67 us
    pallas_call x4, Pallas kernels, call(): pl.pallas_call(kernel, out_shape=[jax.ShapeDtypeStruct(s, jnp.float32) fo...  8.78 us
    all_to_all x1, waiting for transfers between devices, cycles(): sums = lax.all_to_all(part, 'slab', 0, 0, tiled=True)  8.13 us
    ppermute x6, waiting for transfers between devices, swap(): return lax.ppermute(x, axis, pairs)  6.46 us
    ppermute x1, starting transfers between devices, cycles(): s = lax.ppermute(modulus[3:4], 'slab', [(i, i + 2) for i in range(n - 2)])  4.62 us
    ppermute x2, waiting for transfers between devices, shift(): return lax.ppermute(x, axis, [(i, (i + by) % n) for i in range(n)])  4.15 us
  transfers between devices with their start and end apart: 10, of which 6 were waited for; matrix products, arithmetic and copies ran while one was open for 0% of the time, Pallas kernels for 2%

profile of v6, /device:TPU:0, one launch (start us, length us, event | category | flops | bytes accessed | tf_op | source)
XLA Modules:
  0.0 67.9 jit_solution(14015271398252769721)
XLA Ops:
  0.6 0.0 copy-start.1
  0.6 0.0 copy-start
  0.6 1.0 %pad_maximum_fusion = f32[16,32,128]{2,1,0:T(8,128)S(1)} fusion(f32[4,32,128]{2,1,0:T(8,128)} %e_ref.1, f32[12,32,128]{2,1,0:T(8,128)} %bitcast.1), kind=kLoop, calls=%fused_computation | loop fusion | flops 65536 | bytes 524288 | tf_op jit(solution)/shard_map/concatenate | solution.py:449
  1.7 0.7 collective-permute-start.1
  2.4 4.4 %collective-permute-start = (f32[16,32,128]{2,1,0:T(8,128)S(1)}, f32[16,32,128]{2,1,0:T(8,128)S(1)}, u32[]{:S(2)}, u32[]{:S(2)}) collective-permute-start(f32[16,32,128]{2,1,0:T(8,128)S(1)} %pad_maximum_fusion), channel_id=1, source_target_pairs={{0,1},{1,0},{2,3},{3,2},{4,5},{5,4},{6,7},{7,6},{8,9},{9,8},{10,11... | collective-permute-start | bytes 786440 | tf_op jit(solution)/shard_map/ppermute | solution.py:436
  6.8 0.0 copy-done.1
  6.8 4.6 %collective-permute-start.2 = (f32[1,32,128]{2,1,0:T(8,128)S(1)}, f32[1,32,128]{2,1,0:T(8,128)S(1)}, u32[]{:S(2)}, u32[]{:S(2)}) collective-permute-start(f32[1,32,128]{2,1,0:T(8,128)S(1)} %slice.3), channel_id=1, source_target_pairs={{0,2},{1,3},{2,4},{3,5},{4,6},{5,7},{6,8},{7,9},{8,10},{9,11},{10,... | collective-permute-start | bytes 49160 | tf_op jit(solution)/shard_map/ppermute | solution.py:452
  11.4 1.4 %collective-permute-done.2.s_ref = f32[1,32,128]{2,1,0:T(8,128)S(1)} collective-permute-done((f32[1,32,128]{2,1,0:T(8,128)S(1)}, f32[1,32,128]{2,1,0:T(8,128)S(1)}, u32[]{:S(2)}, u32[]{:S(2)}) %collective-permute-start.2) | collective-permute-done | bytes 16416 | tf_op jit(solution)/shard_map/ppermute | solution.py:452
  12.8 0.0 collective-permute-done.1.b_ref
  12.8 0.1 collective-permute-done.a_ref
  13.0 0.0 copy-done
  13.0 1.2 %shard_map.49 = (f32[3,4,32,128]{3,2,1,0:T(8,128)S(1)}, f32[3,8,32,128]{3,2,1,0:T(8,128)S(1)}, f32[13,32,128]{2,1,0:T(8,128)S(1)}, f32[3,12,32,128]{3,2,1,0:T(8,...) custom-call(f32[3,4,32,128]{3,2,1,0:T(8,128)S(1)} %copy-done, ...), custom_call_target="tpu_custom_call" | custom-call | flops 4194304 | bytes 1048576 | tf_op jit(solution)/shard_map/pallas_call | solution.py:413
  14.2 10.6 %collective-permute-start.3 = (f32[17,32,128]{2,1,0:T(8,128)S(1)}, f32[17,32,128]{2,1,0:T(8,128)S(1)}, u32[]{:S(2)}, u32[]{:S(2)}) collective-permute-start(f32[17,32,128]{2,1,0:T(8,128)S(1)} %get-tuple-element.29), channel_id=1, source_target_pairs={{0,63},{1,0},{2,1},{3,2},{4,3},{5,4},{6,5},{7,6},{8,7},{9,8},{10,9... | collective-permute-start | bytes 835592 | tf_op jit(solution)/shard_map/ppermute | solution.py:441
  24.8 0.0 collective-permute-start.4
  24.8 1.3 %collective-permute-start.6 = (f32[18,16,128]{2,1,0:T(8,128)S(1)}, f32[18,16,128]{2,1,0:T(8,128)S(1)}, u32[]{:S(2)}, u32[]{:S(2)}) collective-permute-start(f32[18,16,128]{2,1,0:T(8,128)S(1)} %get-tuple-element.31), channel_id=1, source_target_pairs={{0,2},{63,61},{1,4},{4,1},{3,6},{6,3},{5,8},{8,5},{7,10},{10,7},{9... | collective-permute-start | bytes 442376 | tf_op jit(solution)/shard_map/ppermute | solution.py:436
  26.1 1.9 %collective-permute-start.5 = (f32[18,16,128]{2,1,0:T(8,128)S(1)}, f32[18,16,128]{2,1,0:T(8,128)S(1)}, u32[]{:S(2)}, u32[]{:S(2)}) collective-permute-start(f32[18,16,128]{2,1,0:T(8,128)S(1)} %get-tuple-element.31), channel_id=1, source_target_pairs={{0,3},{3,0},{2,5},{5,2},{4,7},{7,4},{6,9},{9,6},{8,11},{11,8},{10,... | collective-permute-start | bytes 442376 | tf_op jit(solution)/shard_map/ppermute | solution.py:436
  28.0 4.4 %collective-permute-done.6.b3 = f32[18,16,128]{2,1,0:T(8,128)S(1)} collective-permute-done((f32[18,16,128]{2,1,0:T(8,128)S(1)}, f32[18,16,128]{2,1,0:T(8,128)S(1)}, u32[]{:S(2)}, u32[]{:S(2)}) %collective-permute-start.6) | collective-permute-done | bytes 147488 | tf_op jit(solution)/shard_map/ppermute | solution.py:436
  32.4 1.9 %collective-permute-done.5.a3 = f32[18,16,128]{2,1,0:T(8,128)S(1)} collective-permute-done((f32[18,16,128]{2,1,0:T(8,128)S(1)}, f32[18,16,128]{2,1,0:T(8,128)S(1)}, u32[]{:S(2)}, u32[]{:S(2)}) %collective-permute-start.5) | collective-permute-done | bytes 147488 | tf_op jit(solution)/shard_map/ppermute | solution.py:436
  34.3 0.0 collective-permute-done.3.a1
  34.3 4.1 %collective-permute-done.4.b1 = f32[17,32,128]{2,1,0:T(8,128)S(1)} collective-permute-done((f32[17,32,128]{2,1,0:T(8,128)S(1)}, f32[17,32,128]{2,1,0:T(8,128)S(1)}, u32[]{:S(2)}, u32[]{:S(2)}) %collective-permute-start.4) | collective-permute-done | bytes 278560 | tf_op jit(solution)/shard_map/ppermute | solution.py:441
  38.5 4.2 %shard_map.50 = (f32[3,4,32,128]{3,2,1,0:T(8,128)S(1)}, f32[3,6,32,128]{3,2,1,0:T(8,128)S(1)}, f32[6,16,128]{2,1,0:T(8,128)S(1)}, f32[11,16,128]{2,1,0:T(8,128)S...) custom-call(f32[3,4,32,128]{3,2,1,0:T(8,128)S(1)} %copy-done, ...), custom_call_target="tpu_custom_call" | custom-call | flops 4194304 | bytes 1048576 | tf_op jit(solution)/shard_map/pallas_call | solution.py:413
  42.7 1.3 %collective-permute-start.8 = (f32[6,16,128]{2,1,0:T(8,128)S(1)}, f32[6,16,128]{2,1,0:T(8,128)S(1)}, u32[]{:S(2)}, u32[]{:S(2)}) collective-permute-start(f32[6,16,128]{2,1,0:T(8,128)S(1)} %get-tuple-element.34.own), channel_id=1, source_target_pairs={{0,1},{63,62},{2,4},{4,2},{3,5},{5,3},{6,8},{8,6},{7,9},{9,7},{10,... | collective-permute-start | bytes 147464 | tf_op jit(solution)/shard_map/ppermute | solution.py:436
  44.0 0.1 collective-permute-start.7
  44.1 12.3 %all-to-all-start = ((f32[64,1,128]{2,1,0:T(1,128)}), f32[64,1,128]{2,1,0:T(1,128)S(1)}, u32[]{:S(2)}, u32[]{:S(2)}) async-start(f32[64,1,128]{2,1,0:T(1,128)} %get-tuple-element.37), calls=%async_computation | async-start | bytes 65536 | tf_op jit(solution)/shard_map/all_to_all | solution.py:474
  56.4 1.4 %shard_map.52 = f32[3,2,16,64]{3,2,1,0:T(8,128)} custom-call(f32[11,16,128]{2,1,0:T(8,128)S(1)} %get-tuple-element.35.cm_ref, f32[3,10,16,128]{3,2,1,0:T(8,128)S(1)} %get-tuple-element.36.pc_ref, f32[3,2,16,128]{3,2,1,0:T(8,128)S(1)} %get-tuple-element.39.xc_ref, f32[3,8,16,128]{3,2,1,0:T(8,128)S(1)} %get-tuple-element.40.rc_ref, ...), custom_call_target="tpu_custom_call" | custom-call | flops 4194304 | bytes 1048576 | tf_op jit(solution)/shard_map/pallas_call | solution.py:413
  57.8 8.1 %all-to-all-done.sums = f32[64,1,128]{2,1,0:T(1,128)S(1)} async-done(((f32[64,1,128]{2,1,0:T(1,128)}), f32[64,1,128]{2,1,0:T(1,128)S(1)}, u32[]{:S(2)}, u32[]{:S(2)}) %all-to-all-start) | async-done | bytes 32800 | tf_op jit(solution)/shard_map/all_to_all | solution.py:474
  65.9 0.0 collective-permute-done.8.b2
  65.9 0.0 collective-permute-done.7.a2
  65.9 2.0 %shard_map.51 = (f32[3,4,32,128]{3,2,1,0:T(8,128)}, f32[2]{0:T(128)}) custom-call(f32[3,4,32,128]{3,2,1,0:T(8,128)S(1)} %get-tuple-element.32.x_ref, f32[3,6,32,128]{3,2,1,0:T(8,128)S(1)} %get-tuple-element.33.r_ref, f32[6,16,128]{2,1,0:T(8,128)S(1)} %get-tuple-element.34.own, f32[13,32,128]{2,1,0:T(8,128)S(1)} %get-tuple-element.25.m_ref, ...), custom_call_target="tpu_custom_call" | custom-call | flops 4194304 | bytes 1048576 | tf_op jit(solution)/shard_map/pallas_call | solution.py:413
  (1 shorter events, 0.0 us)
Async XLA Ops:
  0.6 6.1 %copy-start.1 = (f32[4,32,128]{2,1,0:T(8,128)S(1)}, f32[4,32,128]{2,1,0:T(8,128)}, u32[]{:S(2)}) copy-start(f32[4,32,128]{2,1,0:T(8,128)} %e_ref.1) | copy-start | bytes 196612
  0.6 12.3 %copy-start = (f32[3,4,32,128]{3,2,1,0:T(8,128)S(1)}, f32[3,4,32,128]{3,2,1,0:T(8,128)}, u32[]{:S(2)}) copy-start(f32[3,4,32,128]{3,2,1,0:T(8,128)} %f_ref.3) | copy-start | bytes 589828
  1.7 11.2 %collective-permute-start.1 = (f32[16,32,128]{2,1,0:T(8,128)S(1)}, f32[16,32,128]{2,1,0:T(8,128)S(1)}, u32[]{:S(2)}, u32[]{:S(2)}) collective-permute-start(f32[16,32,128]{2,1,0:T(8,128)S(1)} %pad_maximum_fusion), channel_id=1, source_target_pairs={{1,2},{2,1},{3,4},{4,3},{5,6},{6,5},{7,8},{8,7},{9,10},{10,9},{11,... | collective-permute-start | bytes 786440 | tf_op jit(solution)/shard_map/ppermute | solution.py:436
  2.4 10.6 %collective-permute-start = (f32[16,32,128]{2,1,0:T(8,128)S(1)}, f32[16,32,128]{2,1,0:T(8,128)S(1)}, u32[]{:S(2)}, u32[]{:S(2)}) collective-permute-start(f32[16,32,128]{2,1,0:T(8,128)S(1)} %pad_maximum_fusion), channel_id=1, source_target_pairs={{0,1},{1,0},{2,3},{3,2},{4,5},{5,4},{6,7},{7,6},{8,9},{9,8},{10,11... | collective-permute-start | bytes 786440 | tf_op jit(solution)/shard_map/ppermute | solution.py:436
  6.8 6.1 %collective-permute-start.2 = (f32[1,32,128]{2,1,0:T(8,128)S(1)}, f32[1,32,128]{2,1,0:T(8,128)S(1)}, u32[]{:S(2)}, u32[]{:S(2)}) collective-permute-start(f32[1,32,128]{2,1,0:T(8,128)S(1)} %slice.3), channel_id=1, source_target_pairs={{0,2},{1,3},{2,4},{3,5},{4,6},{5,7},{6,8},{7,9},{8,10},{9,11},{10,... | collective-permute-start | bytes 49160 | tf_op jit(solution)/shard_map/ppermute | solution.py:452
  14.2 20.1 %collective-permute-start.3 = (f32[17,32,128]{2,1,0:T(8,128)S(1)}, f32[17,32,128]{2,1,0:T(8,128)S(1)}, u32[]{:S(2)}, u32[]{:S(2)}) collective-permute-start(f32[17,32,128]{2,1,0:T(8,128)S(1)} %get-tuple-element.29), channel_id=1, source_target_pairs={{0,63},{1,0},{2,1},{3,2},{4,3},{5,4},{6,5},{7,6},{8,7},{9,8},{10,9... | collective-permute-start | bytes 835592 | tf_op jit(solution)/shard_map/ppermute | solution.py:441
  24.8 13.7 %collective-permute-start.4 = (f32[17,32,128]{2,1,0:T(8,128)S(1)}, f32[17,32,128]{2,1,0:T(8,128)S(1)}, u32[]{:S(2)}, u32[]{:S(2)}) collective-permute-start(f32[17,32,128]{2,1,0:T(8,128)S(1)} %get-tuple-element.30), channel_id=1, source_target_pairs={{0,1},{1,2},{2,3},{3,4},{4,5},{5,6},{6,7},{7,8},{8,9},{9,10},{10,1... | collective-permute-start | bytes 835592 | tf_op jit(solution)/shard_map/ppermute | solution.py:441
  24.8 7.6 %collective-permute-start.6 = (f32[18,16,128]{2,1,0:T(8,128)S(1)}, f32[18,16,128]{2,1,0:T(8,128)S(1)}, u32[]{:S(2)}, u32[]{:S(2)}) collective-permute-start(f32[18,16,128]{2,1,0:T(8,128)S(1)} %get-tuple-element.31), channel_id=1, source_target_pairs={{0,2},{63,61},{1,4},{4,1},{3,6},{6,3},{5,8},{8,5},{7,10},{10,7},{9... | collective-permute-start | bytes 442376 | tf_op jit(solution)/shard_map/ppermute | solution.py:436
  26.1 8.2 %collective-permute-start.5 = (f32[18,16,128]{2,1,0:T(8,128)S(1)}, f32[18,16,128]{2,1,0:T(8,128)S(1)}, u32[]{:S(2)}, u32[]{:S(2)}) collective-permute-start(f32[18,16,128]{2,1,0:T(8,128)S(1)} %get-tuple-element.31), channel_id=1, source_target_pairs={{0,3},{3,0},{2,5},{5,2},{4,7},{7,4},{6,9},{9,6},{8,11},{11,8},{10,... | collective-permute-start | bytes 442376 | tf_op jit(solution)/shard_map/ppermute | solution.py:436
  42.7 23.2 %collective-permute-start.8 = (f32[6,16,128]{2,1,0:T(8,128)S(1)}, f32[6,16,128]{2,1,0:T(8,128)S(1)}, u32[]{:S(2)}, u32[]{:S(2)}) collective-permute-start(f32[6,16,128]{2,1,0:T(8,128)S(1)} %get-tuple-element.34.own), channel_id=1, source_target_pairs={{0,1},{63,62},{2,4},{4,2},{3,5},{5,3},{6,8},{8,6},{7,9},{9,7},{10,... | collective-permute-start | bytes 147464 | tf_op jit(solution)/shard_map/ppermute | solution.py:436
  44.0 21.9 %collective-permute-start.7 = (f32[6,16,128]{2,1,0:T(8,128)S(1)}, f32[6,16,128]{2,1,0:T(8,128)S(1)}, u32[]{:S(2)}, u32[]{:S(2)}) collective-permute-start(f32[6,16,128]{2,1,0:T(8,128)S(1)} %get-tuple-element.34.own), channel_id=1, source_target_pairs={{0,2},{2,0},{1,3},{3,1},{4,6},{6,4},{5,7},{7,5},{8,10},{10,8},{9,1... | collective-permute-start | bytes 147464 | tf_op jit(solution)/shard_map/ppermute | solution.py:436
  44.1 21.8 %all-to-all-start = ((f32[64,1,128]{2,1,0:T(1,128)}), f32[64,1,128]{2,1,0:T(1,128)S(1)}, u32[]{:S(2)}, u32[]{:S(2)}) async-start(f32[64,1,128]{2,1,0:T(1,128)} %get-tuple-element.37), calls=%async_computation | async-start | bytes 65536 | tf_op jit(solution)/shard_map/all_to_all | solution.py:474

commit v7 on v6

--- a/solution.py
+++ b/solution.py
@@ -146,7 +146,7 @@
 
 
 def first_kernel(
-    f_ref, e_ref, a_ref, b_ref, s_ref,
+    top, f_ref, e_ref, a_ref, b_ref, s_ref,
     x_ref, r_ref, m_ref, p_ref, cf_ref, cm_ref, send_a, send_b, far_ref,
     fe,
 ):
@@ -165,7 +165,16 @@
             m_ref[1 + z] = 0.4 * strided(down, 12 + z)
 
     me = lax.axis_index("slab")
-    by_side(me % 2, take, a_ref, b_ref)
+    take(a_ref, b_ref)
+
+    @pl.when(me == 0)
+    def _():
+        m_ref[0:5] = jnp.zeros((5, 32, 128), jnp.float32)
+
+    @pl.when(me == top)
+    def _():
+        m_ref[9:13] = jnp.zeros((4, 32, 128), jnp.float32)
+
     m = tiles(m_ref[...])
     p = inverse(m, 1, GAIN_F)
     r = [tiles(fe[c]) for c in range(3)]
@@ -447,11 +456,11 @@
     if half(top, 3) != 1 or half(top - 2, 3) != 1 or half(top, 2) != 1:
         raise ValueError("slab count")
     block = jnp.concatenate([force.reshape(12, 32, 128), modulus], 0)
-    a = swap(block, 1, 0)
-    b = swap(block, 1, 1)
+    a = shift(block, -1)
+    b = shift(block, 1)
     s = lax.ppermute(modulus[3:4], "slab", [(i, i + 2) for i in range(n - 2)])
     x, r, m, p, cf, cm, send_a, send_b, far = call(
-        first_kernel,
+        functools.partial(first_kernel, top),
         [
             (3, 4, 32, 128), (3, 8, 32, 128), (13, 32, 128), (3, 12, 32, 128), (3, 4, 16, 128),
             (6, 16, 128), (17, 32, 128), (17, 32, 128), (18, 16, 128),

time: 68.1 us -> 67.4 us (0.990)
  starting transfers between devices: 37.2 us -> 32.5 us
  waiting for transfers between devices: 20.2 us -> 24.1 us
    ppermute x2 -> x4, starting transfers between devices: 10.6 us -> 16.3 us  [shift(): return lax.ppermute(x, axis, [(i, (i + by) % n) for i in range(n)])]
    ppermute x6 -> x4, starting transfers between devices: 9.67 us -> 4.58 us  [swap(): return lax.ppermute(x, axis, pairs)]
    ppermute x2 -> x4, waiting for transfers between devices: 4.15 us -> 8.23 us  [shift(): return lax.ppermute(x, axis, [(i, (i + by) % n) for i in range(n)])]
    ppermute x1, starting transfers between devices: 4.62 us -> 1.28 us  [cycles(): s = lax.ppermute(modulus[3:4], 'slab', [(i, i + 2) for i in range(n - 2)])]
    all_to_all x1, starting transfers between devices: 12.3 us -> 10.4 us  [cycles(): sums = lax.all_to_all(part, 'slab', 0, 0, tiled=True)]
    ppermute x6 -> x4, waiting for transfers between devices: 6.46 us -> 6.32 us  [swap(): return lax.ppermute(x, axis, pairs)]
where the time goes in v7:
time: 67.4 us; the launch traced here: 67.2 us
  starting transfers between devices  32.5 us (48%)
  waiting for transfers between devices  24.1 us (36%)
  Pallas kernels  8.78 us (13%)
  other arithmetic  1.02 us (2%)
  between operations  0.72 us (1%)
    ppermute x4, starting transfers between devices, shift(): return lax.ppermute(x, axis, [(i, (i + by) % n) for i in range(n)])  16.3 us
    all_to_all x1, starting transfers between devices, cycles(): sums = lax.all_to_all(part, 'slab', 0, 0, tiled=True)  10.4 us
    pallas_call x4, Pallas kernels, call(): pl.pallas_call(kernel, out_shape=[jax.ShapeDtypeStruct(s, jnp.float32) fo...  8.78 us
    ppermute x4, waiting for transfers between devices, shift(): return lax.ppermute(x, axis, [(i, (i + by) % n) for i in range(n)])  8.23 us
    all_to_all x1, waiting for transfers between devices, cycles(): sums = lax.all_to_all(part, 'slab', 0, 0, tiled=True)  8.13 us
    ppermute x4, waiting for transfers between devices, swap(): return lax.ppermute(x, axis, pairs)  6.32 us
    ppermute x4, starting transfers between devices, swap(): return lax.ppermute(x, axis, pairs)  4.58 us
    ppermute x1, waiting for transfers between devices, cycles(): s = lax.ppermute(modulus[3:4], 'slab', [(i, i + 2) for i in range(n - 2)])  1.43 us
  transfers between devices with their start and end apart: 10, of which 6 were waited for; matrix products, arithmetic and copies ran while one was open for 0% of the time, Pallas kernels for 2%

profile of v7, /device:TPU:0, one launch (start us, length us, event | category | flops | bytes accessed | tf_op | source)
XLA Modules:
  0.0 67.2 jit_solution(15281450445238259212)
XLA Ops:
  0.6 0.0 copy-start.1
  0.6 0.0 copy-start
  0.6 1.0 %pad_maximum_fusion = f32[16,32,128]{2,1,0:T(8,128)S(1)} fusion(f32[4,32,128]{2,1,0:T(8,128)} %e_ref.1, f32[12,32,128]{2,1,0:T(8,128)} %bitcast.1), kind=kLoop, calls=%fused_computation | loop fusion | flops 65536 | bytes 524288 | tf_op jit(solution)/shard_map/concatenate | solution.py:458
  1.7 1.7 %collective-permute-start.1 = (f32[16,32,128]{2,1,0:T(8,128)S(1)}, f32[16,32,128]{2,1,0:T(8,128)S(1)}, u32[]{:S(2)}, u32[]{:S(2)}) collective-permute-start(f32[16,32,128]{2,1,0:T(8,128)S(1)} %pad_maximum_fusion), channel_id=1, source_target_pairs={{0,1},{1,2},{2,3},{3,4},{4,5},{5,6},{6,7},{7,8},{8,9},{9,10},{10,1... | collective-permute-start | bytes 786440 | tf_op jit(solution)/shard_map/ppermute | solution.py:450
  3.3 7.3 %collective-permute-start = (f32[16,32,128]{2,1,0:T(8,128)S(1)}, f32[16,32,128]{2,1,0:T(8,128)S(1)}, u32[]{:S(2)}, u32[]{:S(2)}) collective-permute-start(f32[16,32,128]{2,1,0:T(8,128)S(1)} %pad_maximum_fusion), channel_id=1, source_target_pairs={{0,63},{1,0},{2,1},{3,2},{4,3},{5,4},{6,5},{7,6},{8,7},{9,8},{10,9... | collective-permute-start | bytes 786440 | tf_op jit(solution)/shard_map/ppermute | solution.py:450
  10.6 0.0 copy-done.1
  10.6 1.3 %collective-permute-start.2 = (f32[1,32,128]{2,1,0:T(8,128)S(1)}, f32[1,32,128]{2,1,0:T(8,128)S(1)}, u32[]{:S(2)}, u32[]{:S(2)}) collective-permute-start(f32[1,32,128]{2,1,0:T(8,128)S(1)} %slice.3), channel_id=1, source_target_pairs={{0,2},{1,3},{2,4},{3,5},{4,6},{5,7},{6,8},{7,9},{8,10},{9,11},{10,... | collective-permute-start | bytes 49160 | tf_op jit(solution)/shard_map/ppermute | solution.py:461
  11.9 1.4 %collective-permute-done.2.s_ref = f32[1,32,128]{2,1,0:T(8,128)S(1)} collective-permute-done((f32[1,32,128]{2,1,0:T(8,128)S(1)}, f32[1,32,128]{2,1,0:T(8,128)S(1)}, u32[]{:S(2)}, u32[]{:S(2)}) %collective-permute-start.2) | collective-permute-done | bytes 16416 | tf_op jit(solution)/shard_map/ppermute | solution.py:461
  13.3 3.5 %collective-permute-done.1.b_ref = f32[16,32,128]{2,1,0:T(8,128)S(1)} collective-permute-done((f32[16,32,128]{2,1,0:T(8,128)S(1)}, f32[16,32,128]{2,1,0:T(8,128)S(1)}, u32[]{:S(2)}, u32[]{:S(2)}) %collective-permute-start.1) | collective-permute-done | bytes 262176 | tf_op jit(solution)/shard_map/ppermute | solution.py:450
  16.8 0.0 collective-permute-done.a_ref
  16.8 0.0 copy-done
  16.8 1.2 %shard_map.49 = (f32[3,4,32,128]{3,2,1,0:T(8,128)S(1)}, f32[3,8,32,128]{3,2,1,0:T(8,128)S(1)}, f32[13,32,128]{2,1,0:T(8,128)S(1)}, f32[3,12,32,128]{3,2,1,0:T(8,...) custom-call(f32[3,4,32,128]{3,2,1,0:T(8,128)S(1)} %copy-done, ...), custom_call_target="tpu_custom_call" | custom-call | flops 4194304 | bytes 1048576 | tf_op jit(solution)/shard_map/pallas_call | solution.py:422
  18.1 7.3 %collective-permute-start.3 = (f32[17,32,128]{2,1,0:T(8,128)S(1)}, f32[17,32,128]{2,1,0:T(8,128)S(1)}, u32[]{:S(2)}, u32[]{:S(2)}) collective-permute-start(f32[17,32,128]{2,1,0:T(8,128)S(1)} %get-tuple-element.29), channel_id=1, source_target_pairs={{0,63},{1,0},{2,1},{3,2},{4,3},{5,4},{6,5},{7,6},{8,7},{9,8},{10,9... | collective-permute-start | bytes 835592 | tf_op jit(solution)/shard_map/ppermute | solution.py:450
  25.4 0.0 collective-permute-start.4
  25.4 1.3 %collective-permute-start.6 = (f32[18,16,128]{2,1,0:T(8,128)S(1)}, f32[18,16,128]{2,1,0:T(8,128)S(1)}, u32[]{:S(2)}, u32[]{:S(2)}) collective-permute-start(f32[18,16,128]{2,1,0:T(8,128)S(1)} %get-tuple-element.31), channel_id=1, source_target_pairs={{0,2},{63,61},{1,4},{4,1},{3,6},{6,3},{5,8},{8,5},{7,10},{10,7},{9... | collective-permute-start | bytes 442376 | tf_op jit(solution)/shard_map/ppermute | solution.py:445
  26.7 1.9 %collective-permute-start.5 = (f32[18,16,128]{2,1,0:T(8,128)S(1)}, f32[18,16,128]{2,1,0:T(8,128)S(1)}, u32[]{:S(2)}, u32[]{:S(2)}) collective-permute-start(f32[18,16,128]{2,1,0:T(8,128)S(1)} %get-tuple-element.31), channel_id=1, source_target_pairs={{0,3},{3,0},{2,5},{5,2},{4,7},{7,4},{6,9},{9,6},{8,11},{11,8},{10,... | collective-permute-start | bytes 442376 | tf_op jit(solution)/shard_map/ppermute | solution.py:445
  28.6 5.0 %collective-permute-done.6.b3 = f32[18,16,128]{2,1,0:T(8,128)S(1)} collective-permute-done((f32[18,16,128]{2,1,0:T(8,128)S(1)}, f32[18,16,128]{2,1,0:T(8,128)S(1)}, u32[]{:S(2)}, u32[]{:S(2)}) %collective-permute-start.6) | collective-permute-done | bytes 147488 | tf_op jit(solution)/shard_map/ppermute | solution.py:445
  33.6 1.3 %collective-permute-done.5.a3 = f32[18,16,128]{2,1,0:T(8,128)S(1)} collective-permute-done((f32[18,16,128]{2,1,0:T(8,128)S(1)}, f32[18,16,128]{2,1,0:T(8,128)S(1)}, u32[]{:S(2)}, u32[]{:S(2)}) %collective-permute-start.5) | collective-permute-done | bytes 147488 | tf_op jit(solution)/shard_map/ppermute | solution.py:445
  34.9 0.0 collective-permute-done.3.a1
  34.9 4.7 %collective-permute-done.4.b1 = f32[17,32,128]{2,1,0:T(8,128)S(1)} collective-permute-done((f32[17,32,128]{2,1,0:T(8,128)S(1)}, f32[17,32,128]{2,1,0:T(8,128)S(1)}, u32[]{:S(2)}, u32[]{:S(2)}) %collective-permute-start.4) | collective-permute-done | bytes 278560 | tf_op jit(solution)/shard_map/ppermute | solution.py:450
  39.7 4.2 %shard_map.50 = (f32[3,4,32,128]{3,2,1,0:T(8,128)S(1)}, f32[3,6,32,128]{3,2,1,0:T(8,128)S(1)}, f32[6,16,128]{2,1,0:T(8,128)S(1)}, f32[11,16,128]{2,1,0:T(8,128)S...) custom-call(f32[3,4,32,128]{3,2,1,0:T(8,128)S(1)} %copy-done, ...), custom_call_target="tpu_custom_call" | custom-call | flops 4194304 | bytes 1048576 | tf_op jit(solution)/shard_map/pallas_call | solution.py:422
  43.9 1.3 %collective-permute-start.8 = (f32[6,16,128]{2,1,0:T(8,128)S(1)}, f32[6,16,128]{2,1,0:T(8,128)S(1)}, u32[]{:S(2)}, u32[]{:S(2)}) collective-permute-start(f32[6,16,128]{2,1,0:T(8,128)S(1)} %get-tuple-element.34.own), channel_id=1, source_target_pairs={{0,1},{63,62},{2,4},{4,2},{3,5},{5,3},{6,8},{8,6},{7,9},{9,7},{10,... | collective-permute-start | bytes 147464 | tf_op jit(solution)/shard_map/ppermute | solution.py:445
  45.2 0.1 collective-permute-start.7
  45.3 10.4 %all-to-all-start = ((f32[64,1,128]{2,1,0:T(1,128)}), f32[64,1,128]{2,1,0:T(1,128)S(1)}, u32[]{:S(2)}, u32[]{:S(2)}) async-start(f32[64,1,128]{2,1,0:T(1,128)} %get-tuple-element.37), calls=%async_computation | async-start | bytes 65536 | tf_op jit(solution)/shard_map/all_to_all | solution.py:483
  55.7 1.4 %shard_map.52 = f32[3,2,16,64]{3,2,1,0:T(8,128)} custom-call(f32[11,16,128]{2,1,0:T(8,128)S(1)} %get-tuple-element.35.cm_ref, f32[3,10,16,128]{3,2,1,0:T(8,128)S(1)} %get-tuple-element.36.pc_ref, f32[3,2,16,128]{3,2,1,0:T(8,128)S(1)} %get-tuple-element.39.xc_ref, f32[3,8,16,128]{3,2,1,0:T(8,128)S(1)} %get-tuple-element.40.rc_ref, ...), custom_call_target="tpu_custom_call" | custom-call | flops 4194304 | bytes 1048576 | tf_op jit(solution)/shard_map/pallas_call | solution.py:422
  57.1 8.1 %all-to-all-done.sums = f32[64,1,128]{2,1,0:T(1,128)S(1)} async-done(((f32[64,1,128]{2,1,0:T(1,128)}), f32[64,1,128]{2,1,0:T(1,128)S(1)}, u32[]{:S(2)}, u32[]{:S(2)}) %all-to-all-start) | async-done | bytes 32800 | tf_op jit(solution)/shard_map/all_to_all | solution.py:483
  65.2 0.0 collective-permute-done.8.b2
  65.2 0.0 collective-permute-done.7.a2
  65.2 2.0 %shard_map.51 = (f32[3,4,32,128]{3,2,1,0:T(8,128)}, f32[2]{0:T(128)}) custom-call(f32[3,4,32,128]{3,2,1,0:T(8,128)S(1)} %get-tuple-element.32.x_ref, f32[3,6,32,128]{3,2,1,0:T(8,128)S(1)} %get-tuple-element.33.r_ref, f32[6,16,128]{2,1,0:T(8,128)S(1)} %get-tuple-element.34.own, f32[13,32,128]{2,1,0:T(8,128)S(1)} %get-tuple-element.25.m_ref, ...), custom_call_target="tpu_custom_call" | custom-call | flops 4194304 | bytes 1048576 | tf_op jit(solution)/shard_map/pallas_call | solution.py:422
  (1 shorter events, 0.0 us)
Async XLA Ops:
  0.6 10.0 %copy-start.1 = (f32[4,32,128]{2,1,0:T(8,128)S(1)}, f32[4,32,128]{2,1,0:T(8,128)}, u32[]{:S(2)}) copy-start(f32[4,32,128]{2,1,0:T(8,128)} %e_ref.1) | copy-start | bytes 196612
  0.6 16.2 %copy-start = (f32[3,4,32,128]{3,2,1,0:T(8,128)S(1)}, f32[3,4,32,128]{3,2,1,0:T(8,128)}, u32[]{:S(2)}) copy-start(f32[3,4,32,128]{3,2,1,0:T(8,128)} %f_ref.3) | copy-start | bytes 589828
  1.7 15.2 %collective-permute-start.1 = (f32[16,32,128]{2,1,0:T(8,128)S(1)}, f32[16,32,128]{2,1,0:T(8,128)S(1)}, u32[]{:S(2)}, u32[]{:S(2)}) collective-permute-start(f32[16,32,128]{2,1,0:T(8,128)S(1)} %pad_maximum_fusion), channel_id=1, source_target_pairs={{0,1},{1,2},{2,3},{3,4},{4,5},{5,6},{6,7},{7,8},{8,9},{9,10},{10,1... | collective-permute-start | bytes 786440 | tf_op jit(solution)/shard_map/ppermute | solution.py:450
  3.3 13.5 %collective-permute-start = (f32[16,32,128]{2,1,0:T(8,128)S(1)}, f32[16,32,128]{2,1,0:T(8,128)S(1)}, u32[]{:S(2)}, u32[]{:S(2)}) collective-permute-start(f32[16,32,128]{2,1,0:T(8,128)S(1)} %pad_maximum_fusion), channel_id=1, source_target_pairs={{0,63},{1,0},{2,1},{3,2},{4,3},{5,4},{6,5},{7,6},{8,7},{9,8},{10,9... | collective-permute-start | bytes 786440 | tf_op jit(solution)/shard_map/ppermute | solution.py:450
  10.6 2.7 %collective-permute-start.2 = (f32[1,32,128]{2,1,0:T(8,128)S(1)}, f32[1,32,128]{2,1,0:T(8,128)S(1)}, u32[]{:S(2)}, u32[]{:S(2)}) collective-permute-start(f32[1,32,128]{2,1,0:T(8,128)S(1)} %slice.3), channel_id=1, source_target_pairs={{0,2},{1,3},{2,4},{3,5},{4,6},{5,7},{6,8},{7,9},{8,10},{9,11},{10,... | collective-permute-start | bytes 49160 | tf_op jit(solution)/shard_map/ppermute | solution.py:461
  18.1 16.9 %collective-permute-start.3 = (f32[17,32,128]{2,1,0:T(8,128)S(1)}, f32[17,32,128]{2,1,0:T(8,128)S(1)}, u32[]{:S(2)}, u32[]{:S(2)}) collective-permute-start(f32[17,32,128]{2,1,0:T(8,128)S(1)} %get-tuple-element.29), channel_id=1, source_target_pairs={{0,63},{1,0},{2,1},{3,2},{4,3},{5,4},{6,5},{7,6},{8,7},{9,8},{10,9... | collective-permute-start | bytes 835592 | tf_op jit(solution)/shard_map/ppermute | solution.py:450
  25.4 14.3 %collective-permute-start.4 = (f32[17,32,128]{2,1,0:T(8,128)S(1)}, f32[17,32,128]{2,1,0:T(8,128)S(1)}, u32[]{:S(2)}, u32[]{:S(2)}) collective-permute-start(f32[17,32,128]{2,1,0:T(8,128)S(1)} %get-tuple-element.30), channel_id=1, source_target_pairs={{0,1},{1,2},{2,3},{3,4},{4,5},{5,6},{6,7},{7,8},{8,9},{9,10},{10,1... | collective-permute-start | bytes 835592 | tf_op jit(solution)/shard_map/ppermute | solution.py:450
  25.4 8.2 %collective-permute-start.6 = (f32[18,16,128]{2,1,0:T(8,128)S(1)}, f32[18,16,128]{2,1,0:T(8,128)S(1)}, u32[]{:S(2)}, u32[]{:S(2)}) collective-permute-start(f32[18,16,128]{2,1,0:T(8,128)S(1)} %get-tuple-element.31), channel_id=1, source_target_pairs={{0,2},{63,61},{1,4},{4,1},{3,6},{6,3},{5,8},{8,5},{7,10},{10,7},{9... | collective-permute-start | bytes 442376 | tf_op jit(solution)/shard_map/ppermute | solution.py:445
  26.7 8.2 %collective-permute-start.5 = (f32[18,16,128]{2,1,0:T(8,128)S(1)}, f32[18,16,128]{2,1,0:T(8,128)S(1)}, u32[]{:S(2)}, u32[]{:S(2)}) collective-permute-start(f32[18,16,128]{2,1,0:T(8,128)S(1)} %get-tuple-element.31), channel_id=1, source_target_pairs={{0,3},{3,0},{2,5},{5,2},{4,7},{7,4},{6,9},{9,6},{8,11},{11,8},{10,... | collective-permute-start | bytes 442376 | tf_op jit(solution)/shard_map/ppermute | solution.py:445
  43.9 21.3 %collective-permute-start.8 = (f32[6,16,128]{2,1,0:T(8,128)S(1)}, f32[6,16,128]{2,1,0:T(8,128)S(1)}, u32[]{:S(2)}, u32[]{:S(2)}) collective-permute-start(f32[6,16,128]{2,1,0:T(8,128)S(1)} %get-tuple-element.34.own), channel_id=1, source_target_pairs={{0,1},{63,62},{2,4},{4,2},{3,5},{5,3},{6,8},{8,6},{7,9},{9,7},{10,... | collective-permute-start | bytes 147464 | tf_op jit(solution)/shard_map/ppermute | solution.py:445
  45.2 20.0 %collective-permute-start.7 = (f32[6,16,128]{2,1,0:T(8,128)S(1)}, f32[6,16,128]{2,1,0:T(8,128)S(1)}, u32[]{:S(2)}, u32[]{:S(2)}) collective-permute-start(f32[6,16,128]{2,1,0:T(8,128)S(1)} %get-tuple-element.34.own), channel_id=1, source_target_pairs={{0,2},{2,0},{1,3},{3,1},{4,6},{6,4},{5,7},{7,5},{8,10},{10,8},{9,1... | collective-permute-start | bytes 147464 | tf_op jit(solution)/shard_map/ppermute | solution.py:445
  45.3 19.9 %all-to-all-start = ((f32[64,1,128]{2,1,0:T(1,128)}), f32[64,1,128]{2,1,0:T(1,128)S(1)}, u32[]{:S(2)}, u32[]{:S(2)}) async-start(f32[64,1,128]{2,1,0:T(1,128)} %get-tuple-element.37), calls=%async_computation | async-start | bytes 65536 | tf_op jit(solution)/shard_map/all_to_all | solution.py:483

commit v8 on v7

--- a/solution.py
+++ b/solution.py
@@ -90,9 +90,9 @@
     bx = back_x(here, step)
     lap = (here + below) + (here + by) + (here + bx) + here
     inside = here > 0.0
-    return [
-        jnp.where(inside, scale / jnp.where(inside, lap + d, 1.0), 0.0) for d in (bx, by, below)
-    ]
+    lap = jnp.where(inside, lap, 1.0)
+    top = jnp.where(inside, scale, 0.0)
+    return [top / (lap + d) for d in (bx, by, below)]
 
 
 def trim(v, n=1):
@@ -382,8 +382,9 @@
             cf[c, 4] = jnp.where(even, b2[2 * c + 1], 0.0)
             cf[c, 5] = jnp.zeros((16, 128), jnp.float32)
 
+    added = jnp.sum(sums[...], axis=0)
     for k in range(2):
-        sum_ref[k] = jnp.sum(jnp.where(lanes((64, 1, 128)) == k, sums[...], 0.0)) * scale[k]
+        sum_ref[k] = jnp.sum(jnp.where(lanes((1, 128)) == k, added, 0.0)) * scale[k]
     mc = tiles(cm_ref[...])
     pc = [tiles(pc_ref[c]) for c in range(3)]
     r = []

time: 67.4 us -> 67.3 us (level)
  no operation moved by 1% of the time
where the time goes in v8:
time: 67.3 us; the launch traced here: 67.1 us
  starting transfers between devices  32.5 us (48%)
  waiting for transfers between devices  24.1 us (36%)
  Pallas kernels  8.66 us (13%)
  other arithmetic  1.02 us (2%)
  between operations  0.72 us (1%)
    ppermute x4, starting transfers between devices, shift(): return lax.ppermute(x, axis, [(i, (i + by) % n) for i in range(n)])  16.3 us
    all_to_all x1, starting transfers between devices, cycles(): sums = lax.all_to_all(part, 'slab', 0, 0, tiled=True)  10.4 us
    pallas_call x4, Pallas kernels, call(): pl.pallas_call(kernel, out_shape=[jax.ShapeDtypeStruct(s, jnp.float32) fo...  8.66 us
    ppermute x4, waiting for transfers between devices, shift(): return lax.ppermute(x, axis, [(i, (i + by) % n) for i in range(n)])  8.23 us
    all_to_all x1, waiting for transfers between devices, cycles(): sums = lax.all_to_all(part, 'slab', 0, 0, tiled=True)  8.13 us
    ppermute x4, waiting for transfers between devices, swap(): return lax.ppermute(x, axis, pairs)  6.32 us
    ppermute x4, starting transfers between devices, swap(): return lax.ppermute(x, axis, pairs)  4.58 us
    ppermute x1, waiting for transfers between devices, cycles(): s = lax.ppermute(modulus[3:4], 'slab', [(i, i + 2) for i in range(n - 2)])  1.43 us
  transfers between devices with their start and end apart: 10, of which 6 were waited for; matrix products, arithmetic and copies ran while one was open for 0% of the time, Pallas kernels for 2%

profile of v8, /device:TPU:0, one launch (start us, length us, event | category | flops | bytes accessed | tf_op | source)
XLA Modules:
  0.0 67.1 jit_solution(7402333255599136967)
XLA Ops:
  0.6 0.0 copy-start.1
  0.6 0.0 copy-start
  0.6 1.0 %pad_maximum_fusion = f32[16,32,128]{2,1,0:T(8,128)S(1)} fusion(f32[4,32,128]{2,1,0:T(8,128)} %e_ref.1, f32[12,32,128]{2,1,0:T(8,128)} %bitcast.1), kind=kLoop, calls=%fused_computation | loop fusion | flops 65536 | bytes 524288 | tf_op jit(solution)/shard_map/concatenate | solution.py:459
  1.7 1.7 %collective-permute-start.1 = (f32[16,32,128]{2,1,0:T(8,128)S(1)}, f32[16,32,128]{2,1,0:T(8,128)S(1)}, u32[]{:S(2)}, u32[]{:S(2)}) collective-permute-start(f32[16,32,128]{2,1,0:T(8,128)S(1)} %pad_maximum_fusion), channel_id=1, source_target_pairs={{0,1},{1,2},{2,3},{3,4},{4,5},{5,6},{6,7},{7,8},{8,9},{9,10},{10,1... | collective-permute-start | bytes 786440 | tf_op jit(solution)/shard_map/ppermute | solution.py:451
  3.3 7.3 %collective-permute-start = (f32[16,32,128]{2,1,0:T(8,128)S(1)}, f32[16,32,128]{2,1,0:T(8,128)S(1)}, u32[]{:S(2)}, u32[]{:S(2)}) collective-permute-start(f32[16,32,128]{2,1,0:T(8,128)S(1)} %pad_maximum_fusion), channel_id=1, source_target_pairs={{0,63},{1,0},{2,1},{3,2},{4,3},{5,4},{6,5},{7,6},{8,7},{9,8},{10,9... | collective-permute-start | bytes 786440 | tf_op jit(solution)/shard_map/ppermute | solution.py:451
  10.6 0.0 copy-done.1
  10.6 1.3 %collective-permute-start.2 = (f32[1,32,128]{2,1,0:T(8,128)S(1)}, f32[1,32,128]{2,1,0:T(8,128)S(1)}, u32[]{:S(2)}, u32[]{:S(2)}) collective-permute-start(f32[1,32,128]{2,1,0:T(8,128)S(1)} %slice.3), channel_id=1, source_target_pairs={{0,2},{1,3},{2,4},{3,5},{4,6},{5,7},{6,8},{7,9},{8,10},{9,11},{10,... | collective-permute-start | bytes 49160 | tf_op jit(solution)/shard_map/ppermute | solution.py:462
  11.9 1.4 %collective-permute-done.2.s_ref = f32[1,32,128]{2,1,0:T(8,128)S(1)} collective-permute-done((f32[1,32,128]{2,1,0:T(8,128)S(1)}, f32[1,32,128]{2,1,0:T(8,128)S(1)}, u32[]{:S(2)}, u32[]{:S(2)}) %collective-permute-start.2) | collective-permute-done | bytes 16416 | tf_op jit(solution)/shard_map/ppermute | solution.py:462
  13.3 3.5 %collective-permute-done.1.b_ref = f32[16,32,128]{2,1,0:T(8,128)S(1)} collective-permute-done((f32[16,32,128]{2,1,0:T(8,128)S(1)}, f32[16,32,128]{2,1,0:T(8,128)S(1)}, u32[]{:S(2)}, u32[]{:S(2)}) %collective-permute-start.1) | collective-permute-done | bytes 262176 | tf_op jit(solution)/shard_map/ppermute | solution.py:451
  16.8 0.0 collective-permute-done.a_ref
  16.8 0.0 copy-done
  16.8 1.2 %shard_map.49 = (f32[3,4,32,128]{3,2,1,0:T(8,128)S(1)}, f32[3,8,32,128]{3,2,1,0:T(8,128)S(1)}, f32[13,32,128]{2,1,0:T(8,128)S(1)}, f32[3,12,32,128]{3,2,1,0:T(8,...) custom-call(f32[3,4,32,128]{3,2,1,0:T(8,128)S(1)} %copy-done, ...), custom_call_target="tpu_custom_call" | custom-call | flops 4194304 | bytes 1048576 | tf_op jit(solution)/shard_map/pallas_call | solution.py:423
  18.1 7.3 %collective-permute-start.3 = (f32[17,32,128]{2,1,0:T(8,128)S(1)}, f32[17,32,128]{2,1,0:T(8,128)S(1)}, u32[]{:S(2)}, u32[]{:S(2)}) collective-permute-start(f32[17,32,128]{2,1,0:T(8,128)S(1)} %get-tuple-element.29), channel_id=1, source_target_pairs={{0,63},{1,0},{2,1},{3,2},{4,3},{5,4},{6,5},{7,6},{8,7},{9,8},{10,9... | collective-permute-start | bytes 835592 | tf_op jit(solution)/shard_map/ppermute | solution.py:451
  25.4 0.0 collective-permute-start.4
  25.4 1.3 %collective-permute-start.6 = (f32[18,16,128]{2,1,0:T(8,128)S(1)}, f32[18,16,128]{2,1,0:T(8,128)S(1)}, u32[]{:S(2)}, u32[]{:S(2)}) collective-permute-start(f32[18,16,128]{2,1,0:T(8,128)S(1)} %get-tuple-element.31), channel_id=1, source_target_pairs={{0,2},{63,61},{1,4},{4,1},{3,6},{6,3},{5,8},{8,5},{7,10},{10,7},{9... | collective-permute-start | bytes 442376 | tf_op jit(solution)/shard_map/ppermute | solution.py:446
  26.7 1.9 %collective-permute-start.5 = (f32[18,16,128]{2,1,0:T(8,128)S(1)}, f32[18,16,128]{2,1,0:T(8,128)S(1)}, u32[]{:S(2)}, u32[]{:S(2)}) collective-permute-start(f32[18,16,128]{2,1,0:T(8,128)S(1)} %get-tuple-element.31), channel_id=1, source_target_pairs={{0,3},{3,0},{2,5},{5,2},{4,7},{7,4},{6,9},{9,6},{8,11},{11,8},{10,... | collective-permute-start | bytes 442376 | tf_op jit(solution)/shard_map/ppermute | solution.py:446
  28.6 5.0 %collective-permute-done.6.b3 = f32[18,16,128]{2,1,0:T(8,128)S(1)} collective-permute-done((f32[18,16,128]{2,1,0:T(8,128)S(1)}, f32[18,16,128]{2,1,0:T(8,128)S(1)}, u32[]{:S(2)}, u32[]{:S(2)}) %collective-permute-start.6) | collective-permute-done | bytes 147488 | tf_op jit(solution)/shard_map/ppermute | solution.py:446
  33.6 1.3 %collective-permute-done.5.a3 = f32[18,16,128]{2,1,0:T(8,128)S(1)} collective-permute-done((f32[18,16,128]{2,1,0:T(8,128)S(1)}, f32[18,16,128]{2,1,0:T(8,128)S(1)}, u32[]{:S(2)}, u32[]{:S(2)}) %collective-permute-start.5) | collective-permute-done | bytes 147488 | tf_op jit(solution)/shard_map/ppermute | solution.py:446
  34.9 0.0 collective-permute-done.3.a1
  34.9 4.7 %collective-permute-done.4.b1 = f32[17,32,128]{2,1,0:T(8,128)S(1)} collective-permute-done((f32[17,32,128]{2,1,0:T(8,128)S(1)}, f32[17,32,128]{2,1,0:T(8,128)S(1)}, u32[]{:S(2)}, u32[]{:S(2)}) %collective-permute-start.4) | collective-permute-done | bytes 278560 | tf_op jit(solution)/shard_map/ppermute | solution.py:451
  39.6 4.2 %shard_map.50 = (f32[3,4,32,128]{3,2,1,0:T(8,128)S(1)}, f32[3,6,32,128]{3,2,1,0:T(8,128)S(1)}, f32[6,16,128]{2,1,0:T(8,128)S(1)}, f32[11,16,128]{2,1,0:T(8,128)S...) custom-call(f32[3,4,32,128]{3,2,1,0:T(8,128)S(1)} %copy-done, ...), custom_call_target="tpu_custom_call" | custom-call | flops 4194304 | bytes 1048576 | tf_op jit(solution)/shard_map/pallas_call | solution.py:423
  43.8 1.3 %collective-permute-start.8 = (f32[6,16,128]{2,1,0:T(8,128)S(1)}, f32[6,16,128]{2,1,0:T(8,128)S(1)}, u32[]{:S(2)}, u32[]{:S(2)}) collective-permute-start(f32[6,16,128]{2,1,0:T(8,128)S(1)} %get-tuple-element.34.own), channel_id=1, source_target_pairs={{0,1},{63,62},{2,4},{4,2},{3,5},{5,3},{6,8},{8,6},{7,9},{9,7},{10,... | collective-permute-start | bytes 147464 | tf_op jit(solution)/shard_map/ppermute | solution.py:446
  45.1 0.1 collective-permute-start.7
  45.2 10.4 %all-to-all-start = ((f32[64,1,128]{2,1,0:T(1,128)}), f32[64,1,128]{2,1,0:T(1,128)S(1)}, u32[]{:S(2)}, u32[]{:S(2)}) async-start(f32[64,1,128]{2,1,0:T(1,128)} %get-tuple-element.37), calls=%async_computation | async-start | bytes 65536 | tf_op jit(solution)/shard_map/all_to_all | solution.py:484
  55.6 1.4 %shard_map.52 = f32[3,2,16,64]{3,2,1,0:T(8,128)} custom-call(f32[11,16,128]{2,1,0:T(8,128)S(1)} %get-tuple-element.35.cm_ref, f32[3,10,16,128]{3,2,1,0:T(8,128)S(1)} %get-tuple-element.36.pc_ref, f32[3,2,16,128]{3,2,1,0:T(8,128)S(1)} %get-tuple-element.39.xc_ref, f32[3,8,16,128]{3,2,1,0:T(8,128)S(1)} %get-tuple-element.40.rc_ref, ...), custom_call_target="tpu_custom_call" | custom-call | flops 4194304 | bytes 1048576 | tf_op jit(solution)/shard_map/pallas_call | solution.py:423
  57.0 8.1 %all-to-all-done.sums = f32[64,1,128]{2,1,0:T(1,128)S(1)} async-done(((f32[64,1,128]{2,1,0:T(1,128)}), f32[64,1,128]{2,1,0:T(1,128)S(1)}, u32[]{:S(2)}, u32[]{:S(2)}) %all-to-all-start) | async-done | bytes 32800 | tf_op jit(solution)/shard_map/all_to_all | solution.py:484
  65.1 0.0 collective-permute-done.8.b2
  65.1 0.0 collective-permute-done.7.a2
  65.1 1.9 %shard_map.51 = (f32[3,4,32,128]{3,2,1,0:T(8,128)}, f32[2]{0:T(128)}) custom-call(f32[3,4,32,128]{3,2,1,0:T(8,128)S(1)} %get-tuple-element.32.x_ref, f32[3,6,32,128]{3,2,1,0:T(8,128)S(1)} %get-tuple-element.33.r_ref, f32[6,16,128]{2,1,0:T(8,128)S(1)} %get-tuple-element.34.own, f32[13,32,128]{2,1,0:T(8,128)S(1)} %get-tuple-element.25.m_ref, ...), custom_call_target="tpu_custom_call" | custom-call | flops 4194304 | bytes 1048576 | tf_op jit(solution)/shard_map/pallas_call | solution.py:423
  (1 shorter events, 0.0 us)
Async XLA Ops:
  0.6 10.0 %copy-start.1 = (f32[4,32,128]{2,1,0:T(8,128)S(1)}, f32[4,32,128]{2,1,0:T(8,128)}, u32[]{:S(2)}) copy-start(f32[4,32,128]{2,1,0:T(8,128)} %e_ref.1) | copy-start | bytes 196612
  0.6 16.2 %copy-start = (f32[3,4,32,128]{3,2,1,0:T(8,128)S(1)}, f32[3,4,32,128]{3,2,1,0:T(8,128)}, u32[]{:S(2)}) copy-start(f32[3,4,32,128]{3,2,1,0:T(8,128)} %f_ref.3) | copy-start | bytes 589828
  1.7 15.2 %collective-permute-start.1 = (f32[16,32,128]{2,1,0:T(8,128)S(1)}, f32[16,32,128]{2,1,0:T(8,128)S(1)}, u32[]{:S(2)}, u32[]{:S(2)}) collective-permute-start(f32[16,32,128]{2,1,0:T(8,128)S(1)} %pad_maximum_fusion), channel_id=1, source_target_pairs={{0,1},{1,2},{2,3},{3,4},{4,5},{5,6},{6,7},{7,8},{8,9},{9,10},{10,1... | collective-permute-start | bytes 786440 | tf_op jit(solution)/shard_map/ppermute | solution.py:451
  3.3 13.5 %collective-permute-start = (f32[16,32,128]{2,1,0:T(8,128)S(1)}, f32[16,32,128]{2,1,0:T(8,128)S(1)}, u32[]{:S(2)}, u32[]{:S(2)}) collective-permute-start(f32[16,32,128]{2,1,0:T(8,128)S(1)} %pad_maximum_fusion), channel_id=1, source_target_pairs={{0,63},{1,0},{2,1},{3,2},{4,3},{5,4},{6,5},{7,6},{8,7},{9,8},{10,9... | collective-permute-start | bytes 786440 | tf_op jit(solution)/shard_map/ppermute | solution.py:451
  10.6 2.7 %collective-permute-start.2 = (f32[1,32,128]{2,1,0:T(8,128)S(1)}, f32[1,32,128]{2,1,0:T(8,128)S(1)}, u32[]{:S(2)}, u32[]{:S(2)}) collective-permute-start(f32[1,32,128]{2,1,0:T(8,128)S(1)} %slice.3), channel_id=1, source_target_pairs={{0,2},{1,3},{2,4},{3,5},{4,6},{5,7},{6,8},{7,9},{8,10},{9,11},{10,... | collective-permute-start | bytes 49160 | tf_op jit(solution)/shard_map/ppermute | solution.py:462
  18.1 16.9 %collective-permute-start.3 = (f32[17,32,128]{2,1,0:T(8,128)S(1)}, f32[17,32,128]{2,1,0:T(8,128)S(1)}, u32[]{:S(2)}, u32[]{:S(2)}) collective-permute-start(f32[17,32,128]{2,1,0:T(8,128)S(1)} %get-tuple-element.29), channel_id=1, source_target_pairs={{0,63},{1,0},{2,1},{3,2},{4,3},{5,4},{6,5},{7,6},{8,7},{9,8},{10,9... | collective-permute-start | bytes 835592 | tf_op jit(solution)/shard_map/ppermute | solution.py:451
  25.4 14.3 %collective-permute-start.4 = (f32[17,32,128]{2,1,0:T(8,128)S(1)}, f32[17,32,128]{2,1,0:T(8,128)S(1)}, u32[]{:S(2)}, u32[]{:S(2)}) collective-permute-start(f32[17,32,128]{2,1,0:T(8,128)S(1)} %get-tuple-element.30), channel_id=1, source_target_pairs={{0,1},{1,2},{2,3},{3,4},{4,5},{5,6},{6,7},{7,8},{8,9},{9,10},{10,1... | collective-permute-start | bytes 835592 | tf_op jit(solution)/shard_map/ppermute | solution.py:451
  25.4 8.2 %collective-permute-start.6 = (f32[18,16,128]{2,1,0:T(8,128)S(1)}, f32[18,16,128]{2,1,0:T(8,128)S(1)}, u32[]{:S(2)}, u32[]{:S(2)}) collective-permute-start(f32[18,16,128]{2,1,0:T(8,128)S(1)} %get-tuple-element.31), channel_id=1, source_target_pairs={{0,2},{63,61},{1,4},{4,1},{3,6},{6,3},{5,8},{8,5},{7,10},{10,7},{9... | collective-permute-start | bytes 442376 | tf_op jit(solution)/shard_map/ppermute | solution.py:446
  26.7 8.2 %collective-permute-start.5 = (f32[18,16,128]{2,1,0:T(8,128)S(1)}, f32[18,16,128]{2,1,0:T(8,128)S(1)}, u32[]{:S(2)}, u32[]{:S(2)}) collective-permute-start(f32[18,16,128]{2,1,0:T(8,128)S(1)} %get-tuple-element.31), channel_id=1, source_target_pairs={{0,3},{3,0},{2,5},{5,2},{4,7},{7,4},{6,9},{9,6},{8,11},{11,8},{10,... | collective-permute-start | bytes 442376 | tf_op jit(solution)/shard_map/ppermute | solution.py:446
  43.8 21.3 %collective-permute-start.8 = (f32[6,16,128]{2,1,0:T(8,128)S(1)}, f32[6,16,128]{2,1,0:T(8,128)S(1)}, u32[]{:S(2)}, u32[]{:S(2)}) collective-permute-start(f32[6,16,128]{2,1,0:T(8,128)S(1)} %get-tuple-element.34.own), channel_id=1, source_target_pairs={{0,1},{63,62},{2,4},{4,2},{3,5},{5,3},{6,8},{8,6},{7,9},{9,7},{10,... | collective-permute-start | bytes 147464 | tf_op jit(solution)/shard_map/ppermute | solution.py:446
  45.1 20.0 %collective-permute-start.7 = (f32[6,16,128]{2,1,0:T(8,128)S(1)}, f32[6,16,128]{2,1,0:T(8,128)S(1)}, u32[]{:S(2)}, u32[]{:S(2)}) collective-permute-start(f32[6,16,128]{2,1,0:T(8,128)S(1)} %get-tuple-element.34.own), channel_id=1, source_target_pairs={{0,2},{2,0},{1,3},{3,1},{4,6},{6,4},{5,7},{7,5},{8,10},{10,8},{9,1... | collective-permute-start | bytes 147464 | tf_op jit(solution)/shard_map/ppermute | solution.py:446
  45.2 19.9 %all-to-all-start = ((f32[64,1,128]{2,1,0:T(1,128)}), f32[64,1,128]{2,1,0:T(1,128)S(1)}, u32[]{:S(2)}, u32[]{:S(2)}) async-start(f32[64,1,128]{2,1,0:T(1,128)} %get-tuple-element.37), calls=%async_computation | async-start | bytes 65536 | tf_op jit(solution)/shard_map/all_to_all | solution.py:484
